TPU v7x, 512 devices: a whole 4x8x8 slice. The times are simulated.
512 devices in a mesh: grp: 32 (over z, y_lo, core), dom: 16 (over y_hi, x).
Axes of the slice: x: 4, y: 8 (y_hi: 4, y_lo: 2; y = y_hi * 2 + y_lo), z: 8, core: 2. Of those that a mesh axis runs over, the one named last changes fastest.
Arguments:
- connect: int32 [20, 65536], P(None, ('grp', 'dom')), may hold values from 0 to 511, as said below
- interface_nodes: int32 [512, 4, 32], P(('grp', 'dom')), may hold values from 0 to 511, as said below
- neighbours: int32 [512, 4], P(('grp', 'dom')), may hold values from 0 to 1, as said below
- point_rank: int32 [512, 2048], P(('grp', 'dom')), may hold values from 0 to 2047, each once within a row
- shape_grad: float32 [48, 20], replicated, may hold values from -1.25 to 1.25
- inverse_jacobian: float32 [9, 65536], P(None, ('grp', 'dom')), may hold values from -0.45 to 2.5
- lame_moduli: float32 [2, 65536], P(None, ('grp', 'dom')), may hold values from 0.5 to 2
- point_weights: float32 [16, 65536], P(None, ('grp', 'dom')), may hold values from 0.003 to 0.02
- mass_elem: float32 [20, 65536], P(None, ('grp', 'dom')), may hold values from 0.5 to 2
- source_pattern: float32 [3, 262144], P(None, ('grp', 'dom')), may hold values from -6 to 6
- wavelet: float32 [16], replicated, may hold values from -6 to 6
Outputs:
- strain_db: bfloat16 [16, 6, 1048576], P(None, None, ('grp', 'dom'))
Inputs may be any that keep to these rules, and one draw needn't show every extreme that they name: `connect`: every one of a partition's 512 nodes is named by some element of that partition. `interface_nodes`: entry i of list k of a partition and entry i of the opposite list of the partition beside it in direction k are copies of one node; no node stands twice among a partition's four lists. `neighbours`: the entry of a partition in direction k equals that of the partition beside it in the opposite direction; it is 0 where no partition lies in direction k.
All inputs are finite; a program needn't handle non-finite values.
Results may differ from a plain program's by a relative error of at most 0.001.
Values may be sent and summed in bfloat16 or wider, within the bound.
No kernel may reach another device: no remote copies, remote signals or barrier semaphores. Data moves between devices by JAX's collectives and lax.ppermute only.
A program may use at most 64 MiB of HBM per device.

v0:
```python
import jax
import jax.numpy as jnp
from jax import lax
from jax.sharding import PartitionSpec as P

EL_NODES = 20
POINTS = 16
STRAIN = 6
STEPS = 16


time_step = 0.5


def extended(cells, sides, width):
    for axis, dim in sides:
        count = lax.axis_size(axis)
        ends = count - 1
        head = lax.slice_in_dim(cells, 0, width, axis=dim)
        tail = lax.slice_in_dim(cells, cells.shape[dim] - width, cells.shape[dim], axis=dim)
        cells = jnp.concatenate(
            [
                lax.ppermute(tail, axis, [(i, (i + 1) % count) for i in range(ends)]),
                cells,
                lax.ppermute(head, axis, [((i + 1) % count, i) for i in range(ends)]),
            ],
            axis=dim,
        )
    return cells


def gather_nodes(displace, incidence, elements):
    node_values = lax.dot_general(
        displace,
        incidence.astype(jnp.float32),
        (((1,), (1,)), ((), ())),
        precision=lax.Precision.HIGHEST,
        preferred_element_type=jnp.float32,
    )
    return node_values.reshape(displace.shape[0], EL_NODES, elements)


def scatter_nodes(node_values, incidence):
    flat = node_values.reshape(node_values.shape[0], -1)
    return jnp.dot(
        flat,
        incidence.astype(jnp.float32),
        precision=lax.Precision.HIGHEST,
        preferred_element_type=jnp.float32,
    )


def gradient_at(displace, incidence, shape_grad, inverse_jacobian):
    elements = inverse_jacobian.shape[1]
    node_values = gather_nodes(displace, incidence, elements)
    along_ref = jnp.einsum("mn,cne->cme", shape_grad, node_values, precision=lax.Precision.HIGHEST)
    along_ref = along_ref.reshape(3, 3, POINTS, elements)
    jacobian = inverse_jacobian.reshape(3, 3, elements)
    result = along_ref[:, 0, None] * jacobian[0][None, :, None, :]
    result = result + along_ref[:, 1, None] * jacobian[1][None, :, None, :]
    result = result + along_ref[:, 2, None] * jacobian[2][None, :, None, :]
    return result


def strain_of(tensor):
    return jnp.stack(
        [
            tensor[0, 0],
            tensor[1, 1],
            tensor[2, 2],
            0.5 * (tensor[1, 2] + tensor[2, 1]),
            0.5 * (tensor[0, 2] + tensor[2, 0]),
            0.5 * (tensor[0, 1] + tensor[1, 0]),
        ],
        axis=0,
    )


def element_forces(tensor, lame_moduli, point_weights, inverse_jacobian, shape_grad, incidence):
    elements = inverse_jacobian.shape[1]
    jacobian = inverse_jacobian.reshape(3, 3, elements)
    volume_change = tensor[0, 0] + tensor[1, 1] + tensor[2, 2]
    identity = jnp.eye(3, dtype=jnp.float32)
    stress = lame_moduli[1][None, None, None, :] * (tensor + tensor.transpose(1, 0, 2, 3))
    stress = (
        stress + identity[:, :, None, None] * (lame_moduli[0][None, :] * volume_change)[None, None]
    )
    mapped = stress[:, 0][:, None] * jacobian[:, 0][None, :, None, :]
    mapped = mapped + stress[:, 1][:, None] * jacobian[:, 1][None, :, None, :]
    mapped = mapped + stress[:, 2][:, None] * jacobian[:, 2][None, :, None, :]
    mapped = mapped * point_weights[None, None]
    node_values = jnp.einsum(
        "mn,cme->cne",
        shape_grad,
        mapped.reshape(3, 3 * POINTS, elements),
        precision=lax.Precision.HIGHEST,
    )
    return scatter_nodes(node_values, incidence)


def shards(
    connect,
    interface_nodes,
    neighbours,
    point_rank,
    shape_grad,
    inverse_jacobian,
    lame_moduli,
    point_weights,
    mass_elem,
    source_pattern,
    wavelet,
):
    node_count = source_pattern.shape[1]
    elements = connect.shape[1]
    point_count = point_rank.shape[1]
    shared_nodes = interface_nodes[0]
    neighbour_mask = neighbours[0].astype(jnp.float32)
    node_ids = jnp.arange(node_count, dtype=jnp.int32)
    incidence = (connect.reshape(-1)[:, None] == node_ids[None, :]).astype(jnp.bfloat16)

    def assemble(node_field):
        picked = jnp.take(node_field, shared_nodes, axis=1)
        lower_upper = extended(picked[:, 0:2], (("grp", 1),), 1)
        left_right = extended(picked[:, 2:4], (("dom", 1),), 1)
        received = jnp.concatenate(
            [lower_upper[:, 0:1], lower_upper[:, 3:4], left_right[:, 0:1], left_right[:, 3:4]],
            axis=1,
        )
        return node_field.at[:, shared_nodes].add(received * neighbour_mask[None, :, None])

    node_mass = scatter_nodes(mass_elem[None], incidence)
    inverse_mass = 1.0 / assemble(node_mass)
    inverse_rank = (
        jnp.zeros((point_count,), jnp.int32)
        .at[point_rank[0]]
        .set(jnp.arange(point_count, dtype=jnp.int32))
    )

    def record_strain(strain_store, slot_index, tensor):
        snapshot = strain_of(tensor).reshape(STRAIN, point_count).astype(jnp.bfloat16)
        return lax.dynamic_update_slice(strain_store, snapshot[None], (slot_index, 0, 0))

    def advance(step_index, loop_state):
        displace, velocity, tensor, strain_store = loop_state
        force = wavelet[step_index] * source_pattern - element_forces(
            tensor, lame_moduli, point_weights, inverse_jacobian, shape_grad, incidence
        )
        force = assemble(force)
        velocity = velocity + time_step * inverse_mass * force
        displace = displace + time_step * velocity
        fresh = gradient_at(displace, incidence, shape_grad, inverse_jacobian)
        strain_store = record_strain(strain_store, step_index, fresh)
        return (displace, velocity, fresh, strain_store)

    start = jnp.zeros((3, node_count), jnp.float32)
    first_tensor = jnp.zeros((3, 3, POINTS, elements), jnp.float32)
    strain_store = jnp.zeros((STEPS, STRAIN, point_count), jnp.bfloat16)
    displace, velocity, tensor, strain_store = lax.fori_loop(
        0, STEPS, advance, (start, start, first_tensor, strain_store)
    )
    ordered = jnp.take(strain_store, inverse_rank, axis=2)
    strain_store = lax.all_to_all(ordered, "dom", split_axis=2, concat_axis=2, tiled=True)
    return strain_store


def solution(mesh):
    placed = (
        P(None, ("grp", "dom")),
        P(("grp", "dom"), None, None),
        P(("grp", "dom"), None),
        P(("grp", "dom"), None),
        P(),
        P(None, ("grp", "dom")),
        P(None, ("grp", "dom")),
        P(None, ("grp", "dom")),
        P(None, ("grp", "dom")),
        P(None, ("grp", "dom")),
        P(),
    )
    return jax.shard_map(
        shards, mesh=mesh, in_specs=placed, out_specs=P(None, None, ("grp", "dom")), check_vma=False
    )
```

profile of v0, /device:TPU:256, one launch (start us, length us, event | category | flops | bytes accessed | tf_op | source)
XLA Modules:
  0.0 555.7 jit_solution(7203432960443793795)
XLA Ops:
  9.3 4.5 collective-permute-start.6
  13.9 5.2 collective-permute-start.5
  19.8 8.0 %scatter_custom_fusion.1 = s32[2048]{0:T(1024)S(1)} fusion(s32[2048]{0:T(1024)S(1)} %bitcast.217, s32[2048]{0:T(1024)S(1)} %iota.33, s32[]{:T(128)} %constant.94.clone.1), kind=kCustom, calls=%fused_computation.79 | custom fusion | bytes 8196 | tf_op jit(solution)/shard_map/scatter | solution.py:137
  31.0 428.2 %while.21 = (s32[]{:T(128)}, f32[3,512]{0,1:T(8,128)S(1)}, f32[3,512]{0,1:T(8,128)S(1)}, f32[3,3,16,128]{3,2,1,0:T(8,128)S(1)}, bf16[16,6,2048]{2,1,0:T(8,128)(2...) while((s32[]{:T(128)}, f32[3,512]{0,1:T(8,128)S(1)}, ...), condition=%wide.wide.region_4.5_spmd.clone, body=%wide.wide.region_2.4_spmd.clone.sunk | while | flops 108817296 | bytes 1922756 | solution.py:159
  84.9 5.7 %collective-permute-start.1 = (f32[3,1,32]{2,1,0:T(1,128)S(1)}, f32[3,1,32]{2,1,0:T(1,128)S(1)}, u32[]{:S(2)}, u32[]{:S(2)}) collective-permute-start(f32[3,1,32]{2,1,0:T(1,128)S(1)} %get-tuple-element.593), channel_id=1, source_target_pairs={{0,1},{1,2},{2,3},{3,4},{4,5},{5,6},{6,7},{7,8},{8,9},{9,10},{10,1... | collective-permute-start | bytes 1160 | tf_op jit(solution)/shard_map/while/body/eval_jaxpr/ppermute | solution.py:23
  110.3 7.6 %collective-permute-start.1 = (f32[3,1,32]{2,1,0:T(1,128)S(1)}, f32[3,1,32]{2,1,0:T(1,128)S(1)}, u32[]{:S(2)}, u32[]{:S(2)}) collective-permute-start(f32[3,1,32]{2,1,0:T(1,128)S(1)} %get-tuple-element.593), channel_id=1, source_target_pairs={{0,1},{1,2},{2,3},{3,4},{4,5},{5,6},{6,7},{7,8},{8,9},{9,10},{10,1... | collective-permute-start | bytes 1160 | tf_op jit(solution)/shard_map/while/body/eval_jaxpr/ppermute | solution.py:23
  137.5 7.6 %collective-permute-start.1 = (f32[3,1,32]{2,1,0:T(1,128)S(1)}, f32[3,1,32]{2,1,0:T(1,128)S(1)}, u32[]{:S(2)}, u32[]{:S(2)}) collective-permute-start(f32[3,1,32]{2,1,0:T(1,128)S(1)} %get-tuple-element.593), channel_id=1, source_target_pairs={{0,1},{1,2},{2,3},{3,4},{4,5},{5,6},{6,7},{7,8},{8,9},{9,10},{10,1... | collective-permute-start | bytes 1160 | tf_op jit(solution)/shard_map/while/body/eval_jaxpr/ppermute | solution.py:23
  164.8 7.6 %collective-permute-start.1 = (f32[3,1,32]{2,1,0:T(1,128)S(1)}, f32[3,1,32]{2,1,0:T(1,128)S(1)}, u32[]{:S(2)}, u32[]{:S(2)}) collective-permute-start(f32[3,1,32]{2,1,0:T(1,128)S(1)} %get-tuple-element.593), channel_id=1, source_target_pairs={{0,1},{1,2},{2,3},{3,4},{4,5},{5,6},{6,7},{7,8},{8,9},{9,10},{10,1... | collective-permute-start | bytes 1160 | tf_op jit(solution)/shard_map/while/body/eval_jaxpr/ppermute | solution.py:23
  192.0 7.6 %collective-permute-start.1 = (f32[3,1,32]{2,1,0:T(1,128)S(1)}, f32[3,1,32]{2,1,0:T(1,128)S(1)}, u32[]{:S(2)}, u32[]{:S(2)}) collective-permute-start(f32[3,1,32]{2,1,0:T(1,128)S(1)} %get-tuple-element.593), channel_id=1, source_target_pairs={{0,1},{1,2},{2,3},{3,4},{4,5},{5,6},{6,7},{7,8},{8,9},{9,10},{10,1... | collective-permute-start | bytes 1160 | tf_op jit(solution)/shard_map/while/body/eval_jaxpr/ppermute | solution.py:23
  219.3 7.6 %collective-permute-start.1 = (f32[3,1,32]{2,1,0:T(1,128)S(1)}, f32[3,1,32]{2,1,0:T(1,128)S(1)}, u32[]{:S(2)}, u32[]{:S(2)}) collective-permute-start(f32[3,1,32]{2,1,0:T(1,128)S(1)} %get-tuple-element.593), channel_id=1, source_target_pairs={{0,1},{1,2},{2,3},{3,4},{4,5},{5,6},{6,7},{7,8},{8,9},{9,10},{10,1... | collective-permute-start | bytes 1160 | tf_op jit(solution)/shard_map/while/body/eval_jaxpr/ppermute | solution.py:23
  246.5 7.6 %collective-permute-start.1 = (f32[3,1,32]{2,1,0:T(1,128)S(1)}, f32[3,1,32]{2,1,0:T(1,128)S(1)}, u32[]{:S(2)}, u32[]{:S(2)}) collective-permute-start(f32[3,1,32]{2,1,0:T(1,128)S(1)} %get-tuple-element.593), channel_id=1, source_target_pairs={{0,1},{1,2},{2,3},{3,4},{4,5},{5,6},{6,7},{7,8},{8,9},{9,10},{10,1... | collective-permute-start | bytes 1160 | tf_op jit(solution)/shard_map/while/body/eval_jaxpr/ppermute | solution.py:23
  273.8 7.6 %collective-permute-start.1 = (f32[3,1,32]{2,1,0:T(1,128)S(1)}, f32[3,1,32]{2,1,0:T(1,128)S(1)}, u32[]{:S(2)}, u32[]{:S(2)}) collective-permute-start(f32[3,1,32]{2,1,0:T(1,128)S(1)} %get-tuple-element.593), channel_id=1, source_target_pairs={{0,1},{1,2},{2,3},{3,4},{4,5},{5,6},{6,7},{7,8},{8,9},{9,10},{10,1... | collective-permute-start | bytes 1160 | tf_op jit(solution)/shard_map/while/body/eval_jaxpr/ppermute | solution.py:23
  301.0 7.6 %collective-permute-start.1 = (f32[3,1,32]{2,1,0:T(1,128)S(1)}, f32[3,1,32]{2,1,0:T(1,128)S(1)}, u32[]{:S(2)}, u32[]{:S(2)}) collective-permute-start(f32[3,1,32]{2,1,0:T(1,128)S(1)} %get-tuple-element.593), channel_id=1, source_target_pairs={{0,1},{1,2},{2,3},{3,4},{4,5},{5,6},{6,7},{7,8},{8,9},{9,10},{10,1... | collective-permute-start | bytes 1160 | tf_op jit(solution)/shard_map/while/body/eval_jaxpr/ppermute | solution.py:23
  328.3 7.6 %collective-permute-start.1 = (f32[3,1,32]{2,1,0:T(1,128)S(1)}, f32[3,1,32]{2,1,0:T(1,128)S(1)}, u32[]{:S(2)}, u32[]{:S(2)}) collective-permute-start(f32[3,1,32]{2,1,0:T(1,128)S(1)} %get-tuple-element.593), channel_id=1, source_target_pairs={{0,1},{1,2},{2,3},{3,4},{4,5},{5,6},{6,7},{7,8},{8,9},{9,10},{10,1... | collective-permute-start | bytes 1160 | tf_op jit(solution)/shard_map/while/body/eval_jaxpr/ppermute | solution.py:23
  355.5 7.6 %collective-permute-start.1 = (f32[3,1,32]{2,1,0:T(1,128)S(1)}, f32[3,1,32]{2,1,0:T(1,128)S(1)}, u32[]{:S(2)}, u32[]{:S(2)}) collective-permute-start(f32[3,1,32]{2,1,0:T(1,128)S(1)} %get-tuple-element.593), channel_id=1, source_target_pairs={{0,1},{1,2},{2,3},{3,4},{4,5},{5,6},{6,7},{7,8},{8,9},{9,10},{10,1... | collective-permute-start | bytes 1160 | tf_op jit(solution)/shard_map/while/body/eval_jaxpr/ppermute | solution.py:23
  382.8 7.6 %collective-permute-start.1 = (f32[3,1,32]{2,1,0:T(1,128)S(1)}, f32[3,1,32]{2,1,0:T(1,128)S(1)}, u32[]{:S(2)}, u32[]{:S(2)}) collective-permute-start(f32[3,1,32]{2,1,0:T(1,128)S(1)} %get-tuple-element.593), channel_id=1, source_target_pairs={{0,1},{1,2},{2,3},{3,4},{4,5},{5,6},{6,7},{7,8},{8,9},{9,10},{10,1... | collective-permute-start | bytes 1160 | tf_op jit(solution)/shard_map/while/body/eval_jaxpr/ppermute | solution.py:23
  410.0 7.6 %collective-permute-start.1 = (f32[3,1,32]{2,1,0:T(1,128)S(1)}, f32[3,1,32]{2,1,0:T(1,128)S(1)}, u32[]{:S(2)}, u32[]{:S(2)}) collective-permute-start(f32[3,1,32]{2,1,0:T(1,128)S(1)} %get-tuple-element.593), channel_id=1, source_target_pairs={{0,1},{1,2},{2,3},{3,4},{4,5},{5,6},{6,7},{7,8},{8,9},{9,10},{10,1... | collective-permute-start | bytes 1160 | tf_op jit(solution)/shard_map/while/body/eval_jaxpr/ppermute | solution.py:23
  437.3 7.6 %collective-permute-start.1 = (f32[3,1,32]{2,1,0:T(1,128)S(1)}, f32[3,1,32]{2,1,0:T(1,128)S(1)}, u32[]{:S(2)}, u32[]{:S(2)}) collective-permute-start(f32[3,1,32]{2,1,0:T(1,128)S(1)} %get-tuple-element.593), channel_id=1, source_target_pairs={{0,1},{1,2},{2,3},{3,4},{4,5},{5,6},{6,7},{7,8},{8,9},{9,10},{10,1... | collective-permute-start | bytes 1160 | tf_op jit(solution)/shard_map/while/body/eval_jaxpr/ppermute | solution.py:23
  463.4 16.9 %gather_fusion.2 = bf16[2048,16,6]{1,2,0:T(8,128)(2,1)} fusion(bf16[16,6,2048]{0,1,2:T(8,128)(2,1)} %copy.25, s32[2048]{0:T(1024)S(1)} %fusion.34), kind=kCustom, calls=%fused_computation.2 | custom fusion | bytes 794624 | tf_op jit(solution)/shard_map/jit(_take)/gather | solution.py:162
  480.3 10.9 %fusion.43 = bf16[2048,6,16]{2,1,0:T(8,128)(2,1)} fusion(bf16[2048,16,6]{1,2,0:T(8,128)(2,1)} %gather_fusion.2, pred[2048]{0:T(1024)(128)(4,1)S(1)} %compare_and_fusion.1), kind=kLoop, calls=%fused_computation.91 | loop fusion | flops 196608 | bytes 788480
  491.2 5.0 reshape.572
  496.3 49.8 %all_to_all.5 = bf16[16,2,6144]{2,1,0:T(2,128)(2,1)S(1)} all-to-all(bf16[16,2,6144]{2,1,0:T(2,128)(2,1)S(1)} %reshape.572), channel_id=1, replica_groups=mesh['grp'=32,'dom'=16] {'dom'}, dimensions={0} | all-to-all | bytes 786432 | tf_op jit(solution)/shard_map/all_to_all | solution.py:163
  546.0 4.8 reshape.573
  550.9 4.9 copy.26
  (912 shorter events, 336.5 us)
Async XLA Ops:
  6.1 23.2 %collective-permute-start.4 = (f32[1,1,32]{2,1,0:T(1,128)S(1)}, f32[1,1,32]{2,1,0:T(1,128)S(1)}, u32[]{:S(2)}, u32[]{:S(2)}) collective-permute-start(f32[1,1,32]{2,1,0:T(1,128)S(1)} %get-tuple-element.361), channel_id=1, source_target_pairs={{0,16},{16,32},{32,48},{48,64},{64,80},{80,96},{96,112},{112,128},... | collective-permute-start | bytes 392 | tf_op jit(solution)/shard_map/ppermute | solution.py:23
  8.0 21.3 %collective-permute-start.7 = (f32[1,1,32]{2,1,0:T(1,128)S(1)}, f32[1,1,32]{2,1,0:T(1,128)S(1)}, u32[]{:S(2)}, u32[]{:S(2)}) collective-permute-start(f32[1,1,32]{2,1,0:T(1,128)S(1)} %get-tuple-element.362), channel_id=1, source_target_pairs={{1,0},{2,1},{3,2},{4,3},{5,4},{6,5},{7,6},{8,7},{9,8},{10,9},{11,1... | collective-permute-start | bytes 392 | tf_op jit(solution)/shard_map/ppermute | solution.py:25
  9.3 20.0 %collective-permute-start.6 = (f32[1,1,32]{2,1,0:T(1,128)S(1)}, f32[1,1,32]{2,1,0:T(1,128)S(1)}, u32[]{:S(2)}, u32[]{:S(2)}) collective-permute-start(f32[1,1,32]{2,1,0:T(1,128)S(1)} %get-tuple-element.363), channel_id=1, source_target_pairs={{0,1},{1,2},{2,3},{3,4},{4,5},{5,6},{6,7},{7,8},{8,9},{9,10},{10,1... | collective-permute-start | bytes 392 | tf_op jit(solution)/shard_map/ppermute | solution.py:23
  13.9 15.4 %collective-permute-start.5 = (f32[1,1,32]{2,1,0:T(1,128)S(1)}, f32[1,1,32]{2,1,0:T(1,128)S(1)}, u32[]{:S(2)}, u32[]{:S(2)}) collective-permute-start(f32[1,1,32]{2,1,0:T(1,128)S(1)} %get-tuple-element.364), channel_id=1, source_target_pairs={{16,0},{32,16},{48,32},{64,48},{80,64},{96,80},{112,96},{128,112},... | collective-permute-start | bytes 392 | tf_op jit(solution)/shard_map/ppermute | solution.py:25
  109.0 13.2 %collective-permute-start = (f32[3,1,32]{2,1,0:T(1,128)S(1)}, f32[3,1,32]{2,1,0:T(1,128)S(1)}, u32[]{:S(2)}, u32[]{:S(2)}) collective-permute-start(f32[3,1,32]{2,1,0:T(1,128)S(1)} %get-tuple-element.592), channel_id=1, source_target_pairs={{1,0},{2,1},{3,2},{4,3},{5,4},{6,5},{7,6},{8,7},{9,8},{10,9},{11,1... | collective-permute-start | bytes 1160 | tf_op jit(solution)/shard_map/while/body/eval_jaxpr/ppermute | solution.py:25
  110.3 11.9 %collective-permute-start.1 = (f32[3,1,32]{2,1,0:T(1,128)S(1)}, f32[3,1,32]{2,1,0:T(1,128)S(1)}, u32[]{:S(2)}, u32[]{:S(2)}) collective-permute-start(f32[3,1,32]{2,1,0:T(1,128)S(1)} %get-tuple-element.593), channel_id=1, source_target_pairs={{0,1},{1,2},{2,3},{3,4},{4,5},{5,6},{6,7},{7,8},{8,9},{9,10},{10,1... | collective-permute-start | bytes 1160 | tf_op jit(solution)/shard_map/while/body/eval_jaxpr/ppermute | solution.py:23
  136.2 13.2 %collective-permute-start = (f32[3,1,32]{2,1,0:T(1,128)S(1)}, f32[3,1,32]{2,1,0:T(1,128)S(1)}, u32[]{:S(2)}, u32[]{:S(2)}) collective-permute-start(f32[3,1,32]{2,1,0:T(1,128)S(1)} %get-tuple-element.592), channel_id=1, source_target_pairs={{1,0},{2,1},{3,2},{4,3},{5,4},{6,5},{7,6},{8,7},{9,8},{10,9},{11,1... | collective-permute-start | bytes 1160 | tf_op jit(solution)/shard_map/while/body/eval_jaxpr/ppermute | solution.py:25
  137.5 11.9 %collective-permute-start.1 = (f32[3,1,32]{2,1,0:T(1,128)S(1)}, f32[3,1,32]{2,1,0:T(1,128)S(1)}, u32[]{:S(2)}, u32[]{:S(2)}) collective-permute-start(f32[3,1,32]{2,1,0:T(1,128)S(1)} %get-tuple-element.593), channel_id=1, source_target_pairs={{0,1},{1,2},{2,3},{3,4},{4,5},{5,6},{6,7},{7,8},{8,9},{9,10},{10,1... | collective-permute-start | bytes 1160 | tf_op jit(solution)/shard_map/while/body/eval_jaxpr/ppermute | solution.py:23
  163.5 13.2 %collective-permute-start = (f32[3,1,32]{2,1,0:T(1,128)S(1)}, f32[3,1,32]{2,1,0:T(1,128)S(1)}, u32[]{:S(2)}, u32[]{:S(2)}) collective-permute-start(f32[3,1,32]{2,1,0:T(1,128)S(1)} %get-tuple-element.592), channel_id=1, source_target_pairs={{1,0},{2,1},{3,2},{4,3},{5,4},{6,5},{7,6},{8,7},{9,8},{10,9},{11,1... | collective-permute-start | bytes 1160 | tf_op jit(solution)/shard_map/while/body/eval_jaxpr/ppermute | solution.py:25
  164.8 11.9 %collective-permute-start.1 = (f32[3,1,32]{2,1,0:T(1,128)S(1)}, f32[3,1,32]{2,1,0:T(1,128)S(1)}, u32[]{:S(2)}, u32[]{:S(2)}) collective-permute-start(f32[3,1,32]{2,1,0:T(1,128)S(1)} %get-tuple-element.593), channel_id=1, source_target_pairs={{0,1},{1,2},{2,3},{3,4},{4,5},{5,6},{6,7},{7,8},{8,9},{9,10},{10,1... | collective-permute-start | bytes 1160 | tf_op jit(solution)/shard_map/while/body/eval_jaxpr/ppermute | solution.py:23
  190.7 13.2 %collective-permute-start = (f32[3,1,32]{2,1,0:T(1,128)S(1)}, f32[3,1,32]{2,1,0:T(1,128)S(1)}, u32[]{:S(2)}, u32[]{:S(2)}) collective-permute-start(f32[3,1,32]{2,1,0:T(1,128)S(1)} %get-tuple-element.592), channel_id=1, source_target_pairs={{1,0},{2,1},{3,2},{4,3},{5,4},{6,5},{7,6},{8,7},{9,8},{10,9},{11,1... | collective-permute-start | bytes 1160 | tf_op jit(solution)/shard_map/while/body/eval_jaxpr/ppermute | solution.py:25
  192.0 11.9 %collective-permute-start.1 = (f32[3,1,32]{2,1,0:T(1,128)S(1)}, f32[3,1,32]{2,1,0:T(1,128)S(1)}, u32[]{:S(2)}, u32[]{:S(2)}) collective-permute-start(f32[3,1,32]{2,1,0:T(1,128)S(1)} %get-tuple-element.593), channel_id=1, source_target_pairs={{0,1},{1,2},{2,3},{3,4},{4,5},{5,6},{6,7},{7,8},{8,9},{9,10},{10,1... | collective-permute-start | bytes 1160 | tf_op jit(solution)/shard_map/while/body/eval_jaxpr/ppermute | solution.py:23
  218.0 13.2 %collective-permute-start = (f32[3,1,32]{2,1,0:T(1,128)S(1)}, f32[3,1,32]{2,1,0:T(1,128)S(1)}, u32[]{:S(2)}, u32[]{:S(2)}) collective-permute-start(f32[3,1,32]{2,1,0:T(1,128)S(1)} %get-tuple-element.592), channel_id=1, source_target_pairs={{1,0},{2,1},{3,2},{4,3},{5,4},{6,5},{7,6},{8,7},{9,8},{10,9},{11,1... | collective-permute-start | bytes 1160 | tf_op jit(solution)/shard_map/while/body/eval_jaxpr/ppermute | solution.py:25
  245.2 13.2 %collective-permute-start = (f32[3,1,32]{2,1,0:T(1,128)S(1)}, f32[3,1,32]{2,1,0:T(1,128)S(1)}, u32[]{:S(2)}, u32[]{:S(2)}) collective-permute-start(f32[3,1,32]{2,1,0:T(1,128)S(1)} %get-tuple-element.592), channel_id=1, source_target_pairs={{1,0},{2,1},{3,2},{4,3},{5,4},{6,5},{7,6},{8,7},{9,8},{10,9},{11,1... | collective-permute-start | bytes 1160 | tf_op jit(solution)/shard_map/while/body/eval_jaxpr/ppermute | solution.py:25
  246.5 11.9 %collective-permute-start.1 = (f32[3,1,32]{2,1,0:T(1,128)S(1)}, f32[3,1,32]{2,1,0:T(1,128)S(1)}, u32[]{:S(2)}, u32[]{:S(2)}) collective-permute-start(f32[3,1,32]{2,1,0:T(1,128)S(1)} %get-tuple-element.593), channel_id=1, source_target_pairs={{0,1},{1,2},{2,3},{3,4},{4,5},{5,6},{6,7},{7,8},{8,9},{9,10},{10,1... | collective-permute-start | bytes 1160 | tf_op jit(solution)/shard_map/while/body/eval_jaxpr/ppermute | solution.py:23
  272.5 13.2 %collective-permute-start = (f32[3,1,32]{2,1,0:T(1,128)S(1)}, f32[3,1,32]{2,1,0:T(1,128)S(1)}, u32[]{:S(2)}, u32[]{:S(2)}) collective-permute-start(f32[3,1,32]{2,1,0:T(1,128)S(1)} %get-tuple-element.592), channel_id=1, source_target_pairs={{1,0},{2,1},{3,2},{4,3},{5,4},{6,5},{7,6},{8,7},{9,8},{10,9},{11,1... | collective-permute-start | bytes 1160 | tf_op jit(solution)/shard_map/while/body/eval_jaxpr/ppermute | solution.py:25
  299.7 13.2 %collective-permute-start = (f32[3,1,32]{2,1,0:T(1,128)S(1)}, f32[3,1,32]{2,1,0:T(1,128)S(1)}, u32[]{:S(2)}, u32[]{:S(2)}) collective-permute-start(f32[3,1,32]{2,1,0:T(1,128)S(1)} %get-tuple-element.592), channel_id=1, source_target_pairs={{1,0},{2,1},{3,2},{4,3},{5,4},{6,5},{7,6},{8,7},{9,8},{10,9},{11,1... | collective-permute-start | bytes 1160 | tf_op jit(solution)/shard_map/while/body/eval_jaxpr/ppermute | solution.py:25
  327.0 13.2 %collective-permute-start = (f32[3,1,32]{2,1,0:T(1,128)S(1)}, f32[3,1,32]{2,1,0:T(1,128)S(1)}, u32[]{:S(2)}, u32[]{:S(2)}) collective-permute-start(f32[3,1,32]{2,1,0:T(1,128)S(1)} %get-tuple-element.592), channel_id=1, source_target_pairs={{1,0},{2,1},{3,2},{4,3},{5,4},{6,5},{7,6},{8,7},{9,8},{10,9},{11,1... | collective-permute-start | bytes 1160 | tf_op jit(solution)/shard_map/while/body/eval_jaxpr/ppermute | solution.py:25
  328.3 11.9 %collective-permute-start.1 = (f32[3,1,32]{2,1,0:T(1,128)S(1)}, f32[3,1,32]{2,1,0:T(1,128)S(1)}, u32[]{:S(2)}, u32[]{:S(2)}) collective-permute-start(f32[3,1,32]{2,1,0:T(1,128)S(1)} %get-tuple-element.593), channel_id=1, source_target_pairs={{0,1},{1,2},{2,3},{3,4},{4,5},{5,6},{6,7},{7,8},{8,9},{9,10},{10,1... | collective-permute-start | bytes 1160 | tf_op jit(solution)/shard_map/while/body/eval_jaxpr/ppermute | solution.py:23
  354.2 13.2 %collective-permute-start = (f32[3,1,32]{2,1,0:T(1,128)S(1)}, f32[3,1,32]{2,1,0:T(1,128)S(1)}, u32[]{:S(2)}, u32[]{:S(2)}) collective-permute-start(f32[3,1,32]{2,1,0:T(1,128)S(1)} %get-tuple-element.592), channel_id=1, source_target_pairs={{1,0},{2,1},{3,2},{4,3},{5,4},{6,5},{7,6},{8,7},{9,8},{10,9},{11,1... | collective-permute-start | bytes 1160 | tf_op jit(solution)/shard_map/while/body/eval_jaxpr/ppermute | solution.py:25
  381.5 13.2 %collective-permute-start = (f32[3,1,32]{2,1,0:T(1,128)S(1)}, f32[3,1,32]{2,1,0:T(1,128)S(1)}, u32[]{:S(2)}, u32[]{:S(2)}) collective-permute-start(f32[3,1,32]{2,1,0:T(1,128)S(1)} %get-tuple-element.592), channel_id=1, source_target_pairs={{1,0},{2,1},{3,2},{4,3},{5,4},{6,5},{7,6},{8,7},{9,8},{10,9},{11,1... | collective-permute-start | bytes 1160 | tf_op jit(solution)/shard_map/while/body/eval_jaxpr/ppermute | solution.py:25
  382.8 11.9 %collective-permute-start.1 = (f32[3,1,32]{2,1,0:T(1,128)S(1)}, f32[3,1,32]{2,1,0:T(1,128)S(1)}, u32[]{:S(2)}, u32[]{:S(2)}) collective-permute-start(f32[3,1,32]{2,1,0:T(1,128)S(1)} %get-tuple-element.593), channel_id=1, source_target_pairs={{0,1},{1,2},{2,3},{3,4},{4,5},{5,6},{6,7},{7,8},{8,9},{9,10},{10,1... | collective-permute-start | bytes 1160 | tf_op jit(solution)/shard_map/while/body/eval_jaxpr/ppermute | solution.py:23
  408.7 13.2 %collective-permute-start = (f32[3,1,32]{2,1,0:T(1,128)S(1)}, f32[3,1,32]{2,1,0:T(1,128)S(1)}, u32[]{:S(2)}, u32[]{:S(2)}) collective-permute-start(f32[3,1,32]{2,1,0:T(1,128)S(1)} %get-tuple-element.592), channel_id=1, source_target_pairs={{1,0},{2,1},{3,2},{4,3},{5,4},{6,5},{7,6},{8,7},{9,8},{10,9},{11,1... | collective-permute-start | bytes 1160 | tf_op jit(solution)/shard_map/while/body/eval_jaxpr/ppermute | solution.py:25
  436.0 13.2 %collective-permute-start = (f32[3,1,32]{2,1,0:T(1,128)S(1)}, f32[3,1,32]{2,1,0:T(1,128)S(1)}, u32[]{:S(2)}, u32[]{:S(2)}) collective-permute-start(f32[3,1,32]{2,1,0:T(1,128)S(1)} %get-tuple-element.592), channel_id=1, source_target_pairs={{1,0},{2,1},{3,2},{4,3},{5,4},{6,5},{7,6},{8,7},{9,8},{10,9},{11,1... | collective-permute-start | bytes 1160 | tf_op jit(solution)/shard_map/while/body/eval_jaxpr/ppermute | solution.py:25
  (52 other events, 561.4 us)
where the time goes:
time: 559 us; the launch traced here: 556 us
  starting transfers between devices  216 us (39%)
  matrix products  90.1 us (16%)
  local copies, waits for them, and re-layouts  77.7 us (14%)
  waiting for transfers between devices  72.8 us (13%)
  blocking collectives  49.8 us (9%)
  other arithmetic  44.3 us (8%)
    ppermute x34, starting transfers between devices, extended(): lax.ppermute(tail, axis, [(i, (i + 1) % count) for i in range(ends)])  158 us
    ppermute x34, waiting for transfers between devices, extended(): lax.ppermute(tail, axis, [(i, (i + 1) % count) for i in range(ends)])  72.7 us
    ppermute x34, starting transfers between devices, extended(): lax.ppermute(head, axis, [((i + 1) % count, i) for i in range(ends)])  57.9 us
    all_to_all x1, blocking collectives, shards(): lax.all_to_all(ordered, 'dom', split_axis=2, concat_axis=2, tiled=True)  49.8 us
    dot_general x16, matrix products, gather_nodes(): lax.dot_general(displace, incidence.astype(jnp.float32), (((1,), (1,)), (...  48.8 us
    dot_general x17, matrix products, scatter_nodes(): jnp.dot(flat, incidence.astype(jnp.float32), precision=lax.Precision.HIGH...  34.2 us
    scatter-add x17, other arithmetic, assemble(): node_field.at[:, shared_nodes].add(received * neighbour_mask[None, :, None])  23.2 us
    gather x1, local copies, waits for them, and re-layouts, shards(): ordered = jnp.take(strain_store, inverse_rank, axis=2)  16.9 us
  transfers between devices with their start and end apart: 68, of which 16 were waited for; matrix products, arithmetic and copies ran while one was open for 2% of the time, Pallas kernels for 0%

commit v1 on v0

v1 whole, which is shorter than its diff:
```python
import functools

import jax
import jax.numpy as jnp
from jax import lax
from jax.experimental import pallas as pl
from jax.experimental.pallas import tpu as pltpu
from jax.sharding import PartitionSpec as P


EL_NODES = 20
NODE_ROWS = 24
POINTS = 16
STRAIN = 6
STEPS = 16
LANES = 128
FACES = 4

time_step = 0.5

EXCHANGES = ("dom1", "grp1", "dom0", "grp0")

VMEM = pl.BlockSpec(memory_space=pltpu.VMEM)
SMEM = pl.BlockSpec(memory_space=pltpu.SMEM)


def kernel_call(body, outs, n_in, smem=(), scratch=()):
    return pl.pallas_call(
        body,
        out_shape=outs,
        in_specs=[SMEM if i in smem else VMEM for i in range(n_in)],
        out_specs=[VMEM] * len(outs),
        scratch_shapes=list(scratch),
        compiler_params=pltpu.CompilerParams(vmem_limit_bytes=24 * 1024 * 1024),
    )


def parts_of(x):
    high = x.astype(jnp.bfloat16).astype(jnp.float32)
    rest = x - high
    middle = rest.astype(jnp.bfloat16).astype(jnp.float32)
    low = (rest - middle).astype(jnp.bfloat16).astype(jnp.float32)
    return high, middle, low


def matmul(left, right):
    return jnp.dot(left, right, preferred_element_type=jnp.float32)


def lane_gather(row, index):
    return jnp.take_along_axis(row, index, axis=1)


def pick_lanes(field, index):
    low = jnp.bitwise_and(index, LANES - 1)
    chunk = jnp.right_shift(index, 7)
    out = lane_gather(field[:, 0:LANES], low)
    for j in range(1, field.shape[1] // LANES):
        out = jnp.where(
            chunk == j, lane_gather(field[:, j * LANES : (j + 1) * LANES], low), out
        )
    return out


def spread(received, inverse):
    out = []
    for j in range(inverse.shape[1] // LANES):
        index = inverse[:, j * LANES : (j + 1) * LANES]
        taken = lane_gather(received, jnp.maximum(index, 0))
        out.append(jnp.where(index >= 0, taken, 0.0))
    return jnp.concatenate(out, axis=1)


def merge_received(source, dom1, grp1, dom0, grp0):
    out = jnp.where(source == 0, grp0, grp1)
    out = jnp.where(source == 2, dom0, out)
    return jnp.where(source == 3, dom1, out)


def scatter_nodes(rows, incidence):
    left = jnp.concatenate(parts_of(rows), axis=0).astype(jnp.bfloat16)
    sums = matmul(left, incidence)
    return (sums[16:24] + sums[8:16]) + sums[0:8]


def prepare_kernel(
    connect,
    lists,
    swapped,
    active,
    mass_elem,
    source_pattern,
    incidence,
    field,
    send,
    pick_index,
    inverse_index,
):
    nodes = source_pattern.shape[1]
    lane = lax.broadcasted_iota(jnp.int32, (LANES, nodes), 1)
    for n in range(EL_NODES):
        column = jnp.broadcast_to(connect[n : n + 1, :], (LANES, LANES)).T
        wide = jnp.concatenate([column] * (nodes // LANES), axis=1)
        incidence[n * LANES : (n + 1) * LANES, :] = jnp.where(wide == lane, 1.0, 0.0).astype(
            jnp.bfloat16
        )
    listed = jnp.where(active[...] != 0, lists[...], -1)
    column = jnp.broadcast_to(listed, (LANES, LANES)).T
    wide = jnp.concatenate([column] * (nodes // LANES), axis=1)
    slot = lax.broadcasted_iota(jnp.int32, (LANES, nodes), 0) + 1
    found = jnp.sum(jnp.where(wide == lane, slot, 0), axis=0, keepdims=True)
    inverse_index[...] = jnp.broadcast_to(found - 1, (8, nodes))
    index = jnp.broadcast_to(swapped[...], (8, LANES))
    pick_index[...] = index
    rows = jnp.concatenate(
        [jnp.broadcast_to(mass_elem[n : n + 1, :], (8, LANES)) for n in range(EL_NODES)], axis=1
    )
    field[...] = scatter_nodes(rows, incidence[...])
    field[0:3, :] = source_pattern[...]
    send[...] = pick_lanes(field[...], index)


def strain_and_force(
    displace,
    strain,
    connect,
    left_gradient,
    left_force,
    inverse_jacobian,
    lame_moduli,
    point_weights,
    incidence,
    need_force,
):
    index = connect[...]
    low = jnp.bitwise_and(index, LANES - 1)
    chunk = jnp.right_shift(index, 7)
    is_chunk = [chunk == j for j in range(1, displace.shape[1] // LANES)]
    columns = []
    for c in range(3):
        pieces = []
        for b in range(NODE_ROWS // 8):
            rows = slice(8 * b, 8 * b + 8)
            out = None
            for j in range(displace.shape[1] // LANES):
                row = jnp.broadcast_to(displace[c : c + 1, j * LANES : (j + 1) * LANES], (8, LANES))
                taken = lane_gather(row, low[rows])
                out = taken if j == 0 else jnp.where(is_chunk[j - 1][rows], taken, out)
            pieces.append(out)
        columns.append(jnp.concatenate(pieces, axis=0))
    node_values = jnp.concatenate(columns, axis=1)
    right = jnp.concatenate(parts_of(node_values), axis=0).astype(jnp.bfloat16)
    sums = matmul(left_gradient[...], right)
    height = 3 * POINTS
    along = (sums[2 * height :] + sums[height : 2 * height]) + sums[0:height]
    jac = [inverse_jacobian[i : i + 1, :] for i in range(9)]

    def ref_derivative(c, r):
        return along[r * POINTS : (r + 1) * POINTS, c * LANES : (c + 1) * LANES]

    grad = [
        [
            (ref_derivative(c, 0) * jac[d] + ref_derivative(c, 1) * jac[3 + d])
            + ref_derivative(c, 2) * jac[6 + d]
            for d in range(3)
        ]
        for c in range(3)
    ]
    shear = {(c, d): grad[c][d] + grad[d][c] for c, d in ((1, 2), (0, 2), (0, 1))}
    rows = [grad[0][0], grad[1][1], grad[2][2]] + [0.5 * shear[k] for k in ((1, 2), (0, 2), (0, 1))]
    for s in range(STRAIN):
        strain[s * POINTS : (s + 1) * POINTS, :] = rows[s]
    if not need_force:
        return None
    volume = (grad[0][0] + grad[1][1]) + grad[2][2]
    weights = point_weights[...]
    shear_scale = lame_moduli[1:2, :] * weights
    pressure = (lame_moduli[0:1, :] * weights) * volume
    stress = [[None] * 3 for _ in range(3)]
    for c in range(3):
        for d in range(3):
            if c == d:
                stress[c][d] = shear_scale * (grad[c][c] + grad[c][c]) + pressure
            else:
                stress[c][d] = shear_scale * shear[(min(c, d), max(c, d))]
    columns = []
    for c in range(3):
        mapped = [
            (stress[c][0] * jac[3 * r] + stress[c][1] * jac[3 * r + 1])
            + stress[c][2] * jac[3 * r + 2]
            for r in range(3)
        ]
        columns.append(jnp.concatenate(mapped, axis=0))
    mapped = jnp.concatenate(columns, axis=1)
    right = jnp.concatenate(parts_of(mapped), axis=0).astype(jnp.bfloat16)
    sums = matmul(left_force[...], right)
    node_forces = (sums[2 * NODE_ROWS :] + sums[NODE_ROWS : 2 * NODE_ROWS]) + sums[0:NODE_ROWS]
    row_id = lax.broadcasted_iota(jnp.int32, (8, LANES), 0)
    pieces = []
    for n in range(EL_NODES):
        first, second, third = (
            jnp.broadcast_to(node_forces[n : n + 1, c * LANES : (c + 1) * LANES], (8, LANES))
            for c in range(3)
        )
        pieces.append(jnp.where(row_id == 0, first, jnp.where(row_id == 1, second, third)))
    return scatter_nodes(jnp.concatenate(pieces, axis=1), incidence[...])


def first_kernel(
    wavelet,
    dom1,
    grp1,
    dom0,
    grp0,
    source,
    inverse_index,
    pick_index,
    field,
    connect,
    left_gradient,
    left_force,
    inverse_jacobian,
    lame_moduli,
    point_weights,
    incidence,
    strain,
    displace,
    velocity,
    pattern,
    half_inverse_mass,
    force,
    send,
):
    received = merge_received(source[...], dom1[...], grp1[...], dom0[...], grp0[...])
    total = field[...] + spread(received, inverse_index[...])
    scale = jnp.broadcast_to(time_step * (1.0 / total[3:4, :]), total.shape)
    pattern[...] = total
    half_inverse_mass[...] = scale
    new_velocity = scale * (wavelet[0] * total)
    velocity[...] = new_velocity
    new_displace = time_step * new_velocity
    displace[...] = new_displace
    new_force = strain_and_force(
        new_displace,
        strain,
        connect,
        left_gradient,
        left_force,
        inverse_jacobian,
        lame_moduli,
        point_weights,
        incidence,
        True,
    )
    force[...] = new_force
    send[...] = pick_lanes(new_force, pick_index[...])


def step_kernel(
    step,
    wavelet,
    dom1,
    grp1,
    dom0,
    grp0,
    source,
    inverse_index,
    pick_index,
    connect,
    left_gradient,
    left_force,
    inverse_jacobian,
    lame_moduli,
    point_weights,
    incidence,
    pattern,
    half_inverse_mass,
    old_displace,
    old_velocity,
    old_force,
    strain,
    *rest,
):
    received = merge_received(source[...], dom1[...], grp1[...], dom0[...], grp0[...])
    stiff = old_force[...] + spread(received, inverse_index[...])
    total = wavelet[step] * pattern[...] - stiff
    new_velocity = old_velocity[...] + half_inverse_mass[...] * total
    new_displace = old_displace[...] + time_step * new_velocity
    new_force = strain_and_force(
        new_displace,
        strain,
        connect,
        left_gradient,
        left_force,
        inverse_jacobian,
        lame_moduli,
        point_weights,
        incidence,
        bool(rest),
    )
    if rest:
        displace, velocity, force, send = rest
        displace[...] = new_displace
        velocity[...] = new_velocity
        force[...] = new_force
        send[...] = pick_lanes(new_force, pick_index[...])


def order_kernel(rank, *refs):
    strains, out, store = refs[:STEPS], refs[STEPS], refs[STEPS + 1]
    per_step = STRAIN * POINTS
    for t in range(STEPS):
        store[t * per_step : (t + 1) * per_step, :] = strains[t][...]
    count = rank.shape[0] * LANES
    lane = lax.broadcasted_iota(jnp.int32, (LANES, count), 1)
    total = None
    for q in range(POINTS):
        values = store[pl.ds(q, STEPS * STRAIN, stride=POINTS), :].astype(jnp.bfloat16)
        column = jnp.broadcast_to(rank[q : q + 1, :], (LANES, LANES)).T
        wide = jnp.concatenate([column] * (count // LANES), axis=1)
        chosen = jnp.where(wide == lane, 1.0, 0.0).astype(jnp.bfloat16)
        part = matmul(values, chosen)
        total = part if total is None else total + part
    for w in range(count // LANES):
        out[w] = total[:, w * LANES : (w + 1) * LANES].astype(jnp.bfloat16)


def place_kernel(pieces, out, store):
    writers = pieces.shape[0]
    for w in range(writers):
        store[:, w * LANES : (w + 1) * LANES] = pieces[w].astype(jnp.float32)
    for t in range(STEPS):
        out[t] = store[t * STRAIN : (t + 1) * STRAIN, :].astype(jnp.bfloat16)


def rounded(x):
    return lax.reduce_precision(x, 8, 7)


def left_operand(matrix, rows, columns):
    padded = jnp.pad(matrix, ((0, rows - matrix.shape[0]), (0, columns - matrix.shape[1])))
    high = rounded(padded)
    middle = rounded(padded - high)
    low = rounded(padded - high - middle)
    zero = jnp.zeros_like(padded)
    blocks = [[high, high, high], [middle, middle, zero], [low, zero, zero]]
    return jnp.block(blocks).astype(jnp.bfloat16)


def shards(
    connect,
    interface_nodes,
    neighbours,
    point_rank,
    shape_grad,
    inverse_jacobian,
    lame_moduli,
    point_weights,
    mass_elem,
    source_pattern,
    wavelet,
):
    nodes = source_pattern.shape[1]
    f32 = jnp.float32
    field_t = jax.ShapeDtypeStruct((8, nodes), f32)
    lanes_t = jax.ShapeDtypeStruct((8, LANES), f32)
    index_t = jax.ShapeDtypeStruct((8, LANES), jnp.int32)
    strain_t = jax.ShapeDtypeStruct((STRAIN * POINTS, LANES), f32)

    lists = interface_nodes.reshape(1, LANES)
    swapped = interface_nodes.reshape(2, 2, LANES // 4)[:, ::-1].reshape(1, LANES)
    active = jnp.repeat(neighbours, LANES // FACES, axis=1)
    face = lax.broadcasted_iota(jnp.int32, (8, LANES), 1) // (LANES // FACES)
    parity = jnp.where(face < 2, lax.axis_index("grp") % 2, lax.axis_index("dom") % 2)
    source = 2 * (face // 2) + jnp.bitwise_xor(parity, 1 - face % 2)
    left_gradient = left_operand(shape_grad, 3 * POINTS, NODE_ROWS)
    left_force = left_operand(shape_grad.T, NODE_ROWS, 3 * POINTS)
    padded_connect = jnp.pad(connect, ((0, NODE_ROWS - EL_NODES), (0, 0)))

    def exchange(send):
        received = []
        for name in EXCHANGES:
            axis, offset = name[:3], int(name[3])
            count = lax.axis_size(axis)
            pairs = []
            for i in range(offset, count - 1, 2):
                pairs += [(i, i + 1), (i + 1, i)]
            received.append(lax.ppermute(send, axis, pairs))
        return received

    incidence, field, send, pick_index, inverse_index = kernel_call(
        prepare_kernel,
        [
            jax.ShapeDtypeStruct((EL_NODES * LANES, nodes), jnp.bfloat16),
            field_t,
            lanes_t,
            index_t,
            jax.ShapeDtypeStruct((8, nodes), jnp.int32),
        ],
        6,
    )(connect, lists, swapped, active, mass_elem, source_pattern)
    element_data = (
        padded_connect,
        left_gradient,
        left_force,
        inverse_jacobian,
        lame_moduli,
        point_weights,
        incidence,
    )
    received = exchange(send)
    strain, displace, velocity, pattern, half_inverse_mass, force, send = kernel_call(
        first_kernel,
        [strain_t, field_t, field_t, field_t, field_t, field_t, lanes_t],
        16,
        smem=(0,),
    )(wavelet, *received, source, inverse_index, pick_index, field, *element_data)
    strains = [strain]
    for step in range(1, STEPS):
        received = exchange(send)
        last = step == STEPS - 1
        outs = kernel_call(
            functools.partial(step_kernel, step),
            [strain_t] + ([] if last else [field_t, field_t, field_t, lanes_t]),
            20,
            smem=(0,),
        )(
            wavelet,
            *received,
            source,
            inverse_index,
            pick_index,
            *element_data,
            pattern,
            half_inverse_mass,
            displace,
            velocity,
            force,
        )
        strains.append(outs[0])
        if not last:
            displace, velocity, force, send = outs[1:]
    writers = lax.axis_size("dom")
    (ordered,) = kernel_call(
        order_kernel,
        [jax.ShapeDtypeStruct((writers, STEPS * STRAIN, LANES), jnp.bfloat16)],
        1 + STEPS,
        scratch=[pltpu.VMEM((STEPS * STRAIN * POINTS, LANES), f32)],
    )(point_rank.reshape(POINTS, LANES), *strains)
    pieces = lax.all_to_all(ordered, "dom", split_axis=0, concat_axis=0, tiled=True)
    (placed,) = kernel_call(
        place_kernel,
        [jax.ShapeDtypeStruct((STEPS, STRAIN, writers * LANES), jnp.bfloat16)],
        1,
        scratch=[pltpu.VMEM((STEPS * STRAIN, writers * LANES), f32)],
    )(pieces)
    return placed


def solution(mesh):
    placed = (
        P(None, ("grp", "dom")),
        P(("grp", "dom"), None, None),
        P(("grp", "dom"), None),
        P(("grp", "dom"), None),
        P(),
        P(None, ("grp", "dom")),
        P(None, ("grp", "dom")),
        P(None, ("grp", "dom")),
        P(None, ("grp", "dom")),
        P(None, ("grp", "dom")),
        P(),
    )
    return jax.shard_map(
        shards, mesh=mesh, in_specs=placed, out_specs=P(None, None, ("grp", "dom")), check_vma=False
    )
```

time: 559 us -> 334 us (0.60)
  the two profiles are of different devices: /device:TPU:256 before, /device:TPU:201 now
where the time goes in v1:
time: 334 us; the launch traced here: 332 us
  starting transfers between devices  222 us (66%)
  blocking collectives  36 us (11%)
  waiting for transfers between devices  32.2 us (10%)
  Pallas kernels  29.8 us (9%)
  local copies, waits for them, and re-layouts  9.69 us (3%)
    ppermute x64, starting transfers between devices, exchange(): received.append(lax.ppermute(send, axis, pairs))  222 us
    all_to_all x1, blocking collectives, shards(): lax.all_to_all(ordered, 'dom', split_axis=0, concat_axis=0, tiled=True)  36 us
    ppermute x64, waiting for transfers between devices, exchange(): received.append(lax.ppermute(send, axis, pairs))  32.2 us
    pallas_call x15, Pallas kernels, shards(): kernel_call(functools.partial(step_kernel, step), [strain_t] + ([] if las...  24.8 us
  transfers between devices with their start and end apart: 64, of which 15 were waited for; matrix products, arithmetic and copies ran while one was open for 1% of the time, Pallas kernels for 0%

profile of v1, /device:TPU:201, one launch (start us, length us, event | category | flops | bytes accessed | tf_op | source)
XLA Modules:
  0.0 331.9 jit_solution(9294797539854410354)
XLA Ops:
  11.4 5.3 %collective-permute-start.1 = (f32[8,128]{1,0:T(8,128)S(1)}, f32[8,128]{1,0:T(8,128)S(1)}, u32[]{:S(2)}, u32[]{:S(2)}) collective-permute-start(f32[8,128]{1,0:T(8,128)S(1)} %get-tuple-element.87), channel_id=1, source_target_pairs={{16,32},{32,16},{48,64},{64,48},{80,96},{96,80},{112,128},{128,112... | collective-permute-start | bytes 12296 | tf_op jit(solution)/shard_map/ppermute | solution.py:388
  26.3 5.3 %collective-permute-start.6 = (f32[8,128]{1,0:T(8,128)S(1)}, f32[8,128]{1,0:T(8,128)S(1)}, u32[]{:S(2)}, u32[]{:S(2)}) collective-permute-start(f32[8,128]{1,0:T(8,128)S(1)} %get-tuple-element.93), channel_id=1, source_target_pairs={{0,1},{1,0},{2,3},{3,2},{4,5},{5,4},{6,7},{7,6},{8,9},{9,8},{10,11... | collective-permute-start | bytes 12296 | tf_op jit(solution)/shard_map/ppermute | solution.py:388
  42.3 5.1 %collective-permute-start.10 = (f32[8,128]{1,0:T(8,128)S(1)}, f32[8,128]{1,0:T(8,128)S(1)}, u32[]{:S(2)}, u32[]{:S(2)}) collective-permute-start(f32[8,128]{1,0:T(8,128)S(1)} %get-tuple-element.100), channel_id=1, source_target_pairs={{0,1},{1,0},{2,3},{3,2},{4,5},{5,4},{6,7},{7,6},{8,9},{9,8},{10,11... | collective-permute-start | bytes 12296 | tf_op jit(solution)/shard_map/ppermute | solution.py:388
  47.4 4.9 %collective-permute-start.9 = (f32[8,128]{1,0:T(8,128)S(1)}, f32[8,128]{1,0:T(8,128)S(1)}, u32[]{:S(2)}, u32[]{:S(2)}) collective-permute-start(f32[8,128]{1,0:T(8,128)S(1)} %get-tuple-element.100), channel_id=1, source_target_pairs={{16,32},{32,16},{48,64},{64,48},{80,96},{96,80},{112,128},{128,112... | collective-permute-start | bytes 12296 | tf_op jit(solution)/shard_map/ppermute | solution.py:388
  58.1 7.4 %collective-permute-start.14 = (f32[8,128]{1,0:T(8,128)S(1)}, f32[8,128]{1,0:T(8,128)S(1)}, u32[]{:S(2)}, u32[]{:S(2)}) collective-permute-start(f32[8,128]{1,0:T(8,128)S(1)} %get-tuple-element.105), channel_id=1, source_target_pairs={{0,1},{1,0},{2,3},{3,2},{4,5},{5,4},{6,7},{7,6},{8,9},{9,8},{10,11... | collective-permute-start | bytes 12296 | tf_op jit(solution)/shard_map/ppermute | solution.py:388
  76.2 5.9 %collective-permute-start.18 = (f32[8,128]{1,0:T(8,128)S(1)}, f32[8,128]{1,0:T(8,128)S(1)}, u32[]{:S(2)}, u32[]{:S(2)}) collective-permute-start(f32[8,128]{1,0:T(8,128)S(1)} %get-tuple-element.110), channel_id=1, source_target_pairs={{0,1},{1,0},{2,3},{3,2},{4,5},{5,4},{6,7},{7,6},{8,9},{9,8},{10,11... | collective-permute-start | bytes 12296 | tf_op jit(solution)/shard_map/ppermute | solution.py:388
  82.1 4.9 %collective-permute-start.17 = (f32[8,128]{1,0:T(8,128)S(1)}, f32[8,128]{1,0:T(8,128)S(1)}, u32[]{:S(2)}, u32[]{:S(2)}) collective-permute-start(f32[8,128]{1,0:T(8,128)S(1)} %get-tuple-element.110), channel_id=1, source_target_pairs={{16,32},{32,16},{48,64},{64,48},{80,96},{96,80},{112,128},{128,112... | collective-permute-start | bytes 12296 | tf_op jit(solution)/shard_map/ppermute | solution.py:388
  92.8 7.4 %collective-permute-start.22 = (f32[8,128]{1,0:T(8,128)S(1)}, f32[8,128]{1,0:T(8,128)S(1)}, u32[]{:S(2)}, u32[]{:S(2)}) collective-permute-start(f32[8,128]{1,0:T(8,128)S(1)} %get-tuple-element.115), channel_id=1, source_target_pairs={{0,1},{1,0},{2,3},{3,2},{4,5},{5,4},{6,7},{7,6},{8,9},{9,8},{10,11... | collective-permute-start | bytes 12296 | tf_op jit(solution)/shard_map/ppermute | solution.py:388
  110.9 6.1 %collective-permute-start.26 = (f32[8,128]{1,0:T(8,128)S(1)}, f32[8,128]{1,0:T(8,128)S(1)}, u32[]{:S(2)}, u32[]{:S(2)}) collective-permute-start(f32[8,128]{1,0:T(8,128)S(1)} %get-tuple-element.120), channel_id=1, source_target_pairs={{0,1},{1,0},{2,3},{3,2},{4,5},{5,4},{6,7},{7,6},{8,9},{9,8},{10,11... | collective-permute-start | bytes 12296 | tf_op jit(solution)/shard_map/ppermute | solution.py:388
  117.0 4.9 %collective-permute-start.25 = (f32[8,128]{1,0:T(8,128)S(1)}, f32[8,128]{1,0:T(8,128)S(1)}, u32[]{:S(2)}, u32[]{:S(2)}) collective-permute-start(f32[8,128]{1,0:T(8,128)S(1)} %get-tuple-element.120), channel_id=1, source_target_pairs={{16,32},{32,16},{48,64},{64,48},{80,96},{96,80},{112,128},{128,112... | collective-permute-start | bytes 12296 | tf_op jit(solution)/shard_map/ppermute | solution.py:388
  127.7 8.6 %collective-permute-start.30 = (f32[8,128]{1,0:T(8,128)S(1)}, f32[8,128]{1,0:T(8,128)S(1)}, u32[]{:S(2)}, u32[]{:S(2)}) collective-permute-start(f32[8,128]{1,0:T(8,128)S(1)} %get-tuple-element.125), channel_id=1, source_target_pairs={{0,1},{1,0},{2,3},{3,2},{4,5},{5,4},{6,7},{7,6},{8,9},{9,8},{10,11... | collective-permute-start | bytes 12296 | tf_op jit(solution)/shard_map/ppermute | solution.py:388
  147.0 7.1 %collective-permute-start.34 = (f32[8,128]{1,0:T(8,128)S(1)}, f32[8,128]{1,0:T(8,128)S(1)}, u32[]{:S(2)}, u32[]{:S(2)}) collective-permute-start(f32[8,128]{1,0:T(8,128)S(1)} %get-tuple-element.130), channel_id=1, source_target_pairs={{0,1},{1,0},{2,3},{3,2},{4,5},{5,4},{6,7},{7,6},{8,9},{9,8},{10,11... | collective-permute-start | bytes 12296 | tf_op jit(solution)/shard_map/ppermute | solution.py:388
  154.1 4.9 %collective-permute-start.33 = (f32[8,128]{1,0:T(8,128)S(1)}, f32[8,128]{1,0:T(8,128)S(1)}, u32[]{:S(2)}, u32[]{:S(2)}) collective-permute-start(f32[8,128]{1,0:T(8,128)S(1)} %get-tuple-element.130), channel_id=1, source_target_pairs={{16,32},{32,16},{48,64},{64,48},{80,96},{96,80},{112,128},{128,112... | collective-permute-start | bytes 12296 | tf_op jit(solution)/shard_map/ppermute | solution.py:388
  164.8 8.6 %collective-permute-start.38 = (f32[8,128]{1,0:T(8,128)S(1)}, f32[8,128]{1,0:T(8,128)S(1)}, u32[]{:S(2)}, u32[]{:S(2)}) collective-permute-start(f32[8,128]{1,0:T(8,128)S(1)} %get-tuple-element.135), channel_id=1, source_target_pairs={{0,1},{1,0},{2,3},{3,2},{4,5},{5,4},{6,7},{7,6},{8,9},{9,8},{10,11... | collective-permute-start | bytes 12296 | tf_op jit(solution)/shard_map/ppermute | solution.py:388
  184.2 7.1 %collective-permute-start.42 = (f32[8,128]{1,0:T(8,128)S(1)}, f32[8,128]{1,0:T(8,128)S(1)}, u32[]{:S(2)}, u32[]{:S(2)}) collective-permute-start(f32[8,128]{1,0:T(8,128)S(1)} %get-tuple-element.140), channel_id=1, source_target_pairs={{0,1},{1,0},{2,3},{3,2},{4,5},{5,4},{6,7},{7,6},{8,9},{9,8},{10,11... | collective-permute-start | bytes 12296 | tf_op jit(solution)/shard_map/ppermute | solution.py:388
  191.3 4.9 %collective-permute-start.41 = (f32[8,128]{1,0:T(8,128)S(1)}, f32[8,128]{1,0:T(8,128)S(1)}, u32[]{:S(2)}, u32[]{:S(2)}) collective-permute-start(f32[8,128]{1,0:T(8,128)S(1)} %get-tuple-element.140), channel_id=1, source_target_pairs={{16,32},{32,16},{48,64},{64,48},{80,96},{96,80},{112,128},{128,112... | collective-permute-start | bytes 12296 | tf_op jit(solution)/shard_map/ppermute | solution.py:388
  201.9 8.6 %collective-permute-start.46 = (f32[8,128]{1,0:T(8,128)S(1)}, f32[8,128]{1,0:T(8,128)S(1)}, u32[]{:S(2)}, u32[]{:S(2)}) collective-permute-start(f32[8,128]{1,0:T(8,128)S(1)} %get-tuple-element.145), channel_id=1, source_target_pairs={{0,1},{1,0},{2,3},{3,2},{4,5},{5,4},{6,7},{7,6},{8,9},{9,8},{10,11... | collective-permute-start | bytes 12296 | tf_op jit(solution)/shard_map/ppermute | solution.py:388
  221.3 7.1 %collective-permute-start.50 = (f32[8,128]{1,0:T(8,128)S(1)}, f32[8,128]{1,0:T(8,128)S(1)}, u32[]{:S(2)}, u32[]{:S(2)}) collective-permute-start(f32[8,128]{1,0:T(8,128)S(1)} %get-tuple-element.150), channel_id=1, source_target_pairs={{0,1},{1,0},{2,3},{3,2},{4,5},{5,4},{6,7},{7,6},{8,9},{9,8},{10,11... | collective-permute-start | bytes 12296 | tf_op jit(solution)/shard_map/ppermute | solution.py:388
  228.4 4.9 %collective-permute-start.49 = (f32[8,128]{1,0:T(8,128)S(1)}, f32[8,128]{1,0:T(8,128)S(1)}, u32[]{:S(2)}, u32[]{:S(2)}) collective-permute-start(f32[8,128]{1,0:T(8,128)S(1)} %get-tuple-element.150), channel_id=1, source_target_pairs={{16,32},{32,16},{48,64},{64,48},{80,96},{96,80},{112,128},{128,112... | collective-permute-start | bytes 12296 | tf_op jit(solution)/shard_map/ppermute | solution.py:388
  239.1 8.6 %collective-permute-start.54 = (f32[8,128]{1,0:T(8,128)S(1)}, f32[8,128]{1,0:T(8,128)S(1)}, u32[]{:S(2)}, u32[]{:S(2)}) collective-permute-start(f32[8,128]{1,0:T(8,128)S(1)} %get-tuple-element.155), channel_id=1, source_target_pairs={{0,1},{1,0},{2,3},{3,2},{4,5},{5,4},{6,7},{7,6},{8,9},{9,8},{10,11... | collective-permute-start | bytes 12296 | tf_op jit(solution)/shard_map/ppermute | solution.py:388
  258.4 7.1 %collective-permute-start.58 = (f32[8,128]{1,0:T(8,128)S(1)}, f32[8,128]{1,0:T(8,128)S(1)}, u32[]{:S(2)}, u32[]{:S(2)}) collective-permute-start(f32[8,128]{1,0:T(8,128)S(1)} %get-tuple-element.160), channel_id=1, source_target_pairs={{0,1},{1,0},{2,3},{3,2},{4,5},{5,4},{6,7},{7,6},{8,9},{9,8},{10,11... | collective-permute-start | bytes 12296 | tf_op jit(solution)/shard_map/ppermute | solution.py:388
  265.5 4.9 %collective-permute-start.57 = (f32[8,128]{1,0:T(8,128)S(1)}, f32[8,128]{1,0:T(8,128)S(1)}, u32[]{:S(2)}, u32[]{:S(2)}) collective-permute-start(f32[8,128]{1,0:T(8,128)S(1)} %get-tuple-element.160), channel_id=1, source_target_pairs={{16,32},{32,16},{48,64},{64,48},{80,96},{96,80},{112,128},{128,112... | collective-permute-start | bytes 12296 | tf_op jit(solution)/shard_map/ppermute | solution.py:388
  276.2 8.6 %collective-permute-start.62 = (f32[8,128]{1,0:T(8,128)S(1)}, f32[8,128]{1,0:T(8,128)S(1)}, u32[]{:S(2)}, u32[]{:S(2)}) collective-permute-start(f32[8,128]{1,0:T(8,128)S(1)} %get-tuple-element.165), channel_id=1, source_target_pairs={{0,1},{1,0},{2,3},{3,2},{4,5},{5,4},{6,7},{7,6},{8,9},{9,8},{10,11... | collective-permute-start | bytes 12296 | tf_op jit(solution)/shard_map/ppermute | solution.py:388
  294.8 36.0 %all_to_all.5.pieces = bf16[16,96,128]{2,1,0:T(8,128)(2,1)S(1)} all-to-all(bf16[16,96,128]{2,1,0:T(8,128)(2,1)S(1)} %shard_map.129), channel_id=1, replica_groups=mesh['grp'=32,'dom'=16] {'dom'}, dimensions={0} | all-to-all | bytes 786432 | tf_op jit(solution)/shard_map/all_to_all | solution.py:450
  (159 shorter events, 146.5 us)
Async XLA Ops:
  5.7 14.2 %collective-permute-start.3 = (f32[8,128]{1,0:T(8,128)S(1)}, f32[8,128]{1,0:T(8,128)S(1)}, u32[]{:S(2)}, u32[]{:S(2)}) collective-permute-start(f32[8,128]{1,0:T(8,128)S(1)} %get-tuple-element.87), channel_id=1, source_target_pairs={{0,16},{16,0},{32,48},{48,32},{64,80},{80,64},{96,112},{112,96},{1... | collective-permute-start | bytes 12296 | tf_op jit(solution)/shard_map/ppermute | solution.py:388
  40.3 12.7 %collective-permute-start.11 = (f32[8,128]{1,0:T(8,128)S(1)}, f32[8,128]{1,0:T(8,128)S(1)}, u32[]{:S(2)}, u32[]{:S(2)}) collective-permute-start(f32[8,128]{1,0:T(8,128)S(1)} %get-tuple-element.100), channel_id=1, source_target_pairs={{0,16},{16,0},{32,48},{48,32},{64,80},{80,64},{96,112},{112,96},{1... | collective-permute-start | bytes 12296 | tf_op jit(solution)/shard_map/ppermute | solution.py:388
  56.1 13.4 %collective-permute-start.15 = (f32[8,128]{1,0:T(8,128)S(1)}, f32[8,128]{1,0:T(8,128)S(1)}, u32[]{:S(2)}, u32[]{:S(2)}) collective-permute-start(f32[8,128]{1,0:T(8,128)S(1)} %get-tuple-element.105), channel_id=1, source_target_pairs={{0,16},{16,0},{32,48},{48,32},{64,80},{80,64},{96,112},{112,96},{1... | collective-permute-start | bytes 12296 | tf_op jit(solution)/shard_map/ppermute | solution.py:388
  74.3 13.4 %collective-permute-start.19 = (f32[8,128]{1,0:T(8,128)S(1)}, f32[8,128]{1,0:T(8,128)S(1)}, u32[]{:S(2)}, u32[]{:S(2)}) collective-permute-start(f32[8,128]{1,0:T(8,128)S(1)} %get-tuple-element.110), channel_id=1, source_target_pairs={{0,16},{16,0},{32,48},{48,32},{64,80},{80,64},{96,112},{112,96},{1... | collective-permute-start | bytes 12296 | tf_op jit(solution)/shard_map/ppermute | solution.py:388
  90.8 13.4 %collective-permute-start.23 = (f32[8,128]{1,0:T(8,128)S(1)}, f32[8,128]{1,0:T(8,128)S(1)}, u32[]{:S(2)}, u32[]{:S(2)}) collective-permute-start(f32[8,128]{1,0:T(8,128)S(1)} %get-tuple-element.115), channel_id=1, source_target_pairs={{0,16},{16,0},{32,48},{48,32},{64,80},{80,64},{96,112},{112,96},{1... | collective-permute-start | bytes 12296 | tf_op jit(solution)/shard_map/ppermute | solution.py:388
  109.0 13.7 %collective-permute-start.27 = (f32[8,128]{1,0:T(8,128)S(1)}, f32[8,128]{1,0:T(8,128)S(1)}, u32[]{:S(2)}, u32[]{:S(2)}) collective-permute-start(f32[8,128]{1,0:T(8,128)S(1)} %get-tuple-element.120), channel_id=1, source_target_pairs={{0,16},{16,0},{32,48},{48,32},{64,80},{80,64},{96,112},{112,96},{1... | collective-permute-start | bytes 12296 | tf_op jit(solution)/shard_map/ppermute | solution.py:388
  125.8 14.8 %collective-permute-start.31 = (f32[8,128]{1,0:T(8,128)S(1)}, f32[8,128]{1,0:T(8,128)S(1)}, u32[]{:S(2)}, u32[]{:S(2)}) collective-permute-start(f32[8,128]{1,0:T(8,128)S(1)} %get-tuple-element.125), channel_id=1, source_target_pairs={{0,16},{16,0},{32,48},{48,32},{64,80},{80,64},{96,112},{112,96},{1... | collective-permute-start | bytes 12296 | tf_op jit(solution)/shard_map/ppermute | solution.py:388
  127.7 12.9 %collective-permute-start.30 = (f32[8,128]{1,0:T(8,128)S(1)}, f32[8,128]{1,0:T(8,128)S(1)}, u32[]{:S(2)}, u32[]{:S(2)}) collective-permute-start(f32[8,128]{1,0:T(8,128)S(1)} %get-tuple-element.125), channel_id=1, source_target_pairs={{0,1},{1,0},{2,3},{3,2},{4,5},{5,4},{6,7},{7,6},{8,9},{9,8},{10,11... | collective-permute-start | bytes 12296 | tf_op jit(solution)/shard_map/ppermute | solution.py:388
  145.1 14.6 %collective-permute-start.35 = (f32[8,128]{1,0:T(8,128)S(1)}, f32[8,128]{1,0:T(8,128)S(1)}, u32[]{:S(2)}, u32[]{:S(2)}) collective-permute-start(f32[8,128]{1,0:T(8,128)S(1)} %get-tuple-element.130), channel_id=1, source_target_pairs={{0,16},{16,0},{32,48},{48,32},{64,80},{80,64},{96,112},{112,96},{1... | collective-permute-start | bytes 12296 | tf_op jit(solution)/shard_map/ppermute | solution.py:388
  147.0 12.7 %collective-permute-start.34 = (f32[8,128]{1,0:T(8,128)S(1)}, f32[8,128]{1,0:T(8,128)S(1)}, u32[]{:S(2)}, u32[]{:S(2)}) collective-permute-start(f32[8,128]{1,0:T(8,128)S(1)} %get-tuple-element.130), channel_id=1, source_target_pairs={{0,1},{1,0},{2,3},{3,2},{4,5},{5,4},{6,7},{7,6},{8,9},{9,8},{10,11... | collective-permute-start | bytes 12296 | tf_op jit(solution)/shard_map/ppermute | solution.py:388
  162.9 14.8 %collective-permute-start.39 = (f32[8,128]{1,0:T(8,128)S(1)}, f32[8,128]{1,0:T(8,128)S(1)}, u32[]{:S(2)}, u32[]{:S(2)}) collective-permute-start(f32[8,128]{1,0:T(8,128)S(1)} %get-tuple-element.135), channel_id=1, source_target_pairs={{0,16},{16,0},{32,48},{48,32},{64,80},{80,64},{96,112},{112,96},{1... | collective-permute-start | bytes 12296 | tf_op jit(solution)/shard_map/ppermute | solution.py:388
  164.8 12.9 %collective-permute-start.38 = (f32[8,128]{1,0:T(8,128)S(1)}, f32[8,128]{1,0:T(8,128)S(1)}, u32[]{:S(2)}, u32[]{:S(2)}) collective-permute-start(f32[8,128]{1,0:T(8,128)S(1)} %get-tuple-element.135), channel_id=1, source_target_pairs={{0,1},{1,0},{2,3},{3,2},{4,5},{5,4},{6,7},{7,6},{8,9},{9,8},{10,11... | collective-permute-start | bytes 12296 | tf_op jit(solution)/shard_map/ppermute | solution.py:388
  182.2 14.6 %collective-permute-start.43 = (f32[8,128]{1,0:T(8,128)S(1)}, f32[8,128]{1,0:T(8,128)S(1)}, u32[]{:S(2)}, u32[]{:S(2)}) collective-permute-start(f32[8,128]{1,0:T(8,128)S(1)} %get-tuple-element.140), channel_id=1, source_target_pairs={{0,16},{16,0},{32,48},{48,32},{64,80},{80,64},{96,112},{112,96},{1... | collective-permute-start | bytes 12296 | tf_op jit(solution)/shard_map/ppermute | solution.py:388
  184.2 12.7 %collective-permute-start.42 = (f32[8,128]{1,0:T(8,128)S(1)}, f32[8,128]{1,0:T(8,128)S(1)}, u32[]{:S(2)}, u32[]{:S(2)}) collective-permute-start(f32[8,128]{1,0:T(8,128)S(1)} %get-tuple-element.140), channel_id=1, source_target_pairs={{0,1},{1,0},{2,3},{3,2},{4,5},{5,4},{6,7},{7,6},{8,9},{9,8},{10,11... | collective-permute-start | bytes 12296 | tf_op jit(solution)/shard_map/ppermute | solution.py:388
  200.0 14.8 %collective-permute-start.47 = (f32[8,128]{1,0:T(8,128)S(1)}, f32[8,128]{1,0:T(8,128)S(1)}, u32[]{:S(2)}, u32[]{:S(2)}) collective-permute-start(f32[8,128]{1,0:T(8,128)S(1)} %get-tuple-element.145), channel_id=1, source_target_pairs={{0,16},{16,0},{32,48},{48,32},{64,80},{80,64},{96,112},{112,96},{1... | collective-permute-start | bytes 12296 | tf_op jit(solution)/shard_map/ppermute | solution.py:388
  201.9 12.9 %collective-permute-start.46 = (f32[8,128]{1,0:T(8,128)S(1)}, f32[8,128]{1,0:T(8,128)S(1)}, u32[]{:S(2)}, u32[]{:S(2)}) collective-permute-start(f32[8,128]{1,0:T(8,128)S(1)} %get-tuple-element.145), channel_id=1, source_target_pairs={{0,1},{1,0},{2,3},{3,2},{4,5},{5,4},{6,7},{7,6},{8,9},{9,8},{10,11... | collective-permute-start | bytes 12296 | tf_op jit(solution)/shard_map/ppermute | solution.py:388
  219.3 14.6 %collective-permute-start.51 = (f32[8,128]{1,0:T(8,128)S(1)}, f32[8,128]{1,0:T(8,128)S(1)}, u32[]{:S(2)}, u32[]{:S(2)}) collective-permute-start(f32[8,128]{1,0:T(8,128)S(1)} %get-tuple-element.150), channel_id=1, source_target_pairs={{0,16},{16,0},{32,48},{48,32},{64,80},{80,64},{96,112},{112,96},{1... | collective-permute-start | bytes 12296 | tf_op jit(solution)/shard_map/ppermute | solution.py:388
  221.3 12.7 %collective-permute-start.50 = (f32[8,128]{1,0:T(8,128)S(1)}, f32[8,128]{1,0:T(8,128)S(1)}, u32[]{:S(2)}, u32[]{:S(2)}) collective-permute-start(f32[8,128]{1,0:T(8,128)S(1)} %get-tuple-element.150), channel_id=1, source_target_pairs={{0,1},{1,0},{2,3},{3,2},{4,5},{5,4},{6,7},{7,6},{8,9},{9,8},{10,11... | collective-permute-start | bytes 12296 | tf_op jit(solution)/shard_map/ppermute | solution.py:388
  237.1 15.0 %collective-permute-start.55 = (f32[8,128]{1,0:T(8,128)S(1)}, f32[8,128]{1,0:T(8,128)S(1)}, u32[]{:S(2)}, u32[]{:S(2)}) collective-permute-start(f32[8,128]{1,0:T(8,128)S(1)} %get-tuple-element.155), channel_id=1, source_target_pairs={{0,16},{16,0},{32,48},{48,32},{64,80},{80,64},{96,112},{112,96},{1... | collective-permute-start | bytes 12296 | tf_op jit(solution)/shard_map/ppermute | solution.py:388
  239.1 13.1 %collective-permute-start.54 = (f32[8,128]{1,0:T(8,128)S(1)}, f32[8,128]{1,0:T(8,128)S(1)}, u32[]{:S(2)}, u32[]{:S(2)}) collective-permute-start(f32[8,128]{1,0:T(8,128)S(1)} %get-tuple-element.155), channel_id=1, source_target_pairs={{0,1},{1,0},{2,3},{3,2},{4,5},{5,4},{6,7},{7,6},{8,9},{9,8},{10,11... | collective-permute-start | bytes 12296 | tf_op jit(solution)/shard_map/ppermute | solution.py:388
  256.5 14.6 %collective-permute-start.59 = (f32[8,128]{1,0:T(8,128)S(1)}, f32[8,128]{1,0:T(8,128)S(1)}, u32[]{:S(2)}, u32[]{:S(2)}) collective-permute-start(f32[8,128]{1,0:T(8,128)S(1)} %get-tuple-element.160), channel_id=1, source_target_pairs={{0,16},{16,0},{32,48},{48,32},{64,80},{80,64},{96,112},{112,96},{1... | collective-permute-start | bytes 12296 | tf_op jit(solution)/shard_map/ppermute | solution.py:388
  258.4 12.7 %collective-permute-start.58 = (f32[8,128]{1,0:T(8,128)S(1)}, f32[8,128]{1,0:T(8,128)S(1)}, u32[]{:S(2)}, u32[]{:S(2)}) collective-permute-start(f32[8,128]{1,0:T(8,128)S(1)} %get-tuple-element.160), channel_id=1, source_target_pairs={{0,1},{1,0},{2,3},{3,2},{4,5},{5,4},{6,7},{7,6},{8,9},{9,8},{10,11... | collective-permute-start | bytes 12296 | tf_op jit(solution)/shard_map/ppermute | solution.py:388
  274.2 14.8 %collective-permute-start.63 = (f32[8,128]{1,0:T(8,128)S(1)}, f32[8,128]{1,0:T(8,128)S(1)}, u32[]{:S(2)}, u32[]{:S(2)}) collective-permute-start(f32[8,128]{1,0:T(8,128)S(1)} %get-tuple-element.165), channel_id=1, source_target_pairs={{0,16},{16,0},{32,48},{48,32},{64,80},{80,64},{96,112},{112,96},{1... | collective-permute-start | bytes 12296 | tf_op jit(solution)/shard_map/ppermute | solution.py:388
  276.2 12.9 %collective-permute-start.62 = (f32[8,128]{1,0:T(8,128)S(1)}, f32[8,128]{1,0:T(8,128)S(1)}, u32[]{:S(2)}, u32[]{:S(2)}) collective-permute-start(f32[8,128]{1,0:T(8,128)S(1)} %get-tuple-element.165), channel_id=1, source_target_pairs={{0,1},{1,0},{2,3},{3,2},{4,5},{5,4},{6,7},{7,6},{8,9},{9,8},{10,11... | collective-permute-start | bytes 12296 | tf_op jit(solution)/shard_map/ppermute | solution.py:388
  (49 other events, 313.9 us)

commit v2 on v1

--- a/solution.py
+++ b/solution.py
@@ -15,20 +15,22 @@
 STEPS = 16
 LANES = 128
 FACES = 4
+GRADIENT_BLOCK = 32
+FORCE_BLOCK = 64
 
 time_step = 0.5
 
 EXCHANGES = ("dom1", "grp1", "dom0", "grp0")
 
 VMEM = pl.BlockSpec(memory_space=pltpu.VMEM)
-SMEM = pl.BlockSpec(memory_space=pltpu.SMEM)
-
-
-def kernel_call(body, outs, n_in, smem=(), scratch=()):
+HBM = pl.BlockSpec(memory_space=pltpu.MemorySpace.HBM)
+
+
+def kernel_call(body, outs, specs, scratch=()):
     return pl.pallas_call(
         body,
         out_shape=outs,
-        in_specs=[SMEM if i in smem else VMEM for i in range(n_in)],
+        in_specs=specs,
         out_specs=[VMEM] * len(outs),
         scratch_shapes=list(scratch),
         compiler_params=pltpu.CompilerParams(vmem_limit_bytes=24 * 1024 * 1024),
@@ -84,33 +86,87 @@
 
 
 def prepare_kernel(
-    connect,
-    lists,
-    swapped,
-    active,
-    mass_elem,
-    source_pattern,
+    wavelet_in,
+    neighbours_in,
+    connect_in,
+    lists_in,
+    mass_in,
+    source_in,
+    shape_in,
+    jacobian_in,
+    lame_in,
+    weights_in,
+    rank_in,
     incidence,
     field,
     send,
     pick_index,
     inverse_index,
+    connect,
+    left_gradient,
+    left_force,
+    wave,
+    inverse_jacobian,
+    lame_moduli,
+    point_weights,
+    rank,
+    element_nodes,
+    wavelet,
+    neighbours,
+    lists,
+    mass_elem,
+    source_pattern,
+    shape_t,
+    sems,
 ):
-    nodes = source_pattern.shape[1]
+    moves = [
+        (connect_in, element_nodes),
+        (wavelet_in, wavelet),
+        (neighbours_in, neighbours),
+        (lists_in, lists),
+        (mass_in, mass_elem),
+        (source_in, source_pattern),
+        (shape_in, shape_t),
+        (jacobian_in, inverse_jacobian),
+        (lame_in, lame_moduli),
+        (weights_in, point_weights),
+        (rank_in, rank),
+    ]
+    copies = [pltpu.make_async_copy(a, b, sems.at[i]) for i, (a, b) in enumerate(moves)]
+    for copy in copies:
+        copy.start()
+    copies[0].wait()
+    nodes = field.shape[1]
+    connect[...] = jnp.zeros(connect.shape, jnp.int32)
+    connect[0:EL_NODES, :] = element_nodes[...]
     lane = lax.broadcasted_iota(jnp.int32, (LANES, nodes), 1)
     for n in range(EL_NODES):
-        column = jnp.broadcast_to(connect[n : n + 1, :], (LANES, LANES)).T
+        column = jnp.broadcast_to(element_nodes[n : n + 1, :], (LANES, LANES)).T
         wide = jnp.concatenate([column] * (nodes // LANES), axis=1)
         incidence[n * LANES : (n + 1) * LANES, :] = jnp.where(wide == lane, 1.0, 0.0).astype(
             jnp.bfloat16
         )
-    listed = jnp.where(active[...] != 0, lists[...], -1)
+    for copy in copies[1:]:
+        copy.wait()
+    wave[...] = jnp.concatenate(
+        [jnp.full((1, LANES), wavelet[t], jnp.float32) for t in range(STEPS)], axis=0
+    )
+    face = [lists[0, k : k + 1, :] for k in range(FACES)]
+    listed = jnp.concatenate(face, axis=1)
+    swapped = jnp.concatenate([face[1], face[0], face[3], face[2]], axis=1)
+    side = lax.broadcasted_iota(jnp.int32, (1, LANES), 1) // (LANES // FACES)
+    open_side = jnp.where(
+        side < 2,
+        jnp.where(side == 0, neighbours[0, 0], neighbours[0, 1]),
+        jnp.where(side == 2, neighbours[0, 2], neighbours[0, 3]),
+    )
+    listed = jnp.where(open_side != 0, listed, -1)
     column = jnp.broadcast_to(listed, (LANES, LANES)).T
     wide = jnp.concatenate([column] * (nodes // LANES), axis=1)
     slot = lax.broadcasted_iota(jnp.int32, (LANES, nodes), 0) + 1
     found = jnp.sum(jnp.where(wide == lane, slot, 0), axis=0, keepdims=True)
     inverse_index[...] = jnp.broadcast_to(found - 1, (8, nodes))
-    index = jnp.broadcast_to(swapped[...], (8, LANES))
+    index = jnp.broadcast_to(swapped, (8, LANES))
     pick_index[...] = index
     rows = jnp.concatenate(
         [jnp.broadcast_to(mass_elem[n : n + 1, :], (8, LANES)) for n in range(EL_NODES)], axis=1
@@ -118,6 +174,42 @@
     field[...] = scatter_nodes(rows, incidence[...])
     field[0:3, :] = source_pattern[...]
     send[...] = pick_lanes(field[...], index)
+
+    reference_rows = 3 * POINTS
+    shape_rows = jnp.concatenate(
+        [shape_t[...], jnp.zeros((EL_NODES, LANES - reference_rows), jnp.float32)], axis=1
+    )
+    shape_rows = jnp.concatenate(
+        [shape_rows, jnp.zeros((LANES - EL_NODES, LANES), jnp.float32)], axis=0
+    )
+    forward = parts_of(shape_rows.T[0:reference_rows, :])
+    for j in range(3):
+        block = forward[j]
+        for i in range(1, 3 - j):
+            block = block + pltpu.roll(forward[j], i * GRADIENT_BLOCK, 1)
+        left_gradient[j * reference_rows : (j + 1) * reference_rows, :] = block[
+            :, 0 : 3 * GRADIENT_BLOCK
+        ].astype(jnp.bfloat16)
+    backward = parts_of(shape_rows[0:NODE_ROWS, :])
+    firsts, seconds = [], []
+    for j in range(3):
+        block = backward[j]
+        firsts.append(block if j == 2 else block + pltpu.roll(block, FORCE_BLOCK, 1))
+        seconds.append(block if j == 0 else jnp.zeros_like(block))
+    left_force[:, 0:LANES] = jnp.concatenate(firsts, axis=0).astype(jnp.bfloat16)
+    left_force[:, LANES:] = jnp.concatenate(seconds, axis=0)[:, 0:FORCE_BLOCK].astype(jnp.bfloat16)
+
+
+def stacked_parts(x, height):
+    gap = height - x.shape[0]
+    pieces = []
+    for part in parts_of(x):
+        pieces += [part, jnp.zeros((gap, x.shape[1]), jnp.float32)]
+    return jnp.concatenate(pieces, axis=0).astype(jnp.bfloat16)
+
+
+def wave_row(wave, step, width):
+    return jnp.concatenate([wave[step : step + 1, :]] * (width // LANES), axis=1)
 
 
 def strain_and_force(
@@ -149,7 +241,7 @@
             pieces.append(out)
         columns.append(jnp.concatenate(pieces, axis=0))
     node_values = jnp.concatenate(columns, axis=1)
-    right = jnp.concatenate(parts_of(node_values), axis=0).astype(jnp.bfloat16)
+    right = stacked_parts(node_values, GRADIENT_BLOCK)
     sums = matmul(left_gradient[...], right)
     height = 3 * POINTS
     along = (sums[2 * height :] + sums[height : 2 * height]) + sums[0:height]
@@ -192,7 +284,7 @@
         ]
         columns.append(jnp.concatenate(mapped, axis=0))
     mapped = jnp.concatenate(columns, axis=1)
-    right = jnp.concatenate(parts_of(mapped), axis=0).astype(jnp.bfloat16)
+    right = stacked_parts(mapped, FORCE_BLOCK)
     sums = matmul(left_force[...], right)
     node_forces = (sums[2 * NODE_ROWS :] + sums[NODE_ROWS : 2 * NODE_ROWS]) + sums[0:NODE_ROWS]
     row_id = lax.broadcasted_iota(jnp.int32, (8, LANES), 0)
@@ -207,7 +299,7 @@
 
 
 def first_kernel(
-    wavelet,
+    wave,
     dom1,
     grp1,
     dom0,
@@ -236,7 +328,7 @@
     scale = jnp.broadcast_to(time_step * (1.0 / total[3:4, :]), total.shape)
     pattern[...] = total
     half_inverse_mass[...] = scale
-    new_velocity = scale * (wavelet[0] * total)
+    new_velocity = scale * (wave_row(wave, 0, total.shape[1]) * total)
     velocity[...] = new_velocity
     new_displace = time_step * new_velocity
     displace[...] = new_displace
@@ -258,7 +350,7 @@
 
 def step_kernel(
     step,
-    wavelet,
+    wave,
     dom1,
     grp1,
     dom0,
@@ -283,7 +375,7 @@
 ):
     received = merge_received(source[...], dom1[...], grp1[...], dom0[...], grp0[...])
     stiff = old_force[...] + spread(received, inverse_index[...])
-    total = wavelet[step] * pattern[...] - stiff
+    total = wave_row(wave, step, stiff.shape[1]) * pattern[...] - stiff
     new_velocity = old_velocity[...] + half_inverse_mass[...] * total
     new_displace = old_displace[...] + time_step * new_velocity
     new_force = strain_and_force(
@@ -308,9 +400,10 @@
 
 def order_kernel(rank, *refs):
     strains, out, store = refs[:STEPS], refs[STEPS], refs[STEPS + 1]
-    per_step = STRAIN * POINTS
     for t in range(STEPS):
-        store[t * per_step : (t + 1) * per_step, :] = strains[t][...]
+        for c in range(STRAIN):
+            row = (c * STEPS + t) * POINTS
+            store[row : row + POINTS, :] = strains[t][c * POINTS : (c + 1) * POINTS, :]
     count = rank.shape[0] * LANES
     lane = lax.broadcasted_iota(jnp.int32, (LANES, count), 1)
     total = None
@@ -325,26 +418,10 @@
         out[w] = total[:, w * LANES : (w + 1) * LANES].astype(jnp.bfloat16)
 
 
-def place_kernel(pieces, out, store):
-    writers = pieces.shape[0]
-    for w in range(writers):
-        store[:, w * LANES : (w + 1) * LANES] = pieces[w].astype(jnp.float32)
-    for t in range(STEPS):
-        out[t] = store[t * STRAIN : (t + 1) * STRAIN, :].astype(jnp.bfloat16)
-
-
-def rounded(x):
-    return lax.reduce_precision(x, 8, 7)
-
-
-def left_operand(matrix, rows, columns):
-    padded = jnp.pad(matrix, ((0, rows - matrix.shape[0]), (0, columns - matrix.shape[1])))
-    high = rounded(padded)
-    middle = rounded(padded - high)
-    low = rounded(padded - high - middle)
-    zero = jnp.zeros_like(padded)
-    blocks = [[high, high, high], [middle, middle, zero], [low, zero, zero]]
-    return jnp.block(blocks).astype(jnp.bfloat16)
+def place_kernel(pieces, out):
+    for w in range(pieces.shape[0]):
+        for c in range(STRAIN):
+            out[c, :, w * LANES : (w + 1) * LANES] = pieces[w, c * STEPS : (c + 1) * STEPS, :]
 
 
 def shards(
@@ -367,15 +444,9 @@
     index_t = jax.ShapeDtypeStruct((8, LANES), jnp.int32)
     strain_t = jax.ShapeDtypeStruct((STRAIN * POINTS, LANES), f32)
 
-    lists = interface_nodes.reshape(1, LANES)
-    swapped = interface_nodes.reshape(2, 2, LANES // 4)[:, ::-1].reshape(1, LANES)
-    active = jnp.repeat(neighbours, LANES // FACES, axis=1)
     face = lax.broadcasted_iota(jnp.int32, (8, LANES), 1) // (LANES // FACES)
     parity = jnp.where(face < 2, lax.axis_index("grp") % 2, lax.axis_index("dom") % 2)
     source = 2 * (face // 2) + jnp.bitwise_xor(parity, 1 - face % 2)
-    left_gradient = left_operand(shape_grad, 3 * POINTS, NODE_ROWS)
-    left_force = left_operand(shape_grad.T, NODE_ROWS, 3 * POINTS)
-    padded_connect = jnp.pad(connect, ((0, NODE_ROWS - EL_NODES), (0, 0)))
 
     def exchange(send):
         received = []
@@ -388,33 +459,61 @@
             received.append(lax.ppermute(send, axis, pairs))
         return received
 
-    incidence, field, send, pick_index, inverse_index = kernel_call(
+    i32, bf16 = jnp.int32, jnp.bfloat16
+    rank_rows = point_rank.reshape(POINTS, LANES)
+    outs = kernel_call(
         prepare_kernel,
         [
-            jax.ShapeDtypeStruct((EL_NODES * LANES, nodes), jnp.bfloat16),
+            jax.ShapeDtypeStruct((EL_NODES * LANES, nodes), bf16),
             field_t,
             lanes_t,
             index_t,
-            jax.ShapeDtypeStruct((8, nodes), jnp.int32),
+            jax.ShapeDtypeStruct((8, nodes), i32),
+            jax.ShapeDtypeStruct((NODE_ROWS, LANES), i32),
+            jax.ShapeDtypeStruct((9 * POINTS, 3 * GRADIENT_BLOCK), bf16),
+            jax.ShapeDtypeStruct((3 * NODE_ROWS, 3 * FORCE_BLOCK), bf16),
+            jax.ShapeDtypeStruct((STEPS, LANES), f32),
+            jax.ShapeDtypeStruct(inverse_jacobian.shape, f32),
+            jax.ShapeDtypeStruct(lame_moduli.shape, f32),
+            jax.ShapeDtypeStruct(point_weights.shape, f32),
+            jax.ShapeDtypeStruct(rank_rows.shape, i32),
         ],
-        6,
-    )(connect, lists, swapped, active, mass_elem, source_pattern)
-    element_data = (
-        padded_connect,
-        left_gradient,
-        left_force,
-        inverse_jacobian,
-        lame_moduli,
-        point_weights,
-        incidence,
-    )
+        [HBM] * 11,
+        scratch=[
+            pltpu.VMEM(connect.shape, i32),
+            pltpu.SMEM(wavelet.shape, f32),
+            pltpu.SMEM(neighbours.shape, i32),
+            pltpu.VMEM(interface_nodes.shape, i32),
+            pltpu.VMEM(mass_elem.shape, f32),
+            pltpu.VMEM(source_pattern.shape, f32),
+            pltpu.VMEM(shape_grad.T.shape, f32),
+            pltpu.SemaphoreType.DMA((11,)),
+        ],
+    )(
+        *(
+            pltpu.with_memory_space_constraint(x, pltpu.MemorySpace.HBM)
+            for x in (
+                wavelet,
+                neighbours,
+                connect,
+                interface_nodes,
+                mass_elem,
+                source_pattern,
+                shape_grad.T,
+                inverse_jacobian,
+                lame_moduli,
+                point_weights,
+                rank_rows,
+            )
+        ),
+    )
+    incidence, field, send, pick_index, inverse_index = outs[:5]
+    wave, rank = outs[8], outs[12]
+    element_data = (*outs[5:8], *outs[9:12], incidence)
     received = exchange(send)
     strain, displace, velocity, pattern, half_inverse_mass, force, send = kernel_call(
-        first_kernel,
-        [strain_t, field_t, field_t, field_t, field_t, field_t, lanes_t],
-        16,
-        smem=(0,),
-    )(wavelet, *received, source, inverse_index, pick_index, field, *element_data)
+        first_kernel, [strain_t, field_t, field_t, field_t, field_t, field_t, lanes_t], [VMEM] * 16
+    )(wave, *received, source, inverse_index, pick_index, field, *element_data)
     strains = [strain]
     for step in range(1, STEPS):
         received = exchange(send)
@@ -422,10 +521,9 @@
         outs = kernel_call(
             functools.partial(step_kernel, step),
             [strain_t] + ([] if last else [field_t, field_t, field_t, lanes_t]),
-            20,
-            smem=(0,),
+            [VMEM] * 20,
         )(
-            wavelet,
+            wave,
             *received,
             source,
             inverse_index,
@@ -444,17 +542,14 @@
     (ordered,) = kernel_call(
         order_kernel,
         [jax.ShapeDtypeStruct((writers, STEPS * STRAIN, LANES), jnp.bfloat16)],
-        1 + STEPS,
+        [VMEM] * (1 + STEPS),
         scratch=[pltpu.VMEM((STEPS * STRAIN * POINTS, LANES), f32)],
-    )(point_rank.reshape(POINTS, LANES), *strains)
+    )(rank, *strains)
     pieces = lax.all_to_all(ordered, "dom", split_axis=0, concat_axis=0, tiled=True)
     (placed,) = kernel_call(
-        place_kernel,
-        [jax.ShapeDtypeStruct((STEPS, STRAIN, writers * LANES), jnp.bfloat16)],
-        1,
-        scratch=[pltpu.VMEM((STEPS * STRAIN, writers * LANES), f32)],
+        place_kernel, [jax.ShapeDtypeStruct((STRAIN, STEPS, writers * LANES), jnp.bfloat16)], [VMEM]
     )(pieces)
-    return placed
+    return placed.transpose(1, 0, 2)
 
 
 def solution(mesh):

time: 334 us -> 319 us (0.955)
  local copies, waits for them, and re-layouts: 9.69 us -> 0 us
  Pallas kernels: 29.8 us -> 22.7 us
    pallas_call x15, Pallas kernels: 24.8 us -> 16.8 us  [shards(): kernel_call(functools.partial(step_kernel, step), [strain_t] + ([] if las...]
    unnamed x19 -> x0, local copies, waits for them, and re-layouts: 5.63 us -> none
  transfers between devices with their start and end apart: 64 -> 64, of which waited for: 15 -> 16; matrix products, arithmetic and copies ran while one was open for 1% -> 0% of each run, Pallas kernels for 0% -> 0%
where the time goes in v2:
time: 319 us; the launch traced here: 317 us
  starting transfers between devices  224 us (70%)
  blocking collectives  35.8 us (11%)
  waiting for transfers between devices  33.2 us (10%)
  Pallas kernels  22.7 us (7%)
    ppermute x64, starting transfers between devices, exchange(): received.append(lax.ppermute(send, axis, pairs))  224 us
    all_to_all x1, blocking collectives, shards(): lax.all_to_all(ordered, 'dom', split_axis=0, concat_axis=0, tiled=True)  35.8 us
    ppermute x64, waiting for transfers between devices, exchange(): received.append(lax.ppermute(send, axis, pairs))  33.2 us
    pallas_call x15, Pallas kernels, shards(): kernel_call(functools.partial(step_kernel, step), [strain_t] + ([] if las...  16.8 us
  transfers between devices with their start and end apart: 64, of which 16 were waited for; matrix products, arithmetic and copies ran while one was open for 0% of the time, Pallas kernels for 0%

profile of v2, /device:TPU:201, one launch (start us, length us, event | category | flops | bytes accessed | tf_op | source)
XLA Modules:
  0.0 316.6 jit_solution(10754480277436079304)
XLA Ops:
  7.7 5.3 %collective-permute-start.1 = (f32[8,128]{1,0:T(8,128)S(1)}, f32[8,128]{1,0:T(8,128)S(1)}, u32[]{:S(2)}, u32[]{:S(2)}) collective-permute-start(f32[8,128]{1,0:T(8,128)S(1)} %get-tuple-element.97), channel_id=1, source_target_pairs={{16,32},{32,16},{48,64},{64,48},{80,96},{96,80},{112,128},{128,112... | collective-permute-start | bytes 12296 | tf_op jit(solution)/shard_map/ppermute | solution.py:459
  17.9 5.2 %collective-permute-start.6 = (f32[8,128]{1,0:T(8,128)S(1)}, f32[8,128]{1,0:T(8,128)S(1)}, u32[]{:S(2)}, u32[]{:S(2)}) collective-permute-start(f32[8,128]{1,0:T(8,128)S(1)} %get-tuple-element.109), channel_id=1, source_target_pairs={{0,1},{1,0},{2,3},{3,2},{4,5},{5,4},{6,7},{7,6},{8,9},{9,8},{10,11... | collective-permute-start | bytes 12296 | tf_op jit(solution)/shard_map/ppermute | solution.py:459
  33.2 6.7 %collective-permute-start.10 = (f32[8,128]{1,0:T(8,128)S(1)}, f32[8,128]{1,0:T(8,128)S(1)}, u32[]{:S(2)}, u32[]{:S(2)}) collective-permute-start(f32[8,128]{1,0:T(8,128)S(1)} %get-tuple-element.116), channel_id=1, source_target_pairs={{0,1},{1,0},{2,3},{3,2},{4,5},{5,4},{6,7},{7,6},{8,9},{9,8},{10,11... | collective-permute-start | bytes 12296 | tf_op jit(solution)/shard_map/ppermute | solution.py:459
  39.9 4.9 %collective-permute-start.9 = (f32[8,128]{1,0:T(8,128)S(1)}, f32[8,128]{1,0:T(8,128)S(1)}, u32[]{:S(2)}, u32[]{:S(2)}) collective-permute-start(f32[8,128]{1,0:T(8,128)S(1)} %get-tuple-element.116), channel_id=1, source_target_pairs={{16,32},{32,16},{48,64},{64,48},{80,96},{96,80},{112,128},{128,112... | collective-permute-start | bytes 12296 | tf_op jit(solution)/shard_map/ppermute | solution.py:459
  50.1 7.4 %collective-permute-start.14 = (f32[8,128]{1,0:T(8,128)S(1)}, f32[8,128]{1,0:T(8,128)S(1)}, u32[]{:S(2)}, u32[]{:S(2)}) collective-permute-start(f32[8,128]{1,0:T(8,128)S(1)} %get-tuple-element.121), channel_id=1, source_target_pairs={{0,1},{1,0},{2,3},{3,2},{4,5},{5,4},{6,7},{7,6},{8,9},{9,8},{10,11... | collective-permute-start | bytes 12296 | tf_op jit(solution)/shard_map/ppermute | solution.py:459
  67.6 5.9 %collective-permute-start.18 = (f32[8,128]{1,0:T(8,128)S(1)}, f32[8,128]{1,0:T(8,128)S(1)}, u32[]{:S(2)}, u32[]{:S(2)}) collective-permute-start(f32[8,128]{1,0:T(8,128)S(1)} %get-tuple-element.126), channel_id=1, source_target_pairs={{0,1},{1,0},{2,3},{3,2},{4,5},{5,4},{6,7},{7,6},{8,9},{9,8},{10,11... | collective-permute-start | bytes 12296 | tf_op jit(solution)/shard_map/ppermute | solution.py:459
  73.5 4.9 %collective-permute-start.17 = (f32[8,128]{1,0:T(8,128)S(1)}, f32[8,128]{1,0:T(8,128)S(1)}, u32[]{:S(2)}, u32[]{:S(2)}) collective-permute-start(f32[8,128]{1,0:T(8,128)S(1)} %get-tuple-element.126), channel_id=1, source_target_pairs={{16,32},{32,16},{48,64},{64,48},{80,96},{96,80},{112,128},{128,112... | collective-permute-start | bytes 12296 | tf_op jit(solution)/shard_map/ppermute | solution.py:459
  83.7 7.4 %collective-permute-start.22 = (f32[8,128]{1,0:T(8,128)S(1)}, f32[8,128]{1,0:T(8,128)S(1)}, u32[]{:S(2)}, u32[]{:S(2)}) collective-permute-start(f32[8,128]{1,0:T(8,128)S(1)} %get-tuple-element.131), channel_id=1, source_target_pairs={{0,1},{1,0},{2,3},{3,2},{4,5},{5,4},{6,7},{7,6},{8,9},{9,8},{10,11... | collective-permute-start | bytes 12296 | tf_op jit(solution)/shard_map/ppermute | solution.py:459
  101.2 6.1 %collective-permute-start.26 = (f32[8,128]{1,0:T(8,128)S(1)}, f32[8,128]{1,0:T(8,128)S(1)}, u32[]{:S(2)}, u32[]{:S(2)}) collective-permute-start(f32[8,128]{1,0:T(8,128)S(1)} %get-tuple-element.136), channel_id=1, source_target_pairs={{0,1},{1,0},{2,3},{3,2},{4,5},{5,4},{6,7},{7,6},{8,9},{9,8},{10,11... | collective-permute-start | bytes 12296 | tf_op jit(solution)/shard_map/ppermute | solution.py:459
  107.4 4.9 %collective-permute-start.25 = (f32[8,128]{1,0:T(8,128)S(1)}, f32[8,128]{1,0:T(8,128)S(1)}, u32[]{:S(2)}, u32[]{:S(2)}) collective-permute-start(f32[8,128]{1,0:T(8,128)S(1)} %get-tuple-element.136), channel_id=1, source_target_pairs={{16,32},{32,16},{48,64},{64,48},{80,96},{96,80},{112,128},{128,112... | collective-permute-start | bytes 12296 | tf_op jit(solution)/shard_map/ppermute | solution.py:459
  117.6 8.6 %collective-permute-start.30 = (f32[8,128]{1,0:T(8,128)S(1)}, f32[8,128]{1,0:T(8,128)S(1)}, u32[]{:S(2)}, u32[]{:S(2)}) collective-permute-start(f32[8,128]{1,0:T(8,128)S(1)} %get-tuple-element.141), channel_id=1, source_target_pairs={{0,1},{1,0},{2,3},{3,2},{4,5},{5,4},{6,7},{7,6},{8,9},{9,8},{10,11... | collective-permute-start | bytes 12296 | tf_op jit(solution)/shard_map/ppermute | solution.py:459
  136.3 7.1 %collective-permute-start.34 = (f32[8,128]{1,0:T(8,128)S(1)}, f32[8,128]{1,0:T(8,128)S(1)}, u32[]{:S(2)}, u32[]{:S(2)}) collective-permute-start(f32[8,128]{1,0:T(8,128)S(1)} %get-tuple-element.146), channel_id=1, source_target_pairs={{0,1},{1,0},{2,3},{3,2},{4,5},{5,4},{6,7},{7,6},{8,9},{9,8},{10,11... | collective-permute-start | bytes 12296 | tf_op jit(solution)/shard_map/ppermute | solution.py:459
  143.4 4.9 %collective-permute-start.33 = (f32[8,128]{1,0:T(8,128)S(1)}, f32[8,128]{1,0:T(8,128)S(1)}, u32[]{:S(2)}, u32[]{:S(2)}) collective-permute-start(f32[8,128]{1,0:T(8,128)S(1)} %get-tuple-element.146), channel_id=1, source_target_pairs={{16,32},{32,16},{48,64},{64,48},{80,96},{96,80},{112,128},{128,112... | collective-permute-start | bytes 12296 | tf_op jit(solution)/shard_map/ppermute | solution.py:459
  153.6 8.6 %collective-permute-start.38 = (f32[8,128]{1,0:T(8,128)S(1)}, f32[8,128]{1,0:T(8,128)S(1)}, u32[]{:S(2)}, u32[]{:S(2)}) collective-permute-start(f32[8,128]{1,0:T(8,128)S(1)} %get-tuple-element.151), channel_id=1, source_target_pairs={{0,1},{1,0},{2,3},{3,2},{4,5},{5,4},{6,7},{7,6},{8,9},{9,8},{10,11... | collective-permute-start | bytes 12296 | tf_op jit(solution)/shard_map/ppermute | solution.py:459
  172.4 7.1 %collective-permute-start.42 = (f32[8,128]{1,0:T(8,128)S(1)}, f32[8,128]{1,0:T(8,128)S(1)}, u32[]{:S(2)}, u32[]{:S(2)}) collective-permute-start(f32[8,128]{1,0:T(8,128)S(1)} %get-tuple-element.156), channel_id=1, source_target_pairs={{0,1},{1,0},{2,3},{3,2},{4,5},{5,4},{6,7},{7,6},{8,9},{9,8},{10,11... | collective-permute-start | bytes 12296 | tf_op jit(solution)/shard_map/ppermute | solution.py:459
  179.5 4.9 %collective-permute-start.41 = (f32[8,128]{1,0:T(8,128)S(1)}, f32[8,128]{1,0:T(8,128)S(1)}, u32[]{:S(2)}, u32[]{:S(2)}) collective-permute-start(f32[8,128]{1,0:T(8,128)S(1)} %get-tuple-element.156), channel_id=1, source_target_pairs={{16,32},{32,16},{48,64},{64,48},{80,96},{96,80},{112,128},{128,112... | collective-permute-start | bytes 12296 | tf_op jit(solution)/shard_map/ppermute | solution.py:459
  189.6 8.6 %collective-permute-start.46 = (f32[8,128]{1,0:T(8,128)S(1)}, f32[8,128]{1,0:T(8,128)S(1)}, u32[]{:S(2)}, u32[]{:S(2)}) collective-permute-start(f32[8,128]{1,0:T(8,128)S(1)} %get-tuple-element.161), channel_id=1, source_target_pairs={{0,1},{1,0},{2,3},{3,2},{4,5},{5,4},{6,7},{7,6},{8,9},{9,8},{10,11... | collective-permute-start | bytes 12296 | tf_op jit(solution)/shard_map/ppermute | solution.py:459
  208.4 7.1 %collective-permute-start.50 = (f32[8,128]{1,0:T(8,128)S(1)}, f32[8,128]{1,0:T(8,128)S(1)}, u32[]{:S(2)}, u32[]{:S(2)}) collective-permute-start(f32[8,128]{1,0:T(8,128)S(1)} %get-tuple-element.166), channel_id=1, source_target_pairs={{0,1},{1,0},{2,3},{3,2},{4,5},{5,4},{6,7},{7,6},{8,9},{9,8},{10,11... | collective-permute-start | bytes 12296 | tf_op jit(solution)/shard_map/ppermute | solution.py:459
  215.6 4.9 %collective-permute-start.49 = (f32[8,128]{1,0:T(8,128)S(1)}, f32[8,128]{1,0:T(8,128)S(1)}, u32[]{:S(2)}, u32[]{:S(2)}) collective-permute-start(f32[8,128]{1,0:T(8,128)S(1)} %get-tuple-element.166), channel_id=1, source_target_pairs={{16,32},{32,16},{48,64},{64,48},{80,96},{96,80},{112,128},{128,112... | collective-permute-start | bytes 12296 | tf_op jit(solution)/shard_map/ppermute | solution.py:459
  225.7 8.6 %collective-permute-start.54 = (f32[8,128]{1,0:T(8,128)S(1)}, f32[8,128]{1,0:T(8,128)S(1)}, u32[]{:S(2)}, u32[]{:S(2)}) collective-permute-start(f32[8,128]{1,0:T(8,128)S(1)} %get-tuple-element.171), channel_id=1, source_target_pairs={{0,1},{1,0},{2,3},{3,2},{4,5},{5,4},{6,7},{7,6},{8,9},{9,8},{10,11... | collective-permute-start | bytes 12296 | tf_op jit(solution)/shard_map/ppermute | solution.py:459
  244.5 7.1 %collective-permute-start.58 = (f32[8,128]{1,0:T(8,128)S(1)}, f32[8,128]{1,0:T(8,128)S(1)}, u32[]{:S(2)}, u32[]{:S(2)}) collective-permute-start(f32[8,128]{1,0:T(8,128)S(1)} %get-tuple-element.176), channel_id=1, source_target_pairs={{0,1},{1,0},{2,3},{3,2},{4,5},{5,4},{6,7},{7,6},{8,9},{9,8},{10,11... | collective-permute-start | bytes 12296 | tf_op jit(solution)/shard_map/ppermute | solution.py:459
  251.6 4.9 %collective-permute-start.57 = (f32[8,128]{1,0:T(8,128)S(1)}, f32[8,128]{1,0:T(8,128)S(1)}, u32[]{:S(2)}, u32[]{:S(2)}) collective-permute-start(f32[8,128]{1,0:T(8,128)S(1)} %get-tuple-element.176), channel_id=1, source_target_pairs={{16,32},{32,16},{48,64},{64,48},{80,96},{96,80},{112,128},{128,112... | collective-permute-start | bytes 12296 | tf_op jit(solution)/shard_map/ppermute | solution.py:459
  261.8 8.8 %collective-permute-start.62 = (f32[8,128]{1,0:T(8,128)S(1)}, f32[8,128]{1,0:T(8,128)S(1)}, u32[]{:S(2)}, u32[]{:S(2)}) collective-permute-start(f32[8,128]{1,0:T(8,128)S(1)} %get-tuple-element.181), channel_id=1, source_target_pairs={{0,1},{1,0},{2,3},{3,2},{4,5},{5,4},{6,7},{7,6},{8,9},{9,8},{10,11... | collective-permute-start | bytes 12296 | tf_op jit(solution)/shard_map/ppermute | solution.py:459
  280.0 35.8 %all_to_all.5.pieces = bf16[16,96,128]{2,1,0:T(8,128)(2,1)S(1)} all-to-all(bf16[16,96,128]{2,1,0:T(8,128)(2,1)S(1)} %shard_map.126), channel_id=1, replica_groups=mesh['grp'=32,'dom'=16] {'dom'}, dimensions={0} | all-to-all | bytes 786432 | tf_op jit(solution)/shard_map/all_to_all | solution.py:548
  (127 shorter events, 129.9 us)
Async XLA Ops:
  31.2 14.2 %collective-permute-start.11 = (f32[8,128]{1,0:T(8,128)S(1)}, f32[8,128]{1,0:T(8,128)S(1)}, u32[]{:S(2)}, u32[]{:S(2)}) collective-permute-start(f32[8,128]{1,0:T(8,128)S(1)} %get-tuple-element.116), channel_id=1, source_target_pairs={{0,16},{16,0},{32,48},{48,32},{64,80},{80,64},{96,112},{112,96},{1... | collective-permute-start | bytes 12296 | tf_op jit(solution)/shard_map/ppermute | solution.py:459
  33.2 12.3 %collective-permute-start.10 = (f32[8,128]{1,0:T(8,128)S(1)}, f32[8,128]{1,0:T(8,128)S(1)}, u32[]{:S(2)}, u32[]{:S(2)}) collective-permute-start(f32[8,128]{1,0:T(8,128)S(1)} %get-tuple-element.116), channel_id=1, source_target_pairs={{0,1},{1,0},{2,3},{3,2},{4,5},{5,4},{6,7},{7,6},{8,9},{9,8},{10,11... | collective-permute-start | bytes 12296 | tf_op jit(solution)/shard_map/ppermute | solution.py:459
  48.1 13.4 %collective-permute-start.15 = (f32[8,128]{1,0:T(8,128)S(1)}, f32[8,128]{1,0:T(8,128)S(1)}, u32[]{:S(2)}, u32[]{:S(2)}) collective-permute-start(f32[8,128]{1,0:T(8,128)S(1)} %get-tuple-element.121), channel_id=1, source_target_pairs={{0,16},{16,0},{32,48},{48,32},{64,80},{80,64},{96,112},{112,96},{1... | collective-permute-start | bytes 12296 | tf_op jit(solution)/shard_map/ppermute | solution.py:459
  65.7 13.4 %collective-permute-start.19 = (f32[8,128]{1,0:T(8,128)S(1)}, f32[8,128]{1,0:T(8,128)S(1)}, u32[]{:S(2)}, u32[]{:S(2)}) collective-permute-start(f32[8,128]{1,0:T(8,128)S(1)} %get-tuple-element.126), channel_id=1, source_target_pairs={{0,16},{16,0},{32,48},{48,32},{64,80},{80,64},{96,112},{112,96},{1... | collective-permute-start | bytes 12296 | tf_op jit(solution)/shard_map/ppermute | solution.py:459
  81.7 13.4 %collective-permute-start.23 = (f32[8,128]{1,0:T(8,128)S(1)}, f32[8,128]{1,0:T(8,128)S(1)}, u32[]{:S(2)}, u32[]{:S(2)}) collective-permute-start(f32[8,128]{1,0:T(8,128)S(1)} %get-tuple-element.131), channel_id=1, source_target_pairs={{0,16},{16,0},{32,48},{48,32},{64,80},{80,64},{96,112},{112,96},{1... | collective-permute-start | bytes 12296 | tf_op jit(solution)/shard_map/ppermute | solution.py:459
  99.3 13.7 %collective-permute-start.27 = (f32[8,128]{1,0:T(8,128)S(1)}, f32[8,128]{1,0:T(8,128)S(1)}, u32[]{:S(2)}, u32[]{:S(2)}) collective-permute-start(f32[8,128]{1,0:T(8,128)S(1)} %get-tuple-element.136), channel_id=1, source_target_pairs={{0,16},{16,0},{32,48},{48,32},{64,80},{80,64},{96,112},{112,96},{1... | collective-permute-start | bytes 12296 | tf_op jit(solution)/shard_map/ppermute | solution.py:459
  115.6 14.8 %collective-permute-start.31 = (f32[8,128]{1,0:T(8,128)S(1)}, f32[8,128]{1,0:T(8,128)S(1)}, u32[]{:S(2)}, u32[]{:S(2)}) collective-permute-start(f32[8,128]{1,0:T(8,128)S(1)} %get-tuple-element.141), channel_id=1, source_target_pairs={{0,16},{16,0},{32,48},{48,32},{64,80},{80,64},{96,112},{112,96},{1... | collective-permute-start | bytes 12296 | tf_op jit(solution)/shard_map/ppermute | solution.py:459
  117.6 12.9 %collective-permute-start.30 = (f32[8,128]{1,0:T(8,128)S(1)}, f32[8,128]{1,0:T(8,128)S(1)}, u32[]{:S(2)}, u32[]{:S(2)}) collective-permute-start(f32[8,128]{1,0:T(8,128)S(1)} %get-tuple-element.141), channel_id=1, source_target_pairs={{0,1},{1,0},{2,3},{3,2},{4,5},{5,4},{6,7},{7,6},{8,9},{9,8},{10,11... | collective-permute-start | bytes 12296 | tf_op jit(solution)/shard_map/ppermute | solution.py:459
  134.4 14.6 %collective-permute-start.35 = (f32[8,128]{1,0:T(8,128)S(1)}, f32[8,128]{1,0:T(8,128)S(1)}, u32[]{:S(2)}, u32[]{:S(2)}) collective-permute-start(f32[8,128]{1,0:T(8,128)S(1)} %get-tuple-element.146), channel_id=1, source_target_pairs={{0,16},{16,0},{32,48},{48,32},{64,80},{80,64},{96,112},{112,96},{1... | collective-permute-start | bytes 12296 | tf_op jit(solution)/shard_map/ppermute | solution.py:459
  136.3 12.7 %collective-permute-start.34 = (f32[8,128]{1,0:T(8,128)S(1)}, f32[8,128]{1,0:T(8,128)S(1)}, u32[]{:S(2)}, u32[]{:S(2)}) collective-permute-start(f32[8,128]{1,0:T(8,128)S(1)} %get-tuple-element.146), channel_id=1, source_target_pairs={{0,1},{1,0},{2,3},{3,2},{4,5},{5,4},{6,7},{7,6},{8,9},{9,8},{10,11... | collective-permute-start | bytes 12296 | tf_op jit(solution)/shard_map/ppermute | solution.py:459
  151.7 14.8 %collective-permute-start.39 = (f32[8,128]{1,0:T(8,128)S(1)}, f32[8,128]{1,0:T(8,128)S(1)}, u32[]{:S(2)}, u32[]{:S(2)}) collective-permute-start(f32[8,128]{1,0:T(8,128)S(1)} %get-tuple-element.151), channel_id=1, source_target_pairs={{0,16},{16,0},{32,48},{48,32},{64,80},{80,64},{96,112},{112,96},{1... | collective-permute-start | bytes 12296 | tf_op jit(solution)/shard_map/ppermute | solution.py:459
  153.6 12.9 %collective-permute-start.38 = (f32[8,128]{1,0:T(8,128)S(1)}, f32[8,128]{1,0:T(8,128)S(1)}, u32[]{:S(2)}, u32[]{:S(2)}) collective-permute-start(f32[8,128]{1,0:T(8,128)S(1)} %get-tuple-element.151), channel_id=1, source_target_pairs={{0,1},{1,0},{2,3},{3,2},{4,5},{5,4},{6,7},{7,6},{8,9},{9,8},{10,11... | collective-permute-start | bytes 12296 | tf_op jit(solution)/shard_map/ppermute | solution.py:459
  170.4 14.6 %collective-permute-start.43 = (f32[8,128]{1,0:T(8,128)S(1)}, f32[8,128]{1,0:T(8,128)S(1)}, u32[]{:S(2)}, u32[]{:S(2)}) collective-permute-start(f32[8,128]{1,0:T(8,128)S(1)} %get-tuple-element.156), channel_id=1, source_target_pairs={{0,16},{16,0},{32,48},{48,32},{64,80},{80,64},{96,112},{112,96},{1... | collective-permute-start | bytes 12296 | tf_op jit(solution)/shard_map/ppermute | solution.py:459
  172.4 12.7 %collective-permute-start.42 = (f32[8,128]{1,0:T(8,128)S(1)}, f32[8,128]{1,0:T(8,128)S(1)}, u32[]{:S(2)}, u32[]{:S(2)}) collective-permute-start(f32[8,128]{1,0:T(8,128)S(1)} %get-tuple-element.156), channel_id=1, source_target_pairs={{0,1},{1,0},{2,3},{3,2},{4,5},{5,4},{6,7},{7,6},{8,9},{9,8},{10,11... | collective-permute-start | bytes 12296 | tf_op jit(solution)/shard_map/ppermute | solution.py:459
  187.7 14.8 %collective-permute-start.47 = (f32[8,128]{1,0:T(8,128)S(1)}, f32[8,128]{1,0:T(8,128)S(1)}, u32[]{:S(2)}, u32[]{:S(2)}) collective-permute-start(f32[8,128]{1,0:T(8,128)S(1)} %get-tuple-element.161), channel_id=1, source_target_pairs={{0,16},{16,0},{32,48},{48,32},{64,80},{80,64},{96,112},{112,96},{1... | collective-permute-start | bytes 12296 | tf_op jit(solution)/shard_map/ppermute | solution.py:459
  189.6 12.9 %collective-permute-start.46 = (f32[8,128]{1,0:T(8,128)S(1)}, f32[8,128]{1,0:T(8,128)S(1)}, u32[]{:S(2)}, u32[]{:S(2)}) collective-permute-start(f32[8,128]{1,0:T(8,128)S(1)} %get-tuple-element.161), channel_id=1, source_target_pairs={{0,1},{1,0},{2,3},{3,2},{4,5},{5,4},{6,7},{7,6},{8,9},{9,8},{10,11... | collective-permute-start | bytes 12296 | tf_op jit(solution)/shard_map/ppermute | solution.py:459
  206.5 14.6 %collective-permute-start.51 = (f32[8,128]{1,0:T(8,128)S(1)}, f32[8,128]{1,0:T(8,128)S(1)}, u32[]{:S(2)}, u32[]{:S(2)}) collective-permute-start(f32[8,128]{1,0:T(8,128)S(1)} %get-tuple-element.166), channel_id=1, source_target_pairs={{0,16},{16,0},{32,48},{48,32},{64,80},{80,64},{96,112},{112,96},{1... | collective-permute-start | bytes 12296 | tf_op jit(solution)/shard_map/ppermute | solution.py:459
  208.4 12.7 %collective-permute-start.50 = (f32[8,128]{1,0:T(8,128)S(1)}, f32[8,128]{1,0:T(8,128)S(1)}, u32[]{:S(2)}, u32[]{:S(2)}) collective-permute-start(f32[8,128]{1,0:T(8,128)S(1)} %get-tuple-element.166), channel_id=1, source_target_pairs={{0,1},{1,0},{2,3},{3,2},{4,5},{5,4},{6,7},{7,6},{8,9},{9,8},{10,11... | collective-permute-start | bytes 12296 | tf_op jit(solution)/shard_map/ppermute | solution.py:459
  223.8 14.8 %collective-permute-start.55 = (f32[8,128]{1,0:T(8,128)S(1)}, f32[8,128]{1,0:T(8,128)S(1)}, u32[]{:S(2)}, u32[]{:S(2)}) collective-permute-start(f32[8,128]{1,0:T(8,128)S(1)} %get-tuple-element.171), channel_id=1, source_target_pairs={{0,16},{16,0},{32,48},{48,32},{64,80},{80,64},{96,112},{112,96},{1... | collective-permute-start | bytes 12296 | tf_op jit(solution)/shard_map/ppermute | solution.py:459
  225.7 12.9 %collective-permute-start.54 = (f32[8,128]{1,0:T(8,128)S(1)}, f32[8,128]{1,0:T(8,128)S(1)}, u32[]{:S(2)}, u32[]{:S(2)}) collective-permute-start(f32[8,128]{1,0:T(8,128)S(1)} %get-tuple-element.171), channel_id=1, source_target_pairs={{0,1},{1,0},{2,3},{3,2},{4,5},{5,4},{6,7},{7,6},{8,9},{9,8},{10,11... | collective-permute-start | bytes 12296 | tf_op jit(solution)/shard_map/ppermute | solution.py:459
  242.5 14.8 %collective-permute-start.59 = (f32[8,128]{1,0:T(8,128)S(1)}, f32[8,128]{1,0:T(8,128)S(1)}, u32[]{:S(2)}, u32[]{:S(2)}) collective-permute-start(f32[8,128]{1,0:T(8,128)S(1)} %get-tuple-element.176), channel_id=1, source_target_pairs={{0,16},{16,0},{32,48},{48,32},{64,80},{80,64},{96,112},{112,96},{1... | collective-permute-start | bytes 12296 | tf_op jit(solution)/shard_map/ppermute | solution.py:459
  244.5 12.9 %collective-permute-start.58 = (f32[8,128]{1,0:T(8,128)S(1)}, f32[8,128]{1,0:T(8,128)S(1)}, u32[]{:S(2)}, u32[]{:S(2)}) collective-permute-start(f32[8,128]{1,0:T(8,128)S(1)} %get-tuple-element.176), channel_id=1, source_target_pairs={{0,1},{1,0},{2,3},{3,2},{4,5},{5,4},{6,7},{7,6},{8,9},{9,8},{10,11... | collective-permute-start | bytes 12296 | tf_op jit(solution)/shard_map/ppermute | solution.py:459
  259.8 15.0 %collective-permute-start.63 = (f32[8,128]{1,0:T(8,128)S(1)}, f32[8,128]{1,0:T(8,128)S(1)}, u32[]{:S(2)}, u32[]{:S(2)}) collective-permute-start(f32[8,128]{1,0:T(8,128)S(1)} %get-tuple-element.181), channel_id=1, source_target_pairs={{0,16},{16,0},{32,48},{48,32},{64,80},{80,64},{96,112},{112,96},{1... | collective-permute-start | bytes 12296 | tf_op jit(solution)/shard_map/ppermute | solution.py:459
  261.8 13.1 %collective-permute-start.62 = (f32[8,128]{1,0:T(8,128)S(1)}, f32[8,128]{1,0:T(8,128)S(1)}, u32[]{:S(2)}, u32[]{:S(2)}) collective-permute-start(f32[8,128]{1,0:T(8,128)S(1)} %get-tuple-element.181), channel_id=1, source_target_pairs={{0,1},{1,0},{2,3},{3,2},{4,5},{5,4},{6,7},{7,6},{8,9},{9,8},{10,11... | collective-permute-start | bytes 12296 | tf_op jit(solution)/shard_map/ppermute | solution.py:459
  (40 other events, 245.6 us)

commit v3 on v2

--- a/solution.py
+++ b/solution.py
@@ -20,10 +20,17 @@
 
 time_step = 0.5
 
+DOM_ROW = 4
+
 EXCHANGES = ("dom1", "grp1", "dom0", "grp0")
 
 VMEM = pl.BlockSpec(memory_space=pltpu.VMEM)
 HBM = pl.BlockSpec(memory_space=pltpu.MemorySpace.HBM)
+
+
+def snake(axis, index):
+    row, column = index // DOM_ROW, index % DOM_ROW
+    return index if axis == "grp" or row % 2 == 0 else row * DOM_ROW + DOM_ROW - 1 - column
 
 
 def kernel_call(body, outs, specs, scratch=()):
@@ -85,7 +92,19 @@
     return (sums[16:24] + sums[8:16]) + sums[0:8]
 
 
-def prepare_kernel(
+CONNECT_ROW = 0
+MASS_ROW = 24
+LAME_ROW = 44
+LISTED_ROW = 46
+SWAPPED_ROW = 47
+JACOBIAN_ROW = 48
+WEIGHTS_ROW = 64
+SOURCE_ROW = 80
+RANK_ROW = 96
+PACKED_ROWS = 112
+
+
+def pack_kernel(
     wavelet_in,
     neighbours_in,
     connect_in,
@@ -97,6 +116,69 @@
     lame_in,
     weights_in,
     rank_in,
+    packed,
+    shape_t,
+    wave,
+    wavelet,
+    neighbours,
+    connect,
+    lists,
+    mass_elem,
+    source_pattern,
+    jacobian,
+    lame,
+    weights,
+    rank,
+    sems,
+):
+    moves = [
+        (wavelet_in, wavelet),
+        (neighbours_in, neighbours),
+        (connect_in, connect),
+        (lists_in, lists),
+        (mass_in, mass_elem),
+        (source_in, source_pattern),
+        (shape_in, shape_t),
+        (jacobian_in, jacobian),
+        (lame_in, lame),
+        (weights_in, weights),
+        (rank_in, rank),
+    ]
+    copies = [pltpu.make_async_copy(a, b, sems.at[i]) for i, (a, b) in enumerate(moves)]
+    for copy in copies:
+        copy.start()
+    packed[...] = jnp.zeros(packed.shape, jnp.float32)
+    for copy in copies:
+        copy.wait()
+    wave[...] = jnp.concatenate(
+        [jnp.full((1, LANES), wavelet[t], jnp.float32) for t in range(STEPS)], axis=0
+    )
+    packed[CONNECT_ROW : CONNECT_ROW + EL_NODES, :] = connect[...].astype(jnp.float32)
+    packed[MASS_ROW : MASS_ROW + EL_NODES, :] = mass_elem[...]
+    packed[LAME_ROW : LAME_ROW + 2, :] = lame[...]
+    packed[JACOBIAN_ROW : JACOBIAN_ROW + 9, :] = jacobian[...]
+    packed[WEIGHTS_ROW : WEIGHTS_ROW + POINTS, :] = weights[...]
+    packed[RANK_ROW : RANK_ROW + POINTS, :] = rank[...].astype(jnp.float32)
+    for j in range(source_pattern.shape[1] // LANES):
+        row = SOURCE_ROW + 3 * j
+        packed[row : row + 3, :] = source_pattern[:, j * LANES : (j + 1) * LANES]
+    face = [lists[0, k : k + 1, :] for k in range(FACES)]
+    listed = jnp.concatenate(face, axis=1)
+    swapped = jnp.concatenate([face[1], face[0], face[3], face[2]], axis=1)
+    side = lax.broadcasted_iota(jnp.int32, (1, LANES), 1) // (LANES // FACES)
+    open_side = jnp.where(
+        side < 2,
+        jnp.where(side == 0, neighbours[0, 0], neighbours[0, 1]),
+        jnp.where(side == 2, neighbours[0, 2], neighbours[0, 3]),
+    )
+    listed = jnp.where(open_side != 0, listed, -1)
+    packed[LISTED_ROW : LISTED_ROW + 1, :] = listed.astype(jnp.float32)
+    packed[SWAPPED_ROW : SWAPPED_ROW + 1, :] = swapped.astype(jnp.float32)
+
+
+def prepare_kernel(
+    packed,
+    shape_t,
     incidence,
     field,
     send,
@@ -105,40 +187,18 @@
     connect,
     left_gradient,
     left_force,
-    wave,
     inverse_jacobian,
     lame_moduli,
     point_weights,
     rank,
-    element_nodes,
-    wavelet,
-    neighbours,
-    lists,
-    mass_elem,
-    source_pattern,
-    shape_t,
-    sems,
 ):
-    moves = [
-        (connect_in, element_nodes),
-        (wavelet_in, wavelet),
-        (neighbours_in, neighbours),
-        (lists_in, lists),
-        (mass_in, mass_elem),
-        (source_in, source_pattern),
-        (shape_in, shape_t),
-        (jacobian_in, inverse_jacobian),
-        (lame_in, lame_moduli),
-        (weights_in, point_weights),
-        (rank_in, rank),
-    ]
-    copies = [pltpu.make_async_copy(a, b, sems.at[i]) for i, (a, b) in enumerate(moves)]
-    for copy in copies:
-        copy.start()
-    copies[0].wait()
     nodes = field.shape[1]
-    connect[...] = jnp.zeros(connect.shape, jnp.int32)
-    connect[0:EL_NODES, :] = element_nodes[...]
+    element_nodes = packed[CONNECT_ROW : CONNECT_ROW + NODE_ROWS, :].astype(jnp.int32)
+    connect[...] = element_nodes
+    inverse_jacobian[...] = packed[JACOBIAN_ROW : JACOBIAN_ROW + 9, :]
+    lame_moduli[...] = packed[LAME_ROW : LAME_ROW + 2, :]
+    point_weights[...] = packed[WEIGHTS_ROW : WEIGHTS_ROW + POINTS, :]
+    rank[...] = packed[RANK_ROW : RANK_ROW + POINTS, :].astype(jnp.int32)
     lane = lax.broadcasted_iota(jnp.int32, (LANES, nodes), 1)
     for n in range(EL_NODES):
         column = jnp.broadcast_to(element_nodes[n : n + 1, :], (LANES, LANES)).T
@@ -146,33 +206,26 @@
         incidence[n * LANES : (n + 1) * LANES, :] = jnp.where(wide == lane, 1.0, 0.0).astype(
             jnp.bfloat16
         )
-    for copy in copies[1:]:
-        copy.wait()
-    wave[...] = jnp.concatenate(
-        [jnp.full((1, LANES), wavelet[t], jnp.float32) for t in range(STEPS)], axis=0
-    )
-    face = [lists[0, k : k + 1, :] for k in range(FACES)]
-    listed = jnp.concatenate(face, axis=1)
-    swapped = jnp.concatenate([face[1], face[0], face[3], face[2]], axis=1)
-    side = lax.broadcasted_iota(jnp.int32, (1, LANES), 1) // (LANES // FACES)
-    open_side = jnp.where(
-        side < 2,
-        jnp.where(side == 0, neighbours[0, 0], neighbours[0, 1]),
-        jnp.where(side == 2, neighbours[0, 2], neighbours[0, 3]),
-    )
-    listed = jnp.where(open_side != 0, listed, -1)
+    listed = packed[LISTED_ROW : LISTED_ROW + 1, :].astype(jnp.int32)
     column = jnp.broadcast_to(listed, (LANES, LANES)).T
     wide = jnp.concatenate([column] * (nodes // LANES), axis=1)
     slot = lax.broadcasted_iota(jnp.int32, (LANES, nodes), 0) + 1
     found = jnp.sum(jnp.where(wide == lane, slot, 0), axis=0, keepdims=True)
     inverse_index[...] = jnp.broadcast_to(found - 1, (8, nodes))
+    swapped = packed[SWAPPED_ROW : SWAPPED_ROW + 1, :].astype(jnp.int32)
     index = jnp.broadcast_to(swapped, (8, LANES))
     pick_index[...] = index
     rows = jnp.concatenate(
-        [jnp.broadcast_to(mass_elem[n : n + 1, :], (8, LANES)) for n in range(EL_NODES)], axis=1
+        [
+            jnp.broadcast_to(packed[MASS_ROW + n : MASS_ROW + n + 1, :], (8, LANES))
+            for n in range(EL_NODES)
+        ],
+        axis=1,
     )
     field[...] = scatter_nodes(rows, incidence[...])
-    field[0:3, :] = source_pattern[...]
+    for j in range(nodes // LANES):
+        row = SOURCE_ROW + 3 * j
+        field[0:3, j * LANES : (j + 1) * LANES] = packed[row : row + 3, :]
     send[...] = pick_lanes(field[...], index)
 
     reference_rows = 3 * POINTS
@@ -420,8 +473,9 @@
 
 def place_kernel(pieces, out):
     for w in range(pieces.shape[0]):
+        held = snake("dom", w)
         for c in range(STRAIN):
-            out[c, :, w * LANES : (w + 1) * LANES] = pieces[w, c * STEPS : (c + 1) * STEPS, :]
+            out[c, :, w * LANES : (w + 1) * LANES] = pieces[held, c * STEPS : (c + 1) * STEPS, :]
 
 
 def shards(
@@ -445,7 +499,8 @@
     strain_t = jax.ShapeDtypeStruct((STRAIN * POINTS, LANES), f32)
 
     face = lax.broadcasted_iota(jnp.int32, (8, LANES), 1) // (LANES // FACES)
-    parity = jnp.where(face < 2, lax.axis_index("grp") % 2, lax.axis_index("dom") % 2)
+    dom = lax.axis_index("dom")
+    parity = jnp.where(face < 2, lax.axis_index("grp") % 2, (dom // DOM_ROW + dom) % 2)
     source = 2 * (face // 2) + jnp.bitwise_xor(parity, 1 - face % 2)
 
     def exchange(send):
@@ -455,12 +510,40 @@
             count = lax.axis_size(axis)
             pairs = []
             for i in range(offset, count - 1, 2):
-                pairs += [(i, i + 1), (i + 1, i)]
+                first, second = snake(axis, i), snake(axis, i + 1)
+                pairs += [(first, second), (second, first)]
             received.append(lax.ppermute(send, axis, pairs))
         return received
 
     i32, bf16 = jnp.int32, jnp.bfloat16
     rank_rows = point_rank.reshape(POINTS, LANES)
+    arguments = (
+        wavelet,
+        neighbours,
+        connect,
+        interface_nodes,
+        mass_elem,
+        source_pattern,
+        shape_grad.T,
+        inverse_jacobian,
+        lame_moduli,
+        point_weights,
+        rank_rows,
+    )
+    buffers = [pltpu.SMEM(x.shape, x.dtype) for x in arguments[:2]]
+    buffers += [pltpu.VMEM(x.shape, x.dtype) for x in arguments[2:6] + arguments[7:]]
+    packed, shape_t, wave = kernel_call(
+        pack_kernel,
+        [
+            jax.ShapeDtypeStruct((PACKED_ROWS, LANES), f32),
+            jax.ShapeDtypeStruct(shape_grad.T.shape, f32),
+            jax.ShapeDtypeStruct((STEPS, LANES), f32),
+        ],
+        [HBM] * len(arguments),
+        scratch=buffers + [pltpu.SemaphoreType.DMA((len(arguments),))],
+    )(*(pltpu.with_memory_space_constraint(x, pltpu.MemorySpace.HBM) for x in arguments))
+    writers = lax.axis_size("dom")
+    packed = lax.ppermute(packed, "dom", [(i, snake("dom", i)) for i in range(writers)])
     outs = kernel_call(
         prepare_kernel,
         [
@@ -472,44 +555,16 @@
             jax.ShapeDtypeStruct((NODE_ROWS, LANES), i32),
             jax.ShapeDtypeStruct((9 * POINTS, 3 * GRADIENT_BLOCK), bf16),
             jax.ShapeDtypeStruct((3 * NODE_ROWS, 3 * FORCE_BLOCK), bf16),
-            jax.ShapeDtypeStruct((STEPS, LANES), f32),
             jax.ShapeDtypeStruct(inverse_jacobian.shape, f32),
             jax.ShapeDtypeStruct(lame_moduli.shape, f32),
             jax.ShapeDtypeStruct(point_weights.shape, f32),
             jax.ShapeDtypeStruct(rank_rows.shape, i32),
         ],
-        [HBM] * 11,
-        scratch=[
-            pltpu.VMEM(connect.shape, i32),
-            pltpu.SMEM(wavelet.shape, f32),
-            pltpu.SMEM(neighbours.shape, i32),
-            pltpu.VMEM(interface_nodes.shape, i32),
-            pltpu.VMEM(mass_elem.shape, f32),
-            pltpu.VMEM(source_pattern.shape, f32),
-            pltpu.VMEM(shape_grad.T.shape, f32),
-            pltpu.SemaphoreType.DMA((11,)),
-        ],
-    )(
-        *(
-            pltpu.with_memory_space_constraint(x, pltpu.MemorySpace.HBM)
-            for x in (
-                wavelet,
-                neighbours,
-                connect,
-                interface_nodes,
-                mass_elem,
-                source_pattern,
-                shape_grad.T,
-                inverse_jacobian,
-                lame_moduli,
-                point_weights,
-                rank_rows,
-            )
-        ),
-    )
+        [VMEM, VMEM],
+    )(packed, shape_t)
     incidence, field, send, pick_index, inverse_index = outs[:5]
-    wave, rank = outs[8], outs[12]
-    element_data = (*outs[5:8], *outs[9:12], incidence)
+    rank = outs[11]
+    element_data = (*outs[5:11], incidence)
     received = exchange(send)
     strain, displace, velocity, pattern, half_inverse_mass, force, send = kernel_call(
         first_kernel, [strain_t, field_t, field_t, field_t, field_t, field_t, lanes_t], [VMEM] * 16
@@ -538,7 +593,6 @@
         strains.append(outs[0])
         if not last:
             displace, velocity, force, send = outs[1:]
-    writers = lax.axis_size("dom")
     (ordered,) = kernel_call(
         order_kernel,
         [jax.ShapeDtypeStruct((writers, STEPS * STRAIN, LANES), jnp.bfloat16)],

time: 319 us -> 288 us (0.903)
  the two profiles are of different devices: /device:TPU:201 before, /device:TPU:200 now
where the time goes in v3:
time: 288 us; the launch traced here: 286 us
  starting transfers between devices  198 us (69%)
  waiting for transfers between devices  36.6 us (13%)
  blocking collectives  27.8 us (10%)
  Pallas kernels  23 us (8%)
    ppermute x64, starting transfers between devices, exchange(): received.append(lax.ppermute(send, axis, pairs))  197 us
    ppermute x64, waiting for transfers between devices, exchange(): received.append(lax.ppermute(send, axis, pairs))  36.6 us
    all_to_all x1, blocking collectives, shards(): lax.all_to_all(ordered, 'dom', split_axis=0, concat_axis=0, tiled=True)  27.8 us
    pallas_call x15, Pallas kernels, shards(): kernel_call(functools.partial(step_kernel, step), [strain_t] + ([] if las...  16.8 us
  transfers between devices with their start and end apart: 65, of which 16 were waited for; matrix products, arithmetic and copies ran while one was open for 0% of the time, Pallas kernels for 0%

profile of v3, /device:TPU:200, one launch (start us, length us, event | category | flops | bytes accessed | tf_op | source)
XLA Modules:
  0.0 285.9 jit_solution(18391650992472321155)
XLA Ops:
  14.4 4.2 %collective-permute-start.8 = (f32[8,128]{1,0:T(8,128)S(1)}, f32[8,128]{1,0:T(8,128)S(1)}, u32[]{:S(2)}, u32[]{:S(2)}) collective-permute-start(f32[8,128]{1,0:T(8,128)S(1)} %get-tuple-element.113), channel_id=1, source_target_pairs={{0,16},{16,0},{32,48},{48,32},{64,80},{80,64},{96,112},{112,96},{1... | collective-permute-start | bytes 12296 | tf_op jit(solution)/shard_map/ppermute | solution.py:515
  18.7 5.5 %collective-permute-start.7 = (f32[8,128]{1,0:T(8,128)S(1)}, f32[8,128]{1,0:T(8,128)S(1)}, u32[]{:S(2)}, u32[]{:S(2)}) collective-permute-start(f32[8,128]{1,0:T(8,128)S(1)} %get-tuple-element.113), channel_id=1, source_target_pairs={{0,1},{1,0},{2,3},{3,2},{7,6},{6,7},{5,4},{4,5},{8,9},{9,8},{10,11... | collective-permute-start | bytes 12296 | tf_op jit(solution)/shard_map/ppermute | solution.py:515
  34.0 10.5 %collective-permute-start.11 = (f32[8,128]{1,0:T(8,128)S(1)}, f32[8,128]{1,0:T(8,128)S(1)}, u32[]{:S(2)}, u32[]{:S(2)}) collective-permute-start(f32[8,128]{1,0:T(8,128)S(1)} %get-tuple-element.120), channel_id=1, source_target_pairs={{0,1},{1,0},{2,3},{3,2},{7,6},{6,7},{5,4},{4,5},{8,9},{9,8},{10,11... | collective-permute-start | bytes 12296 | tf_op jit(solution)/shard_map/ppermute | solution.py:515
  54.4 6.1 %collective-permute-start.15 = (f32[8,128]{1,0:T(8,128)S(1)}, f32[8,128]{1,0:T(8,128)S(1)}, u32[]{:S(2)}, u32[]{:S(2)}) collective-permute-start(f32[8,128]{1,0:T(8,128)S(1)} %get-tuple-element.125), channel_id=1, source_target_pairs={{0,1},{1,0},{2,3},{3,2},{7,6},{6,7},{5,4},{4,5},{8,9},{9,8},{10,11... | collective-permute-start | bytes 12296 | tf_op jit(solution)/shard_map/ppermute | solution.py:515
  66.7 3.8 %collective-permute-start.20 = (f32[8,128]{1,0:T(8,128)S(1)}, f32[8,128]{1,0:T(8,128)S(1)}, u32[]{:S(2)}, u32[]{:S(2)}) collective-permute-start(f32[8,128]{1,0:T(8,128)S(1)} %get-tuple-element.130), channel_id=1, source_target_pairs={{0,16},{16,0},{32,48},{48,32},{64,80},{80,64},{96,112},{112,96},{1... | collective-permute-start | bytes 12296 | tf_op jit(solution)/shard_map/ppermute | solution.py:515
  70.4 4.6 %collective-permute-start.19 = (f32[8,128]{1,0:T(8,128)S(1)}, f32[8,128]{1,0:T(8,128)S(1)}, u32[]{:S(2)}, u32[]{:S(2)}) collective-permute-start(f32[8,128]{1,0:T(8,128)S(1)} %get-tuple-element.130), channel_id=1, source_target_pairs={{0,1},{1,0},{2,3},{3,2},{7,6},{6,7},{5,4},{4,5},{8,9},{9,8},{10,11... | collective-permute-start | bytes 12296 | tf_op jit(solution)/shard_map/ppermute | solution.py:515
  84.9 5.9 %collective-permute-start.23 = (f32[8,128]{1,0:T(8,128)S(1)}, f32[8,128]{1,0:T(8,128)S(1)}, u32[]{:S(2)}, u32[]{:S(2)}) collective-permute-start(f32[8,128]{1,0:T(8,128)S(1)} %get-tuple-element.135), channel_id=1, source_target_pairs={{0,1},{1,0},{2,3},{3,2},{7,6},{6,7},{5,4},{4,5},{8,9},{9,8},{10,11... | collective-permute-start | bytes 12296 | tf_op jit(solution)/shard_map/ppermute | solution.py:515
  96.9 3.8 %collective-permute-start.28 = (f32[8,128]{1,0:T(8,128)S(1)}, f32[8,128]{1,0:T(8,128)S(1)}, u32[]{:S(2)}, u32[]{:S(2)}) collective-permute-start(f32[8,128]{1,0:T(8,128)S(1)} %get-tuple-element.140), channel_id=1, source_target_pairs={{0,16},{16,0},{32,48},{48,32},{64,80},{80,64},{96,112},{112,96},{1... | collective-permute-start | bytes 12296 | tf_op jit(solution)/shard_map/ppermute | solution.py:515
  100.7 5.3 %collective-permute-start.27 = (f32[8,128]{1,0:T(8,128)S(1)}, f32[8,128]{1,0:T(8,128)S(1)}, u32[]{:S(2)}, u32[]{:S(2)}) collective-permute-start(f32[8,128]{1,0:T(8,128)S(1)} %get-tuple-element.140), channel_id=1, source_target_pairs={{0,1},{1,0},{2,3},{3,2},{7,6},{6,7},{5,4},{4,5},{8,9},{9,8},{10,11... | collective-permute-start | bytes 12296 | tf_op jit(solution)/shard_map/ppermute | solution.py:515
  112.1 3.8 %collective-permute-start.32 = (f32[8,128]{1,0:T(8,128)S(1)}, f32[8,128]{1,0:T(8,128)S(1)}, u32[]{:S(2)}, u32[]{:S(2)}) collective-permute-start(f32[8,128]{1,0:T(8,128)S(1)} %get-tuple-element.145), channel_id=1, source_target_pairs={{0,16},{16,0},{32,48},{48,32},{64,80},{80,64},{96,112},{112,96},{1... | collective-permute-start | bytes 12296 | tf_op jit(solution)/shard_map/ppermute | solution.py:515
  115.8 6.8 %collective-permute-start.31 = (f32[8,128]{1,0:T(8,128)S(1)}, f32[8,128]{1,0:T(8,128)S(1)}, u32[]{:S(2)}, u32[]{:S(2)}) collective-permute-start(f32[8,128]{1,0:T(8,128)S(1)} %get-tuple-element.145), channel_id=1, source_target_pairs={{0,1},{1,0},{2,3},{3,2},{7,6},{6,7},{5,4},{4,5},{8,9},{9,8},{10,11... | collective-permute-start | bytes 12296 | tf_op jit(solution)/shard_map/ppermute | solution.py:515
  128.7 3.8 %collective-permute-start.36 = (f32[8,128]{1,0:T(8,128)S(1)}, f32[8,128]{1,0:T(8,128)S(1)}, u32[]{:S(2)}, u32[]{:S(2)}) collective-permute-start(f32[8,128]{1,0:T(8,128)S(1)} %get-tuple-element.150), channel_id=1, source_target_pairs={{0,16},{16,0},{32,48},{48,32},{64,80},{80,64},{96,112},{112,96},{1... | collective-permute-start | bytes 12296 | tf_op jit(solution)/shard_map/ppermute | solution.py:515
  132.5 5.3 %collective-permute-start.35 = (f32[8,128]{1,0:T(8,128)S(1)}, f32[8,128]{1,0:T(8,128)S(1)}, u32[]{:S(2)}, u32[]{:S(2)}) collective-permute-start(f32[8,128]{1,0:T(8,128)S(1)} %get-tuple-element.150), channel_id=1, source_target_pairs={{0,1},{1,0},{2,3},{3,2},{7,6},{6,7},{5,4},{4,5},{8,9},{9,8},{10,11... | collective-permute-start | bytes 12296 | tf_op jit(solution)/shard_map/ppermute | solution.py:515
  143.9 3.8 %collective-permute-start.40 = (f32[8,128]{1,0:T(8,128)S(1)}, f32[8,128]{1,0:T(8,128)S(1)}, u32[]{:S(2)}, u32[]{:S(2)}) collective-permute-start(f32[8,128]{1,0:T(8,128)S(1)} %get-tuple-element.155), channel_id=1, source_target_pairs={{0,16},{16,0},{32,48},{48,32},{64,80},{80,64},{96,112},{112,96},{1... | collective-permute-start | bytes 12296 | tf_op jit(solution)/shard_map/ppermute | solution.py:515
  147.6 6.8 %collective-permute-start.39 = (f32[8,128]{1,0:T(8,128)S(1)}, f32[8,128]{1,0:T(8,128)S(1)}, u32[]{:S(2)}, u32[]{:S(2)}) collective-permute-start(f32[8,128]{1,0:T(8,128)S(1)} %get-tuple-element.155), channel_id=1, source_target_pairs={{0,1},{1,0},{2,3},{3,2},{7,6},{6,7},{5,4},{4,5},{8,9},{9,8},{10,11... | collective-permute-start | bytes 12296 | tf_op jit(solution)/shard_map/ppermute | solution.py:515
  160.5 3.8 %collective-permute-start.44 = (f32[8,128]{1,0:T(8,128)S(1)}, f32[8,128]{1,0:T(8,128)S(1)}, u32[]{:S(2)}, u32[]{:S(2)}) collective-permute-start(f32[8,128]{1,0:T(8,128)S(1)} %get-tuple-element.160), channel_id=1, source_target_pairs={{0,16},{16,0},{32,48},{48,32},{64,80},{80,64},{96,112},{112,96},{1... | collective-permute-start | bytes 12296 | tf_op jit(solution)/shard_map/ppermute | solution.py:515
  164.3 5.3 %collective-permute-start.43 = (f32[8,128]{1,0:T(8,128)S(1)}, f32[8,128]{1,0:T(8,128)S(1)}, u32[]{:S(2)}, u32[]{:S(2)}) collective-permute-start(f32[8,128]{1,0:T(8,128)S(1)} %get-tuple-element.160), channel_id=1, source_target_pairs={{0,1},{1,0},{2,3},{3,2},{7,6},{6,7},{5,4},{4,5},{8,9},{9,8},{10,11... | collective-permute-start | bytes 12296 | tf_op jit(solution)/shard_map/ppermute | solution.py:515
  179.5 6.8 %collective-permute-start.47 = (f32[8,128]{1,0:T(8,128)S(1)}, f32[8,128]{1,0:T(8,128)S(1)}, u32[]{:S(2)}, u32[]{:S(2)}) collective-permute-start(f32[8,128]{1,0:T(8,128)S(1)} %get-tuple-element.165), channel_id=1, source_target_pairs={{0,1},{1,0},{2,3},{3,2},{7,6},{6,7},{5,4},{4,5},{8,9},{9,8},{10,11... | collective-permute-start | bytes 12296 | tf_op jit(solution)/shard_map/ppermute | solution.py:515
  196.1 5.3 %collective-permute-start.51 = (f32[8,128]{1,0:T(8,128)S(1)}, f32[8,128]{1,0:T(8,128)S(1)}, u32[]{:S(2)}, u32[]{:S(2)}) collective-permute-start(f32[8,128]{1,0:T(8,128)S(1)} %get-tuple-element.170), channel_id=1, source_target_pairs={{0,1},{1,0},{2,3},{3,2},{7,6},{6,7},{5,4},{4,5},{8,9},{9,8},{10,11... | collective-permute-start | bytes 12296 | tf_op jit(solution)/shard_map/ppermute | solution.py:515
  211.3 6.8 %collective-permute-start.55 = (f32[8,128]{1,0:T(8,128)S(1)}, f32[8,128]{1,0:T(8,128)S(1)}, u32[]{:S(2)}, u32[]{:S(2)}) collective-permute-start(f32[8,128]{1,0:T(8,128)S(1)} %get-tuple-element.175), channel_id=1, source_target_pairs={{0,1},{1,0},{2,3},{3,2},{7,6},{6,7},{5,4},{4,5},{8,9},{9,8},{10,11... | collective-permute-start | bytes 12296 | tf_op jit(solution)/shard_map/ppermute | solution.py:515
  224.2 3.8 %collective-permute-start.60 = (f32[8,128]{1,0:T(8,128)S(1)}, f32[8,128]{1,0:T(8,128)S(1)}, u32[]{:S(2)}, u32[]{:S(2)}) collective-permute-start(f32[8,128]{1,0:T(8,128)S(1)} %get-tuple-element.180), channel_id=1, source_target_pairs={{0,16},{16,0},{32,48},{48,32},{64,80},{80,64},{96,112},{112,96},{1... | collective-permute-start | bytes 12296 | tf_op jit(solution)/shard_map/ppermute | solution.py:515
  228.0 5.3 %collective-permute-start.59 = (f32[8,128]{1,0:T(8,128)S(1)}, f32[8,128]{1,0:T(8,128)S(1)}, u32[]{:S(2)}, u32[]{:S(2)}) collective-permute-start(f32[8,128]{1,0:T(8,128)S(1)} %get-tuple-element.180), channel_id=1, source_target_pairs={{0,1},{1,0},{2,3},{3,2},{7,6},{6,7},{5,4},{4,5},{8,9},{9,8},{10,11... | collective-permute-start | bytes 12296 | tf_op jit(solution)/shard_map/ppermute | solution.py:515
  243.1 6.8 %collective-permute-start.63 = (f32[8,128]{1,0:T(8,128)S(1)}, f32[8,128]{1,0:T(8,128)S(1)}, u32[]{:S(2)}, u32[]{:S(2)}) collective-permute-start(f32[8,128]{1,0:T(8,128)S(1)} %get-tuple-element.185), channel_id=1, source_target_pairs={{0,1},{1,0},{2,3},{3,2},{7,6},{6,7},{5,4},{4,5},{8,9},{9,8},{10,11... | collective-permute-start | bytes 12296 | tf_op jit(solution)/shard_map/ppermute | solution.py:515
  257.2 27.8 %all_to_all.5.pieces = bf16[16,96,128]{2,1,0:T(8,128)(2,1)S(1)} all-to-all(bf16[16,96,128]{2,1,0:T(8,128)(2,1)S(1)} %shard_map.127), channel_id=1, replica_groups=mesh['grp'=32,'dom'=16] {'dom'}, dimensions={0} | all-to-all | bytes 786432 | tf_op jit(solution)/shard_map/all_to_all | solution.py:602
  (130 shorter events, 133.6 us)
Async XLA Ops:
  3.0 8.2 %collective-permute-start.4 = (f32[8,128]{1,0:T(8,128)S(1)}, f32[8,128]{1,0:T(8,128)S(1)}, u32[]{:S(2)}, u32[]{:S(2)}) collective-permute-start(f32[8,128]{1,0:T(8,128)S(1)} %get-tuple-element.101), channel_id=1, source_target_pairs={{0,16},{16,0},{32,48},{48,32},{64,80},{80,64},{96,112},{112,96},{1... | collective-permute-start | bytes 12296 | tf_op jit(solution)/shard_map/ppermute | solution.py:515
  14.4 12.3 %collective-permute-start.8 = (f32[8,128]{1,0:T(8,128)S(1)}, f32[8,128]{1,0:T(8,128)S(1)}, u32[]{:S(2)}, u32[]{:S(2)}) collective-permute-start(f32[8,128]{1,0:T(8,128)S(1)} %get-tuple-element.113), channel_id=1, source_target_pairs={{0,16},{16,0},{32,48},{48,32},{64,80},{80,64},{96,112},{112,96},{1... | collective-permute-start | bytes 12296 | tf_op jit(solution)/shard_map/ppermute | solution.py:515
  30.2 16.9 %collective-permute-start.12 = (f32[8,128]{1,0:T(8,128)S(1)}, f32[8,128]{1,0:T(8,128)S(1)}, u32[]{:S(2)}, u32[]{:S(2)}) collective-permute-start(f32[8,128]{1,0:T(8,128)S(1)} %get-tuple-element.120), channel_id=1, source_target_pairs={{0,16},{16,0},{32,48},{48,32},{64,80},{80,64},{96,112},{112,96},{1... | collective-permute-start | bytes 12296 | tf_op jit(solution)/shard_map/ppermute | solution.py:515
  34.0 13.2 %collective-permute-start.11 = (f32[8,128]{1,0:T(8,128)S(1)}, f32[8,128]{1,0:T(8,128)S(1)}, u32[]{:S(2)}, u32[]{:S(2)}) collective-permute-start(f32[8,128]{1,0:T(8,128)S(1)} %get-tuple-element.120), channel_id=1, source_target_pairs={{0,1},{1,0},{2,3},{3,2},{7,6},{6,7},{5,4},{4,5},{8,9},{9,8},{10,11... | collective-permute-start | bytes 12296 | tf_op jit(solution)/shard_map/ppermute | solution.py:515
  50.6 12.5 %collective-permute-start.16 = (f32[8,128]{1,0:T(8,128)S(1)}, f32[8,128]{1,0:T(8,128)S(1)}, u32[]{:S(2)}, u32[]{:S(2)}) collective-permute-start(f32[8,128]{1,0:T(8,128)S(1)} %get-tuple-element.125), channel_id=1, source_target_pairs={{0,16},{16,0},{32,48},{48,32},{64,80},{80,64},{96,112},{112,96},{1... | collective-permute-start | bytes 12296 | tf_op jit(solution)/shard_map/ppermute | solution.py:515
  54.4 8.8 %collective-permute-start.15 = (f32[8,128]{1,0:T(8,128)S(1)}, f32[8,128]{1,0:T(8,128)S(1)}, u32[]{:S(2)}, u32[]{:S(2)}) collective-permute-start(f32[8,128]{1,0:T(8,128)S(1)} %get-tuple-element.125), channel_id=1, source_target_pairs={{0,1},{1,0},{2,3},{3,2},{7,6},{6,7},{5,4},{4,5},{8,9},{9,8},{10,11... | collective-permute-start | bytes 12296 | tf_op jit(solution)/shard_map/ppermute | solution.py:515
  66.7 11.0 %collective-permute-start.20 = (f32[8,128]{1,0:T(8,128)S(1)}, f32[8,128]{1,0:T(8,128)S(1)}, u32[]{:S(2)}, u32[]{:S(2)}) collective-permute-start(f32[8,128]{1,0:T(8,128)S(1)} %get-tuple-element.130), channel_id=1, source_target_pairs={{0,16},{16,0},{32,48},{48,32},{64,80},{80,64},{96,112},{112,96},{1... | collective-permute-start | bytes 12296 | tf_op jit(solution)/shard_map/ppermute | solution.py:515
  81.2 12.2 %collective-permute-start.24 = (f32[8,128]{1,0:T(8,128)S(1)}, f32[8,128]{1,0:T(8,128)S(1)}, u32[]{:S(2)}, u32[]{:S(2)}) collective-permute-start(f32[8,128]{1,0:T(8,128)S(1)} %get-tuple-element.135), channel_id=1, source_target_pairs={{0,16},{16,0},{32,48},{48,32},{64,80},{80,64},{96,112},{112,96},{1... | collective-permute-start | bytes 12296 | tf_op jit(solution)/shard_map/ppermute | solution.py:515
  84.9 8.5 %collective-permute-start.23 = (f32[8,128]{1,0:T(8,128)S(1)}, f32[8,128]{1,0:T(8,128)S(1)}, u32[]{:S(2)}, u32[]{:S(2)}) collective-permute-start(f32[8,128]{1,0:T(8,128)S(1)} %get-tuple-element.135), channel_id=1, source_target_pairs={{0,1},{1,0},{2,3},{3,2},{7,6},{6,7},{5,4},{4,5},{8,9},{9,8},{10,11... | collective-permute-start | bytes 12296 | tf_op jit(solution)/shard_map/ppermute | solution.py:515
  96.9 11.7 %collective-permute-start.28 = (f32[8,128]{1,0:T(8,128)S(1)}, f32[8,128]{1,0:T(8,128)S(1)}, u32[]{:S(2)}, u32[]{:S(2)}) collective-permute-start(f32[8,128]{1,0:T(8,128)S(1)} %get-tuple-element.140), channel_id=1, source_target_pairs={{0,16},{16,0},{32,48},{48,32},{64,80},{80,64},{96,112},{112,96},{1... | collective-permute-start | bytes 12296 | tf_op jit(solution)/shard_map/ppermute | solution.py:515
  112.1 13.2 %collective-permute-start.32 = (f32[8,128]{1,0:T(8,128)S(1)}, f32[8,128]{1,0:T(8,128)S(1)}, u32[]{:S(2)}, u32[]{:S(2)}) collective-permute-start(f32[8,128]{1,0:T(8,128)S(1)} %get-tuple-element.145), channel_id=1, source_target_pairs={{0,16},{16,0},{32,48},{48,32},{64,80},{80,64},{96,112},{112,96},{1... | collective-permute-start | bytes 12296 | tf_op jit(solution)/shard_map/ppermute | solution.py:515
  115.8 9.4 %collective-permute-start.31 = (f32[8,128]{1,0:T(8,128)S(1)}, f32[8,128]{1,0:T(8,128)S(1)}, u32[]{:S(2)}, u32[]{:S(2)}) collective-permute-start(f32[8,128]{1,0:T(8,128)S(1)} %get-tuple-element.145), channel_id=1, source_target_pairs={{0,1},{1,0},{2,3},{3,2},{7,6},{6,7},{5,4},{4,5},{8,9},{9,8},{10,11... | collective-permute-start | bytes 12296 | tf_op jit(solution)/shard_map/ppermute | solution.py:515
  128.7 11.7 %collective-permute-start.36 = (f32[8,128]{1,0:T(8,128)S(1)}, f32[8,128]{1,0:T(8,128)S(1)}, u32[]{:S(2)}, u32[]{:S(2)}) collective-permute-start(f32[8,128]{1,0:T(8,128)S(1)} %get-tuple-element.150), channel_id=1, source_target_pairs={{0,16},{16,0},{32,48},{48,32},{64,80},{80,64},{96,112},{112,96},{1... | collective-permute-start | bytes 12296 | tf_op jit(solution)/shard_map/ppermute | solution.py:515
  143.9 13.2 %collective-permute-start.40 = (f32[8,128]{1,0:T(8,128)S(1)}, f32[8,128]{1,0:T(8,128)S(1)}, u32[]{:S(2)}, u32[]{:S(2)}) collective-permute-start(f32[8,128]{1,0:T(8,128)S(1)} %get-tuple-element.155), channel_id=1, source_target_pairs={{0,16},{16,0},{32,48},{48,32},{64,80},{80,64},{96,112},{112,96},{1... | collective-permute-start | bytes 12296 | tf_op jit(solution)/shard_map/ppermute | solution.py:515
  147.6 9.4 %collective-permute-start.39 = (f32[8,128]{1,0:T(8,128)S(1)}, f32[8,128]{1,0:T(8,128)S(1)}, u32[]{:S(2)}, u32[]{:S(2)}) collective-permute-start(f32[8,128]{1,0:T(8,128)S(1)} %get-tuple-element.155), channel_id=1, source_target_pairs={{0,1},{1,0},{2,3},{3,2},{7,6},{6,7},{5,4},{4,5},{8,9},{9,8},{10,11... | collective-permute-start | bytes 12296 | tf_op jit(solution)/shard_map/ppermute | solution.py:515
  160.5 11.7 %collective-permute-start.44 = (f32[8,128]{1,0:T(8,128)S(1)}, f32[8,128]{1,0:T(8,128)S(1)}, u32[]{:S(2)}, u32[]{:S(2)}) collective-permute-start(f32[8,128]{1,0:T(8,128)S(1)} %get-tuple-element.160), channel_id=1, source_target_pairs={{0,16},{16,0},{32,48},{48,32},{64,80},{80,64},{96,112},{112,96},{1... | collective-permute-start | bytes 12296 | tf_op jit(solution)/shard_map/ppermute | solution.py:515
  175.7 13.2 %collective-permute-start.48 = (f32[8,128]{1,0:T(8,128)S(1)}, f32[8,128]{1,0:T(8,128)S(1)}, u32[]{:S(2)}, u32[]{:S(2)}) collective-permute-start(f32[8,128]{1,0:T(8,128)S(1)} %get-tuple-element.165), channel_id=1, source_target_pairs={{0,16},{16,0},{32,48},{48,32},{64,80},{80,64},{96,112},{112,96},{1... | collective-permute-start | bytes 12296 | tf_op jit(solution)/shard_map/ppermute | solution.py:515
  179.5 9.4 %collective-permute-start.47 = (f32[8,128]{1,0:T(8,128)S(1)}, f32[8,128]{1,0:T(8,128)S(1)}, u32[]{:S(2)}, u32[]{:S(2)}) collective-permute-start(f32[8,128]{1,0:T(8,128)S(1)} %get-tuple-element.165), channel_id=1, source_target_pairs={{0,1},{1,0},{2,3},{3,2},{7,6},{6,7},{5,4},{4,5},{8,9},{9,8},{10,11... | collective-permute-start | bytes 12296 | tf_op jit(solution)/shard_map/ppermute | solution.py:515
  192.4 11.7 %collective-permute-start.52 = (f32[8,128]{1,0:T(8,128)S(1)}, f32[8,128]{1,0:T(8,128)S(1)}, u32[]{:S(2)}, u32[]{:S(2)}) collective-permute-start(f32[8,128]{1,0:T(8,128)S(1)} %get-tuple-element.170), channel_id=1, source_target_pairs={{0,16},{16,0},{32,48},{48,32},{64,80},{80,64},{96,112},{112,96},{1... | collective-permute-start | bytes 12296 | tf_op jit(solution)/shard_map/ppermute | solution.py:515
  207.5 13.3 %collective-permute-start.56 = (f32[8,128]{1,0:T(8,128)S(1)}, f32[8,128]{1,0:T(8,128)S(1)}, u32[]{:S(2)}, u32[]{:S(2)}) collective-permute-start(f32[8,128]{1,0:T(8,128)S(1)} %get-tuple-element.175), channel_id=1, source_target_pairs={{0,16},{16,0},{32,48},{48,32},{64,80},{80,64},{96,112},{112,96},{1... | collective-permute-start | bytes 12296 | tf_op jit(solution)/shard_map/ppermute | solution.py:515
  211.3 9.6 %collective-permute-start.55 = (f32[8,128]{1,0:T(8,128)S(1)}, f32[8,128]{1,0:T(8,128)S(1)}, u32[]{:S(2)}, u32[]{:S(2)}) collective-permute-start(f32[8,128]{1,0:T(8,128)S(1)} %get-tuple-element.175), channel_id=1, source_target_pairs={{0,1},{1,0},{2,3},{3,2},{7,6},{6,7},{5,4},{4,5},{8,9},{9,8},{10,11... | collective-permute-start | bytes 12296 | tf_op jit(solution)/shard_map/ppermute | solution.py:515
  224.2 11.7 %collective-permute-start.60 = (f32[8,128]{1,0:T(8,128)S(1)}, f32[8,128]{1,0:T(8,128)S(1)}, u32[]{:S(2)}, u32[]{:S(2)}) collective-permute-start(f32[8,128]{1,0:T(8,128)S(1)} %get-tuple-element.180), channel_id=1, source_target_pairs={{0,16},{16,0},{32,48},{48,32},{64,80},{80,64},{96,112},{112,96},{1... | collective-permute-start | bytes 12296 | tf_op jit(solution)/shard_map/ppermute | solution.py:515
  239.4 13.2 %collective-permute-start.64 = (f32[8,128]{1,0:T(8,128)S(1)}, f32[8,128]{1,0:T(8,128)S(1)}, u32[]{:S(2)}, u32[]{:S(2)}) collective-permute-start(f32[8,128]{1,0:T(8,128)S(1)} %get-tuple-element.185), channel_id=1, source_target_pairs={{0,16},{16,0},{32,48},{48,32},{64,80},{80,64},{96,112},{112,96},{1... | collective-permute-start | bytes 12296 | tf_op jit(solution)/shard_map/ppermute | solution.py:515
  243.1 9.4 %collective-permute-start.63 = (f32[8,128]{1,0:T(8,128)S(1)}, f32[8,128]{1,0:T(8,128)S(1)}, u32[]{:S(2)}, u32[]{:S(2)}) collective-permute-start(f32[8,128]{1,0:T(8,128)S(1)} %get-tuple-element.185), channel_id=1, source_target_pairs={{0,1},{1,0},{2,3},{3,2},{7,6},{6,7},{5,4},{4,5},{8,9},{9,8},{10,11... | collective-permute-start | bytes 12296 | tf_op jit(solution)/shard_map/ppermute | solution.py:515
  (41 other events, 188.5 us)

commit v4 on v3

--- a/solution.py
+++ b/solution.py
@@ -1,5 +1,3 @@
-import functools
-
 import jax
 import jax.numpy as jnp
 from jax import lax
@@ -86,10 +84,21 @@
     return jnp.where(source == 3, dom1, out)
 
 
-def scatter_nodes(rows, incidence):
-    left = jnp.concatenate(parts_of(rows), axis=0).astype(jnp.bfloat16)
+def scatter_nodes(pieces, chunks, incidence):
+    group = lax.broadcasted_iota(jnp.int32, (8, LANES), 0) // 4
+    parts = [[], [], []]
+    for piece, chunk in zip(pieces, chunks):
+        both = [jnp.where(chunk == group + base, piece, 0.0) for base in (0, 2)]
+        for i, part in enumerate(parts_of(jnp.concatenate(both, axis=0))):
+            parts[i].append(part.astype(jnp.bfloat16))
+    left = jnp.concatenate([jnp.concatenate(p, axis=1) for p in parts], axis=0)
     sums = matmul(left, incidence)
-    return (sums[16:24] + sums[8:16]) + sums[0:8]
+    total = (sums[32:48] + sums[16:32]) + sums[0:16]
+    fields = []
+    for base in (0, 8):
+        rows = total[base : base + 8]
+        fields += [rows, pltpu.roll(rows, 4, 0)]
+    return jnp.concatenate(fields, axis=1)
 
 
 CONNECT_ROW = 0
@@ -199,13 +208,15 @@
     lame_moduli[...] = packed[LAME_ROW : LAME_ROW + 2, :]
     point_weights[...] = packed[WEIGHTS_ROW : WEIGHTS_ROW + POINTS, :]
     rank[...] = packed[RANK_ROW : RANK_ROW + POINTS, :].astype(jnp.int32)
+    low = jnp.bitwise_and(element_nodes, LANES - 1)
+    chunk = jnp.right_shift(element_nodes, 7)
+    own_lane = lax.broadcasted_iota(jnp.int32, (LANES, LANES), 1)
+    for n in range(EL_NODES):
+        column = jnp.broadcast_to(low[n : n + 1, :], (LANES, LANES)).T
+        incidence[n * LANES : (n + 1) * LANES, :] = jnp.where(
+            column == own_lane, 1.0, 0.0
+        ).astype(jnp.bfloat16)
     lane = lax.broadcasted_iota(jnp.int32, (LANES, nodes), 1)
-    for n in range(EL_NODES):
-        column = jnp.broadcast_to(element_nodes[n : n + 1, :], (LANES, LANES)).T
-        wide = jnp.concatenate([column] * (nodes // LANES), axis=1)
-        incidence[n * LANES : (n + 1) * LANES, :] = jnp.where(wide == lane, 1.0, 0.0).astype(
-            jnp.bfloat16
-        )
     listed = packed[LISTED_ROW : LISTED_ROW + 1, :].astype(jnp.int32)
     column = jnp.broadcast_to(listed, (LANES, LANES)).T
     wide = jnp.concatenate([column] * (nodes // LANES), axis=1)
@@ -215,14 +226,12 @@
     swapped = packed[SWAPPED_ROW : SWAPPED_ROW + 1, :].astype(jnp.int32)
     index = jnp.broadcast_to(swapped, (8, LANES))
     pick_index[...] = index
-    rows = jnp.concatenate(
-        [
-            jnp.broadcast_to(packed[MASS_ROW + n : MASS_ROW + n + 1, :], (8, LANES))
-            for n in range(EL_NODES)
-        ],
-        axis=1,
-    )
-    field[...] = scatter_nodes(rows, incidence[...])
+    masses = [
+        jnp.broadcast_to(packed[MASS_ROW + n : MASS_ROW + n + 1, :], (8, LANES))
+        for n in range(EL_NODES)
+    ]
+    chunks = [chunk[n : n + 1, :] for n in range(EL_NODES)]
+    field[...] = scatter_nodes(masses, chunks, incidence[...])
     for j in range(nodes // LANES):
         row = SOURCE_ROW + 3 * j
         field[0:3, j * LANES : (j + 1) * LANES] = packed[row : row + 3, :]
@@ -261,8 +270,12 @@
     return jnp.concatenate(pieces, axis=0).astype(jnp.bfloat16)
 
 
-def wave_row(wave, step, width):
-    return jnp.concatenate([wave[step : step + 1, :]] * (width // LANES), axis=1)
+def wave_row(wave, width):
+    return jnp.concatenate([wave[0:1, :]] * (width // LANES), axis=1)
+
+
+def moved_up(wave):
+    return pltpu.roll(wave[...], STEPS - 1, 0)
 
 
 def strain_and_force(
@@ -340,7 +353,7 @@
     right = stacked_parts(mapped, FORCE_BLOCK)
     sums = matmul(left_force[...], right)
     node_forces = (sums[2 * NODE_ROWS :] + sums[NODE_ROWS : 2 * NODE_ROWS]) + sums[0:NODE_ROWS]
-    row_id = lax.broadcasted_iota(jnp.int32, (8, LANES), 0)
+    row_id = lax.broadcasted_iota(jnp.int32, (8, LANES), 0) % 4
     pieces = []
     for n in range(EL_NODES):
         first, second, third = (
@@ -348,7 +361,8 @@
             for c in range(3)
         )
         pieces.append(jnp.where(row_id == 0, first, jnp.where(row_id == 1, second, third)))
-    return scatter_nodes(jnp.concatenate(pieces, axis=1), incidence[...])
+    chunks = [chunk[n : n + 1, :] for n in range(EL_NODES)]
+    return scatter_nodes(pieces, chunks, incidence[...])
 
 
 def first_kernel(
@@ -375,13 +389,15 @@
     half_inverse_mass,
     force,
     send,
+    next_wave,
 ):
+    next_wave[...] = moved_up(wave)
     received = merge_received(source[...], dom1[...], grp1[...], dom0[...], grp0[...])
     total = field[...] + spread(received, inverse_index[...])
     scale = jnp.broadcast_to(time_step * (1.0 / total[3:4, :]), total.shape)
     pattern[...] = total
     half_inverse_mass[...] = scale
-    new_velocity = scale * (wave_row(wave, 0, total.shape[1]) * total)
+    new_velocity = scale * (wave_row(wave, total.shape[1]) * total)
     velocity[...] = new_velocity
     new_displace = time_step * new_velocity
     displace[...] = new_displace
@@ -402,7 +418,6 @@
 
 
 def step_kernel(
-    step,
     wave,
     dom1,
     grp1,
@@ -428,7 +443,7 @@
 ):
     received = merge_received(source[...], dom1[...], grp1[...], dom0[...], grp0[...])
     stiff = old_force[...] + spread(received, inverse_index[...])
-    total = wave_row(wave, step, stiff.shape[1]) * pattern[...] - stiff
+    total = wave_row(wave, stiff.shape[1]) * pattern[...] - stiff
     new_velocity = old_velocity[...] + half_inverse_mass[...] * total
     new_displace = old_displace[...] + time_step * new_velocity
     new_force = strain_and_force(
@@ -444,19 +459,20 @@
         bool(rest),
     )
     if rest:
-        displace, velocity, force, send = rest
+        displace, velocity, force, send, next_wave = rest
+        next_wave[...] = moved_up(wave)
         displace[...] = new_displace
         velocity[...] = new_velocity
         force[...] = new_force
         send[...] = pick_lanes(new_force, pick_index[...])
 
 
-def order_kernel(rank, *refs):
-    strains, out, store = refs[:STEPS], refs[STEPS], refs[STEPS + 1]
+def order_kernel(rank, strains, last, out, store):
     for t in range(STEPS):
         for c in range(STRAIN):
             row = (c * STEPS + t) * POINTS
-            store[row : row + POINTS, :] = strains[t][c * POINTS : (c + 1) * POINTS, :]
+            rows = slice(c * POINTS, (c + 1) * POINTS)
+            store[row : row + POINTS, :] = strains[t, rows, :] if t < STEPS - 1 else last[rows, :]
     count = rank.shape[0] * LANES
     lane = lax.broadcasted_iota(jnp.int32, (LANES, count), 1)
     total = None
@@ -547,7 +563,7 @@
     outs = kernel_call(
         prepare_kernel,
         [
-            jax.ShapeDtypeStruct((EL_NODES * LANES, nodes), bf16),
+            jax.ShapeDtypeStruct((EL_NODES * LANES, LANES), bf16),
             field_t,
             lanes_t,
             index_t,
@@ -566,16 +582,20 @@
     rank = outs[11]
     element_data = (*outs[5:11], incidence)
     received = exchange(send)
-    strain, displace, velocity, pattern, half_inverse_mass, force, send = kernel_call(
-        first_kernel, [strain_t, field_t, field_t, field_t, field_t, field_t, lanes_t], [VMEM] * 16
+    wave_t = jax.ShapeDtypeStruct((STEPS, LANES), f32)
+    strain, displace, velocity, pattern, half_inverse_mass, force, send, wave = kernel_call(
+        first_kernel,
+        [strain_t, field_t, field_t, field_t, field_t, field_t, lanes_t, wave_t],
+        [VMEM] * 16,
     )(wave, *received, source, inverse_index, pick_index, field, *element_data)
-    strains = [strain]
-    for step in range(1, STEPS):
+    strains = jnp.zeros((STEPS - 1, STRAIN * POINTS, LANES), f32)
+    strains = lax.dynamic_update_index_in_dim(strains, strain, 0, 0)
+
+    def advance(last, displace, velocity, force, send, wave):
         received = exchange(send)
-        last = step == STEPS - 1
-        outs = kernel_call(
-            functools.partial(step_kernel, step),
-            [strain_t] + ([] if last else [field_t, field_t, field_t, lanes_t]),
+        return kernel_call(
+            step_kernel,
+            [strain_t] + ([] if last else [field_t, field_t, field_t, lanes_t, wave_t]),
             [VMEM] * 20,
         )(
             wave,
@@ -590,15 +610,21 @@
             velocity,
             force,
         )
-        strains.append(outs[0])
-        if not last:
-            displace, velocity, force, send = outs[1:]
+
+    def body(step, carried):
+        strains, *state = carried
+        strain, *state = advance(False, *state)
+        return (lax.dynamic_update_index_in_dim(strains, strain, step, 0), *state)
+
+    carried = (strains, displace, velocity, force, send, wave)
+    strains, *state = lax.fori_loop(1, STEPS - 1, body, carried)
+    (strain,) = advance(True, *state)
     (ordered,) = kernel_call(
         order_kernel,
         [jax.ShapeDtypeStruct((writers, STEPS * STRAIN, LANES), jnp.bfloat16)],
-        [VMEM] * (1 + STEPS),
+        [VMEM] * 3,
         scratch=[pltpu.VMEM((STEPS * STRAIN * POINTS, LANES), f32)],
-    )(rank, *strains)
+    )(rank, strains, strain)
     pieces = lax.all_to_all(ordered, "dom", split_axis=0, concat_axis=0, tiled=True)
     (placed,) = kernel_call(
         place_kernel, [jax.ShapeDtypeStruct((STRAIN, STEPS, writers * LANES), jnp.bfloat16)], [VMEM]

time: 288 us -> 288 us (level)
  blocking collectives: 27.8 us -> 19.3 us
  waiting for transfers between devices: 36.6 us -> 44.1 us
  Pallas kernels: 23 us -> 18.2 us
  starting transfers between devices: 198 us -> 202 us
    all_to_all x1, blocking collectives: 27.8 us -> 19.3 us  [shards(): lax.all_to_all(ordered, 'dom', split_axis=0, concat_axis=0, tiled=True)]
    ppermute x64, waiting for transfers between devices: 36.6 us -> 44.1 us  [exchange(): received.append(lax.ppermute(send, axis, pairs))]
    pallas_call x16, Pallas kernels: 18 us -> 13.5 us  [the longest x15 12.7 us: advance(): kernel_call(step_kernel, [strain_t] + ([] if last else [field_t, field_t,...]
    ppermute x64, starting transfers between devices: 197 us -> 201 us  [exchange(): received.append(lax.ppermute(send, axis, pairs))]
where the time goes in v4:
time: 288 us; the launch traced here: 286 us
  starting transfers between devices  202 us (70%)
  waiting for transfers between devices  44.1 us (15%)
  blocking collectives  19.3 us (7%)
  Pallas kernels  18.2 us (6%)
    ppermute x64, starting transfers between devices, exchange(): received.append(lax.ppermute(send, axis, pairs))  201 us
    ppermute x64, waiting for transfers between devices, exchange(): received.append(lax.ppermute(send, axis, pairs))  44.1 us
    all_to_all x1, blocking collectives, shards(): lax.all_to_all(ordered, 'dom', split_axis=0, concat_axis=0, tiled=True)  19.3 us
    pallas_call x15, Pallas kernels, advance(): kernel_call(step_kernel, [strain_t] + ([] if last else [field_t, field_t,...  12.7 us
  transfers between devices with their start and end apart: 65, of which 16 were waited for; matrix products, arithmetic and copies ran while one was open for 0% of the time, Pallas kernels for 0%

profile of v4, /device:TPU:200, one launch (start us, length us, event | category | flops | bytes accessed | tf_op | source)
XLA Modules:
  0.0 286.2 jit_solution(2885469496286311376)
XLA Ops:
  13.8 232.5 %while.26 = (s32[]{:T(128)}, f32[15,96,128]{2,1,0:T(8,128)S(1)}, f32[8,512]{1,0:T(8,128)S(1)}, f32[8,512]{1,0:T(8,128)S(1)}, f32[8,512]{1,0:T(8,128)S(1)}, /*ind...) while((s32[]{:T(128)}, f32[15,96,128]{2,1,0:T(8,128)S(1)}, ...), condition=%wide.region_1.2_spmd.clone, body=%wide.region_0.1_spmd.clone.sunk | while | flops 26629 | bytes 284211 | solution.py:620
  18.7 8.2 %collective-permute-start.2 = (f32[8,128]{1,0:T(8,128)S(1)}, f32[8,128]{1,0:T(8,128)S(1)}, u32[]{:S(2)}, u32[]{:S(2)}) collective-permute-start(f32[8,128]{1,0:T(8,128)S(1)} %get-tuple-element.786), channel_id=1, source_target_pairs={{0,1},{1,0},{2,3},{3,2},{7,6},{6,7},{5,4},{4,5},{8,9},{9,8},{10,11... | collective-permute-start | bytes 12296 | tf_op jit(solution)/shard_map/while/body/eval_jaxpr/ppermute | solution.py:531
  37.2 12.9 %collective-permute-start.2 = (f32[8,128]{1,0:T(8,128)S(1)}, f32[8,128]{1,0:T(8,128)S(1)}, u32[]{:S(2)}, u32[]{:S(2)}) collective-permute-start(f32[8,128]{1,0:T(8,128)S(1)} %get-tuple-element.786), channel_id=1, source_target_pairs={{0,1},{1,0},{2,3},{3,2},{7,6},{6,7},{5,4},{4,5},{8,9},{9,8},{10,11... | collective-permute-start | bytes 12296 | tf_op jit(solution)/shard_map/while/body/eval_jaxpr/ppermute | solution.py:531
  74.9 5.1 %collective-permute-start.2 = (f32[8,128]{1,0:T(8,128)S(1)}, f32[8,128]{1,0:T(8,128)S(1)}, u32[]{:S(2)}, u32[]{:S(2)}) collective-permute-start(f32[8,128]{1,0:T(8,128)S(1)} %get-tuple-element.786), channel_id=1, source_target_pairs={{0,1},{1,0},{2,3},{3,2},{7,6},{6,7},{5,4},{4,5},{8,9},{9,8},{10,11... | collective-permute-start | bytes 12296 | tf_op jit(solution)/shard_map/while/body/eval_jaxpr/ppermute | solution.py:531
  90.3 7.0 %collective-permute-start.2 = (f32[8,128]{1,0:T(8,128)S(1)}, f32[8,128]{1,0:T(8,128)S(1)}, u32[]{:S(2)}, u32[]{:S(2)}) collective-permute-start(f32[8,128]{1,0:T(8,128)S(1)} %get-tuple-element.786), channel_id=1, source_target_pairs={{0,1},{1,0},{2,3},{3,2},{7,6},{6,7},{5,4},{4,5},{8,9},{9,8},{10,11... | collective-permute-start | bytes 12296 | tf_op jit(solution)/shard_map/while/body/eval_jaxpr/ppermute | solution.py:531
  107.9 5.5 %collective-permute-start.2 = (f32[8,128]{1,0:T(8,128)S(1)}, f32[8,128]{1,0:T(8,128)S(1)}, u32[]{:S(2)}, u32[]{:S(2)}) collective-permute-start(f32[8,128]{1,0:T(8,128)S(1)} %get-tuple-element.786), channel_id=1, source_target_pairs={{0,1},{1,0},{2,3},{3,2},{7,6},{6,7},{5,4},{4,5},{8,9},{9,8},{10,11... | collective-permute-start | bytes 12296 | tf_op jit(solution)/shard_map/while/body/eval_jaxpr/ppermute | solution.py:531
  119.9 4.3 %collective-permute-start.3 = (f32[8,128]{1,0:T(8,128)S(1)}, f32[8,128]{1,0:T(8,128)S(1)}, u32[]{:S(2)}, u32[]{:S(2)}) collective-permute-start(f32[8,128]{1,0:T(8,128)S(1)} %get-tuple-element.786), channel_id=1, source_target_pairs={{0,16},{16,0},{32,48},{48,32},{64,80},{80,64},{96,112},{112,96},{1... | collective-permute-start | bytes 12296 | tf_op jit(solution)/shard_map/while/body/eval_jaxpr/ppermute | solution.py:531
  124.3 4.4 %collective-permute-start.2 = (f32[8,128]{1,0:T(8,128)S(1)}, f32[8,128]{1,0:T(8,128)S(1)}, u32[]{:S(2)}, u32[]{:S(2)}) collective-permute-start(f32[8,128]{1,0:T(8,128)S(1)} %get-tuple-element.786), channel_id=1, source_target_pairs={{0,1},{1,0},{2,3},{3,2},{7,6},{6,7},{5,4},{4,5},{8,9},{9,8},{10,11... | collective-permute-start | bytes 12296 | tf_op jit(solution)/shard_map/while/body/eval_jaxpr/ppermute | solution.py:531
  135.2 4.3 %collective-permute-start.3 = (f32[8,128]{1,0:T(8,128)S(1)}, f32[8,128]{1,0:T(8,128)S(1)}, u32[]{:S(2)}, u32[]{:S(2)}) collective-permute-start(f32[8,128]{1,0:T(8,128)S(1)} %get-tuple-element.786), channel_id=1, source_target_pairs={{0,16},{16,0},{32,48},{48,32},{64,80},{80,64},{96,112},{112,96},{1... | collective-permute-start | bytes 12296 | tf_op jit(solution)/shard_map/while/body/eval_jaxpr/ppermute | solution.py:531
  139.5 5.5 %collective-permute-start.2 = (f32[8,128]{1,0:T(8,128)S(1)}, f32[8,128]{1,0:T(8,128)S(1)}, u32[]{:S(2)}, u32[]{:S(2)}) collective-permute-start(f32[8,128]{1,0:T(8,128)S(1)} %get-tuple-element.786), channel_id=1, source_target_pairs={{0,1},{1,0},{2,3},{3,2},{7,6},{6,7},{5,4},{4,5},{8,9},{9,8},{10,11... | collective-permute-start | bytes 12296 | tf_op jit(solution)/shard_map/while/body/eval_jaxpr/ppermute | solution.py:531
  151.5 4.3 %collective-permute-start.3 = (f32[8,128]{1,0:T(8,128)S(1)}, f32[8,128]{1,0:T(8,128)S(1)}, u32[]{:S(2)}, u32[]{:S(2)}) collective-permute-start(f32[8,128]{1,0:T(8,128)S(1)} %get-tuple-element.786), channel_id=1, source_target_pairs={{0,16},{16,0},{32,48},{48,32},{64,80},{80,64},{96,112},{112,96},{1... | collective-permute-start | bytes 12296 | tf_op jit(solution)/shard_map/while/body/eval_jaxpr/ppermute | solution.py:531
  155.9 5.1 %collective-permute-start.2 = (f32[8,128]{1,0:T(8,128)S(1)}, f32[8,128]{1,0:T(8,128)S(1)}, u32[]{:S(2)}, u32[]{:S(2)}) collective-permute-start(f32[8,128]{1,0:T(8,128)S(1)} %get-tuple-element.786), channel_id=1, source_target_pairs={{0,1},{1,0},{2,3},{3,2},{7,6},{6,7},{5,4},{4,5},{8,9},{9,8},{10,11... | collective-permute-start | bytes 12296 | tf_op jit(solution)/shard_map/while/body/eval_jaxpr/ppermute | solution.py:531
  167.4 4.3 %collective-permute-start.3 = (f32[8,128]{1,0:T(8,128)S(1)}, f32[8,128]{1,0:T(8,128)S(1)}, u32[]{:S(2)}, u32[]{:S(2)}) collective-permute-start(f32[8,128]{1,0:T(8,128)S(1)} %get-tuple-element.786), channel_id=1, source_target_pairs={{0,16},{16,0},{32,48},{48,32},{64,80},{80,64},{96,112},{112,96},{1... | collective-permute-start | bytes 12296 | tf_op jit(solution)/shard_map/while/body/eval_jaxpr/ppermute | solution.py:531
  171.8 4.9 %collective-permute-start.2 = (f32[8,128]{1,0:T(8,128)S(1)}, f32[8,128]{1,0:T(8,128)S(1)}, u32[]{:S(2)}, u32[]{:S(2)}) collective-permute-start(f32[8,128]{1,0:T(8,128)S(1)} %get-tuple-element.786), channel_id=1, source_target_pairs={{0,1},{1,0},{2,3},{3,2},{7,6},{6,7},{5,4},{4,5},{8,9},{9,8},{10,11... | collective-permute-start | bytes 12296 | tf_op jit(solution)/shard_map/while/body/eval_jaxpr/ppermute | solution.py:531
  183.2 4.3 %collective-permute-start.3 = (f32[8,128]{1,0:T(8,128)S(1)}, f32[8,128]{1,0:T(8,128)S(1)}, u32[]{:S(2)}, u32[]{:S(2)}) collective-permute-start(f32[8,128]{1,0:T(8,128)S(1)} %get-tuple-element.786), channel_id=1, source_target_pairs={{0,16},{16,0},{32,48},{48,32},{64,80},{80,64},{96,112},{112,96},{1... | collective-permute-start | bytes 12296 | tf_op jit(solution)/shard_map/while/body/eval_jaxpr/ppermute | solution.py:531
  187.5 5.0 %collective-permute-start.2 = (f32[8,128]{1,0:T(8,128)S(1)}, f32[8,128]{1,0:T(8,128)S(1)}, u32[]{:S(2)}, u32[]{:S(2)}) collective-permute-start(f32[8,128]{1,0:T(8,128)S(1)} %get-tuple-element.786), channel_id=1, source_target_pairs={{0,1},{1,0},{2,3},{3,2},{7,6},{6,7},{5,4},{4,5},{8,9},{9,8},{10,11... | collective-permute-start | bytes 12296 | tf_op jit(solution)/shard_map/while/body/eval_jaxpr/ppermute | solution.py:531
  199.0 4.3 %collective-permute-start.3 = (f32[8,128]{1,0:T(8,128)S(1)}, f32[8,128]{1,0:T(8,128)S(1)}, u32[]{:S(2)}, u32[]{:S(2)}) collective-permute-start(f32[8,128]{1,0:T(8,128)S(1)} %get-tuple-element.786), channel_id=1, source_target_pairs={{0,16},{16,0},{32,48},{48,32},{64,80},{80,64},{96,112},{112,96},{1... | collective-permute-start | bytes 12296 | tf_op jit(solution)/shard_map/while/body/eval_jaxpr/ppermute | solution.py:531
  203.3 5.5 %collective-permute-start.2 = (f32[8,128]{1,0:T(8,128)S(1)}, f32[8,128]{1,0:T(8,128)S(1)}, u32[]{:S(2)}, u32[]{:S(2)}) collective-permute-start(f32[8,128]{1,0:T(8,128)S(1)} %get-tuple-element.786), channel_id=1, source_target_pairs={{0,1},{1,0},{2,3},{3,2},{7,6},{6,7},{5,4},{4,5},{8,9},{9,8},{10,11... | collective-permute-start | bytes 12296 | tf_op jit(solution)/shard_map/while/body/eval_jaxpr/ppermute | solution.py:531
  215.4 4.3 %collective-permute-start.3 = (f32[8,128]{1,0:T(8,128)S(1)}, f32[8,128]{1,0:T(8,128)S(1)}, u32[]{:S(2)}, u32[]{:S(2)}) collective-permute-start(f32[8,128]{1,0:T(8,128)S(1)} %get-tuple-element.786), channel_id=1, source_target_pairs={{0,16},{16,0},{32,48},{48,32},{64,80},{80,64},{96,112},{112,96},{1... | collective-permute-start | bytes 12296 | tf_op jit(solution)/shard_map/while/body/eval_jaxpr/ppermute | solution.py:531
  219.7 4.9 %collective-permute-start.2 = (f32[8,128]{1,0:T(8,128)S(1)}, f32[8,128]{1,0:T(8,128)S(1)}, u32[]{:S(2)}, u32[]{:S(2)}) collective-permute-start(f32[8,128]{1,0:T(8,128)S(1)} %get-tuple-element.786), channel_id=1, source_target_pairs={{0,1},{1,0},{2,3},{3,2},{7,6},{6,7},{5,4},{4,5},{8,9},{9,8},{10,11... | collective-permute-start | bytes 12296 | tf_op jit(solution)/shard_map/while/body/eval_jaxpr/ppermute | solution.py:531
  235.4 5.0 %collective-permute-start.2 = (f32[8,128]{1,0:T(8,128)S(1)}, f32[8,128]{1,0:T(8,128)S(1)}, u32[]{:S(2)}, u32[]{:S(2)}) collective-permute-start(f32[8,128]{1,0:T(8,128)S(1)} %get-tuple-element.786), channel_id=1, source_target_pairs={{0,1},{1,0},{2,3},{3,2},{7,6},{6,7},{5,4},{4,5},{8,9},{9,8},{10,11... | collective-permute-start | bytes 12296 | tf_op jit(solution)/shard_map/while/body/eval_jaxpr/ppermute | solution.py:531
  248.9 8.1 %collective-permute-start.12 = (f32[8,128]{1,0:T(8,128)S(1)}, f32[8,128]{1,0:T(8,128)S(1)}, u32[]{:S(2)}, u32[]{:S(2)}) collective-permute-start(f32[8,128]{1,0:T(8,128)S(1)} %get-tuple-element.493), channel_id=1, source_target_pairs={{0,16},{16,0},{32,48},{48,32},{64,80},{80,64},{96,112},{112,96},{1... | collective-permute-start | bytes 12296 | tf_op jit(solution)/shard_map/ppermute | solution.py:531
  257.0 5.1 %collective-permute-start.11 = (f32[8,128]{1,0:T(8,128)S(1)}, f32[8,128]{1,0:T(8,128)S(1)}, u32[]{:S(2)}, u32[]{:S(2)}) collective-permute-start(f32[8,128]{1,0:T(8,128)S(1)} %get-tuple-element.493), channel_id=1, source_target_pairs={{0,1},{1,0},{2,3},{3,2},{7,6},{6,7},{5,4},{4,5},{8,9},{9,8},{10,11... | collective-permute-start | bytes 12296 | tf_op jit(solution)/shard_map/ppermute | solution.py:531
  266.0 19.3 %all_to_all.5.pieces = bf16[16,96,128]{2,1,0:T(8,128)(2,1)S(1)} all-to-all(bf16[16,96,128]{2,1,0:T(8,128)(2,1)S(1)} %shard_map.113), channel_id=1, replica_groups=mesh['grp'=32,'dom'=16] {'dom'}, dimensions={0} | all-to-all | bytes 786432 | tf_op jit(solution)/shard_map/all_to_all | solution.py:628
  (216 shorter events, 142.4 us)
Async XLA Ops:
  13.8 15.1 %collective-permute-start = (f32[8,128]{1,0:T(8,128)S(1)}, f32[8,128]{1,0:T(8,128)S(1)}, u32[]{:S(2)}, u32[]{:S(2)}) collective-permute-start(f32[8,128]{1,0:T(8,128)S(1)} %get-tuple-element.786), channel_id=1, source_target_pairs={{1,2},{2,1},{3,7},{7,3},{6,5},{5,6},{4,8},{8,4},{9,10},{10,9},{11,... | collective-permute-start | bytes 12296 | tf_op jit(solution)/shard_map/while/body/eval_jaxpr/ppermute | solution.py:531
  14.5 14.4 %collective-permute-start.3 = (f32[8,128]{1,0:T(8,128)S(1)}, f32[8,128]{1,0:T(8,128)S(1)}, u32[]{:S(2)}, u32[]{:S(2)}) collective-permute-start(f32[8,128]{1,0:T(8,128)S(1)} %get-tuple-element.786), channel_id=1, source_target_pairs={{0,16},{16,0},{32,48},{48,32},{64,80},{80,64},{96,112},{112,96},{1... | collective-permute-start | bytes 12296 | tf_op jit(solution)/shard_map/while/body/eval_jaxpr/ppermute | solution.py:531
  32.7 19.3 %collective-permute-start = (f32[8,128]{1,0:T(8,128)S(1)}, f32[8,128]{1,0:T(8,128)S(1)}, u32[]{:S(2)}, u32[]{:S(2)}) collective-permute-start(f32[8,128]{1,0:T(8,128)S(1)} %get-tuple-element.786), channel_id=1, source_target_pairs={{1,2},{2,1},{3,7},{7,3},{6,5},{5,6},{4,8},{8,4},{9,10},{10,9},{11,... | collective-permute-start | bytes 12296 | tf_op jit(solution)/shard_map/while/body/eval_jaxpr/ppermute | solution.py:531
  33.4 18.7 %collective-permute-start.3 = (f32[8,128]{1,0:T(8,128)S(1)}, f32[8,128]{1,0:T(8,128)S(1)}, u32[]{:S(2)}, u32[]{:S(2)}) collective-permute-start(f32[8,128]{1,0:T(8,128)S(1)} %get-tuple-element.786), channel_id=1, source_target_pairs={{0,16},{16,0},{32,48},{48,32},{64,80},{80,64},{96,112},{112,96},{1... | collective-permute-start | bytes 12296 | tf_op jit(solution)/shard_map/while/body/eval_jaxpr/ppermute | solution.py:531
  37.2 14.9 %collective-permute-start.2 = (f32[8,128]{1,0:T(8,128)S(1)}, f32[8,128]{1,0:T(8,128)S(1)}, u32[]{:S(2)}, u32[]{:S(2)}) collective-permute-start(f32[8,128]{1,0:T(8,128)S(1)} %get-tuple-element.786), channel_id=1, source_target_pairs={{0,1},{1,0},{2,3},{3,2},{7,6},{6,7},{5,4},{4,5},{8,9},{9,8},{10,11... | collective-permute-start | bytes 12296 | tf_op jit(solution)/shard_map/while/body/eval_jaxpr/ppermute | solution.py:531
  70.5 11.6 %collective-permute-start = (f32[8,128]{1,0:T(8,128)S(1)}, f32[8,128]{1,0:T(8,128)S(1)}, u32[]{:S(2)}, u32[]{:S(2)}) collective-permute-start(f32[8,128]{1,0:T(8,128)S(1)} %get-tuple-element.786), channel_id=1, source_target_pairs={{1,2},{2,1},{3,7},{7,3},{6,5},{5,6},{4,8},{8,4},{9,10},{10,9},{11,... | collective-permute-start | bytes 12296 | tf_op jit(solution)/shard_map/while/body/eval_jaxpr/ppermute | solution.py:531
  85.9 13.5 %collective-permute-start = (f32[8,128]{1,0:T(8,128)S(1)}, f32[8,128]{1,0:T(8,128)S(1)}, u32[]{:S(2)}, u32[]{:S(2)}) collective-permute-start(f32[8,128]{1,0:T(8,128)S(1)} %get-tuple-element.786), channel_id=1, source_target_pairs={{1,2},{2,1},{3,7},{7,3},{6,5},{5,6},{4,8},{8,4},{9,10},{10,9},{11,... | collective-permute-start | bytes 12296 | tf_op jit(solution)/shard_map/while/body/eval_jaxpr/ppermute | solution.py:531
  86.5 12.8 %collective-permute-start.3 = (f32[8,128]{1,0:T(8,128)S(1)}, f32[8,128]{1,0:T(8,128)S(1)}, u32[]{:S(2)}, u32[]{:S(2)}) collective-permute-start(f32[8,128]{1,0:T(8,128)S(1)} %get-tuple-element.786), channel_id=1, source_target_pairs={{0,16},{16,0},{32,48},{48,32},{64,80},{80,64},{96,112},{112,96},{1... | collective-permute-start | bytes 12296 | tf_op jit(solution)/shard_map/while/body/eval_jaxpr/ppermute | solution.py:531
  103.2 12.3 %collective-permute-start = (f32[8,128]{1,0:T(8,128)S(1)}, f32[8,128]{1,0:T(8,128)S(1)}, u32[]{:S(2)}, u32[]{:S(2)}) collective-permute-start(f32[8,128]{1,0:T(8,128)S(1)} %get-tuple-element.786), channel_id=1, source_target_pairs={{1,2},{2,1},{3,7},{7,3},{6,5},{5,6},{4,8},{8,4},{9,10},{10,9},{11,... | collective-permute-start | bytes 12296 | tf_op jit(solution)/shard_map/while/body/eval_jaxpr/ppermute | solution.py:531
  103.8 11.6 %collective-permute-start.3 = (f32[8,128]{1,0:T(8,128)S(1)}, f32[8,128]{1,0:T(8,128)S(1)}, u32[]{:S(2)}, u32[]{:S(2)}) collective-permute-start(f32[8,128]{1,0:T(8,128)S(1)} %get-tuple-element.786), channel_id=1, source_target_pairs={{0,16},{16,0},{32,48},{48,32},{64,80},{80,64},{96,112},{112,96},{1... | collective-permute-start | bytes 12296 | tf_op jit(solution)/shard_map/while/body/eval_jaxpr/ppermute | solution.py:531
  119.3 11.4 %collective-permute-start = (f32[8,128]{1,0:T(8,128)S(1)}, f32[8,128]{1,0:T(8,128)S(1)}, u32[]{:S(2)}, u32[]{:S(2)}) collective-permute-start(f32[8,128]{1,0:T(8,128)S(1)} %get-tuple-element.786), channel_id=1, source_target_pairs={{1,2},{2,1},{3,7},{7,3},{6,5},{5,6},{4,8},{8,4},{9,10},{10,9},{11,... | collective-permute-start | bytes 12296 | tf_op jit(solution)/shard_map/while/body/eval_jaxpr/ppermute | solution.py:531
  134.5 12.5 %collective-permute-start = (f32[8,128]{1,0:T(8,128)S(1)}, f32[8,128]{1,0:T(8,128)S(1)}, u32[]{:S(2)}, u32[]{:S(2)}) collective-permute-start(f32[8,128]{1,0:T(8,128)S(1)} %get-tuple-element.786), channel_id=1, source_target_pairs={{1,2},{2,1},{3,7},{7,3},{6,5},{5,6},{4,8},{8,4},{9,10},{10,9},{11,... | collective-permute-start | bytes 12296 | tf_op jit(solution)/shard_map/while/body/eval_jaxpr/ppermute | solution.py:531
  135.2 11.9 %collective-permute-start.3 = (f32[8,128]{1,0:T(8,128)S(1)}, f32[8,128]{1,0:T(8,128)S(1)}, u32[]{:S(2)}, u32[]{:S(2)}) collective-permute-start(f32[8,128]{1,0:T(8,128)S(1)} %get-tuple-element.786), channel_id=1, source_target_pairs={{0,16},{16,0},{32,48},{48,32},{64,80},{80,64},{96,112},{112,96},{1... | collective-permute-start | bytes 12296 | tf_op jit(solution)/shard_map/while/body/eval_jaxpr/ppermute | solution.py:531
  150.9 12.1 %collective-permute-start = (f32[8,128]{1,0:T(8,128)S(1)}, f32[8,128]{1,0:T(8,128)S(1)}, u32[]{:S(2)}, u32[]{:S(2)}) collective-permute-start(f32[8,128]{1,0:T(8,128)S(1)} %get-tuple-element.786), channel_id=1, source_target_pairs={{1,2},{2,1},{3,7},{7,3},{6,5},{5,6},{4,8},{8,4},{9,10},{10,9},{11,... | collective-permute-start | bytes 12296 | tf_op jit(solution)/shard_map/while/body/eval_jaxpr/ppermute | solution.py:531
  151.5 11.4 %collective-permute-start.3 = (f32[8,128]{1,0:T(8,128)S(1)}, f32[8,128]{1,0:T(8,128)S(1)}, u32[]{:S(2)}, u32[]{:S(2)}) collective-permute-start(f32[8,128]{1,0:T(8,128)S(1)} %get-tuple-element.786), channel_id=1, source_target_pairs={{0,16},{16,0},{32,48},{48,32},{64,80},{80,64},{96,112},{112,96},{1... | collective-permute-start | bytes 12296 | tf_op jit(solution)/shard_map/while/body/eval_jaxpr/ppermute | solution.py:531
  166.8 11.9 %collective-permute-start = (f32[8,128]{1,0:T(8,128)S(1)}, f32[8,128]{1,0:T(8,128)S(1)}, u32[]{:S(2)}, u32[]{:S(2)}) collective-permute-start(f32[8,128]{1,0:T(8,128)S(1)} %get-tuple-element.786), channel_id=1, source_target_pairs={{1,2},{2,1},{3,7},{7,3},{6,5},{5,6},{4,8},{8,4},{9,10},{10,9},{11,... | collective-permute-start | bytes 12296 | tf_op jit(solution)/shard_map/while/body/eval_jaxpr/ppermute | solution.py:531
  182.5 12.0 %collective-permute-start = (f32[8,128]{1,0:T(8,128)S(1)}, f32[8,128]{1,0:T(8,128)S(1)}, u32[]{:S(2)}, u32[]{:S(2)}) collective-permute-start(f32[8,128]{1,0:T(8,128)S(1)} %get-tuple-element.786), channel_id=1, source_target_pairs={{1,2},{2,1},{3,7},{7,3},{6,5},{5,6},{4,8},{8,4},{9,10},{10,9},{11,... | collective-permute-start | bytes 12296 | tf_op jit(solution)/shard_map/while/body/eval_jaxpr/ppermute | solution.py:531
  198.3 12.5 %collective-permute-start = (f32[8,128]{1,0:T(8,128)S(1)}, f32[8,128]{1,0:T(8,128)S(1)}, u32[]{:S(2)}, u32[]{:S(2)}) collective-permute-start(f32[8,128]{1,0:T(8,128)S(1)} %get-tuple-element.786), channel_id=1, source_target_pairs={{1,2},{2,1},{3,7},{7,3},{6,5},{5,6},{4,8},{8,4},{9,10},{10,9},{11,... | collective-permute-start | bytes 12296 | tf_op jit(solution)/shard_map/while/body/eval_jaxpr/ppermute | solution.py:531
  199.0 11.9 %collective-permute-start.3 = (f32[8,128]{1,0:T(8,128)S(1)}, f32[8,128]{1,0:T(8,128)S(1)}, u32[]{:S(2)}, u32[]{:S(2)}) collective-permute-start(f32[8,128]{1,0:T(8,128)S(1)} %get-tuple-element.786), channel_id=1, source_target_pairs={{0,16},{16,0},{32,48},{48,32},{64,80},{80,64},{96,112},{112,96},{1... | collective-permute-start | bytes 12296 | tf_op jit(solution)/shard_map/while/body/eval_jaxpr/ppermute | solution.py:531
  214.7 11.9 %collective-permute-start = (f32[8,128]{1,0:T(8,128)S(1)}, f32[8,128]{1,0:T(8,128)S(1)}, u32[]{:S(2)}, u32[]{:S(2)}) collective-permute-start(f32[8,128]{1,0:T(8,128)S(1)} %get-tuple-element.786), channel_id=1, source_target_pairs={{1,2},{2,1},{3,7},{7,3},{6,5},{5,6},{4,8},{8,4},{9,10},{10,9},{11,... | collective-permute-start | bytes 12296 | tf_op jit(solution)/shard_map/while/body/eval_jaxpr/ppermute | solution.py:531
  230.4 12.0 %collective-permute-start = (f32[8,128]{1,0:T(8,128)S(1)}, f32[8,128]{1,0:T(8,128)S(1)}, u32[]{:S(2)}, u32[]{:S(2)}) collective-permute-start(f32[8,128]{1,0:T(8,128)S(1)} %get-tuple-element.786), channel_id=1, source_target_pairs={{1,2},{2,1},{3,7},{7,3},{6,5},{5,6},{4,8},{8,4},{9,10},{10,9},{11,... | collective-permute-start | bytes 12296 | tf_op jit(solution)/shard_map/while/body/eval_jaxpr/ppermute | solution.py:531
  246.3 15.8 %collective-permute-start.10 = (f32[8,128]{1,0:T(8,128)S(1)}, f32[8,128]{1,0:T(8,128)S(1)}, u32[]{:S(2)}, u32[]{:S(2)}) collective-permute-start(f32[8,128]{1,0:T(8,128)S(1)} %get-tuple-element.493), channel_id=1, source_target_pairs={{16,32},{32,16},{48,64},{64,48},{80,96},{96,80},{112,128},{128,112... | collective-permute-start | bytes 12296 | tf_op jit(solution)/shard_map/ppermute | solution.py:531
  248.2 13.9 %collective-permute-start.9 = (f32[8,128]{1,0:T(8,128)S(1)}, f32[8,128]{1,0:T(8,128)S(1)}, u32[]{:S(2)}, u32[]{:S(2)}) collective-permute-start(f32[8,128]{1,0:T(8,128)S(1)} %get-tuple-element.493), channel_id=1, source_target_pairs={{1,2},{2,1},{3,7},{7,3},{6,5},{5,6},{4,8},{8,4},{9,10},{10,9},{11,... | collective-permute-start | bytes 12296 | tf_op jit(solution)/shard_map/ppermute | solution.py:531
  248.9 13.3 %collective-permute-start.12 = (f32[8,128]{1,0:T(8,128)S(1)}, f32[8,128]{1,0:T(8,128)S(1)}, u32[]{:S(2)}, u32[]{:S(2)}) collective-permute-start(f32[8,128]{1,0:T(8,128)S(1)} %get-tuple-element.493), channel_id=1, source_target_pairs={{0,16},{16,0},{32,48},{48,32},{64,80},{80,64},{96,112},{112,96},{1... | collective-permute-start | bytes 12296 | tf_op jit(solution)/shard_map/ppermute | solution.py:531
  (41 other events, 283.1 us)
